TPU v7x, 32 devices: a whole 2x2x4 slice. The times are simulated.
32 devices in a mesh: pair: 2 (over x), tp: 4 (over z), side: 4 (over y, core).
Axes of the slice: x: 2, y: 2, z: 4, core: 2. Of those that a mesh axis runs over, the one named last changes fastest.
Arguments:
- x_prompt: bfloat16 [8, 2048, 4096], P(('pair', 'side')), parts along dimension 0
- s_len: int32 [8], P(('pair', 'side')), parts along dimension 0
- y_tok: bfloat16 [16, 4096], P(('pair', 'side')), parts along dimension 0
- c_len: int32 [16], P(('pair', 'side')), parts along dimension 0
- k_cache: bfloat16 [1, 16, 1024, 32, 128], P(None, ('pair', 'side'), 'tp'), parts along dimension 1
- v_cache: bfloat16 [1, 16, 1024, 32, 128], P(None, ('pair', 'side'), 'tp'), parts along dimension 1
- attn_gain: bfloat16 [1, 4096], replicated
- w_qkv: bfloat16 [1, 4096, 32, 3, 128], P(None, None, 'tp')
- w_out: bfloat16 [1, 32, 1, 128, 4096], P(None, 'tp')
- mlp_gain: bfloat16 [1, 4096], replicated
- w_gate_up: bfloat16 [1, 4096, 2, 11008], P(None, None, None, 'tp')
- w_down: bfloat16 [1, 11008, 4096], P(None, 'tp')
Outputs:
- output 1: bfloat16 [8, 2048, 4096], P(('pair', 'side')), parts along dimension 0
- output 2: bfloat16 [16, 4096], P(('pair', 'side')), parts along dimension 0
- output 3: bfloat16 [1, 8, 2048, 32, 128], P(None, ('pair', 'side'), 'tp'), parts along dimension 1
- output 4: bfloat16 [1, 8, 2048, 32, 128], P(None, ('pair', 'side'), 'tp'), parts along dimension 1
- output 5: bfloat16 [1, 16, 1024, 32, 128], P(None, ('pair', 'side'), 'tp'), parts along dimension 1
- output 6: bfloat16 [1, 16, 1024, 32, 128], P(None, ('pair', 'side'), 'tp'), parts along dimension 1
There are 2 independent parts. A program takes and returns all parts, laid end to end along the dimension named above; an argument that names none is the same for every part.
All inputs are finite; a program needn't handle non-finite values.
Results may differ from a plain program's by a relative error of at most 0.00695739.
Values are sent between devices in bfloat16 or wider.
A program may use at most 1 GiB of HBM per device.

v0:
```python
import functools

import jax
import jax.numpy as jnp
from jax import lax
from jax.experimental import pallas as pl
from jax.experimental.pallas import tpu as pltpu
from jax.sharding import PartitionSpec as P


ROPE_BASE = 10000.0
NORM_EPS = 1e-5

ORDER = (
    'Q0', 'T0', 'G0', 'T1', 'w2', 'Q1', 'T2', 'G12', 'T3', 'G3', 'D1', 'K', 'D2', 'w3', 'O012', 'k2', 'k1', 'k3', 'k0',
    'O3', 'B', 'l0', 'l2', 'l1', 'l3',
)


def rms_scale(values_f32, gain_f32):
    inv_rms = lax.rsqrt(jnp.mean(values_f32 * values_f32, axis=-1, keepdims=True) + NORM_EPS)
    return (values_f32 * inv_rms * gain_f32).astype(jnp.bfloat16)


def rope_tables(positions, head_dim):
    half_dim = head_dim // 2
    inv_freq = ROPE_BASE ** (-2.0 * jnp.arange(half_dim, dtype=jnp.float32) / head_dim)
    angles = positions.astype(jnp.float32)[:, None] * inv_freq[None, :]
    cos_table = jnp.cos(angles)
    sin_table = jnp.sin(angles)
    return jnp.concatenate([cos_table, cos_table], axis=1), jnp.concatenate([-sin_table, sin_table], axis=1)


def qkv_kernel(head_dim, extra, *refs):
    x_ref, gain_ref, wq_ref, wk_ref, wv_ref, cos_ref, sin_ref = refs[:7]
    extra_refs = refs[7:10] if extra else None
    normed_ref = refs[-1]
    q_ref, k_ref, v_ref, token_ref = refs[-5 - 3 * extra:-1 - 3 * extra]
    extra_outs = refs[-4:-1] if extra else (None,) * 3
    rows = x_ref.shape[0]
    chunk = pl.program_id(1)

    @pl.when(pl.program_id(0) == 0)
    def _():
        gain = gain_ref[...].astype(jnp.float32)
        normed_ref[chunk, :rows] = rms_scale(x_ref[...].astype(jnp.float32), gain)
        if extra:
            normed_ref[chunk, rows:] = rms_scale(extra_refs[0][...].astype(jnp.float32), gain)
        token_ref[...] = jnp.zeros_like(token_ref)

    cos, sin = cos_ref[...], sin_ref[...]
    if extra:
        cos = jnp.concatenate([cos, extra_refs[1][...]], axis=0)
        sin = jnp.concatenate([sin, extra_refs[2][...]], axis=0)
    for w_ref, out_ref, extra_out in zip((wq_ref, wk_ref, wv_ref), (q_ref, k_ref, v_ref), extra_outs):
        acc = jnp.dot(normed_ref[chunk], w_ref[...], preferred_element_type=jnp.float32)
        for start in range(0, acc.shape[1], head_dim):
            vals = acc[:, start:start + head_dim]
            if out_ref is not v_ref:
                vals = vals * cos + pltpu.roll(vals, head_dim // 2, 1) * sin
            out_ref[:, start:start + head_dim] = vals[:rows].astype(out_ref.dtype)
            if extra:
                extra_out[:, start:start + head_dim] = vals[rows:].astype(out_ref.dtype)


TOKEN = jax.ShapeDtypeStruct((8, 128), jnp.float32)


def project_qkv(half, rows, token, x, extra_rows, gain, w_all, tables, extra_tables, head_dim):
    depth = x.shape[1]
    width = w_all.shape[1] // 3
    block = 2 * head_dim
    steps = width // block
    extra = extra_rows is not None
    extras = [extra_rows, *extra_tables] if extra else []
    pad = extra_rows.shape[0] if extra else 0
    bf16 = jnp.bfloat16
    whole = lambda shape: pl.BlockSpec(shape, lambda n, c: (0, 0), pipeline_mode=pl.Buffered(1))
    columns = lambda part: pl.BlockSpec((depth, block), lambda n, c: (0, part * steps + n))
    table = pl.BlockSpec((rows, head_dim), lambda n, c: (2 * half + c, 0))
    extra_outs = [jax.ShapeDtypeStruct((pad, width), bf16)] * 3 if extra else []
    return pl.pallas_call(
        functools.partial(qkv_kernel, head_dim, extra),
        out_shape=[jax.ShapeDtypeStruct((2 * rows, width), bf16)] * 3 + [TOKEN] + extra_outs,
        grid=(steps, 2),
        in_specs=[
            pl.BlockSpec((rows, depth), lambda n, c: (2 * half + lax.select(n == 0, c, 1), 0)),
            whole((1, depth)),
            columns(0),
            columns(1),
            columns(2),
            table,
            table,
        ] + [whole(e.shape) for e in extras] + [pl.BlockSpec(memory_space=pl.ANY)],
        out_specs=[pl.BlockSpec((rows, block), lambda n, c: (c, n))] * 3 + [whole(TOKEN.shape)] + [pl.BlockSpec((pad, block), lambda n, c: (0, n))] * len(extra_outs),
        scratch_shapes=[pltpu.VMEM((2, rows + pad, depth), bf16)],
        compiler_params=pltpu.CompilerParams(dimension_semantics=("arbitrary", "arbitrary"), vmem_limit_bytes=56 << 20),
        cost_estimate=pl.CostEstimate(flops=12 * rows * depth * width, bytes_accessed=2 * (2 * rows * depth + 3 * depth * width + 6 * rows * width), transcendentals=0),
        name="project_qkv",
    )(x, gain, w_all, w_all, w_all, *tables, *extras, token)


def attend_kernel(chunk, first_checked, q_rows, slen_ref, *refs):
    q_ref = refs[0]
    k_refs = refs[1:chunk + 2]
    v_refs = refs[chunk + 2:2 * chunk + 3]
    out_ref, token_ref = refs[-2:]
    token_ref[...] = jnp.zeros_like(token_ref)
    rows, head_dim = q_ref.shape
    scale = head_dim ** -0.5
    limit = slen_ref[0]
    for start in range(0, rows, q_rows):
        query = q_ref[start:start + q_rows, :]
        scores = []
        values = []
        for part in range(chunk + 1):
            keys = rows if part < chunk else start + q_rows
            score = lax.dot_general(query, k_refs[part][:keys, :], (((1,), (1,)), ((), ())), preferred_element_type=jnp.float32) * scale
            key_pos = lax.broadcasted_iota(jnp.int32, score.shape, 1)
            if part == chunk:
                allowed = key_pos <= lax.broadcasted_iota(jnp.int32, score.shape, 0) + start
                if part >= first_checked:
                    allowed = allowed & (key_pos < limit - part * rows)
                score = jnp.where(allowed, score, -1e30)
            elif part >= first_checked:
                score = jnp.where(key_pos < limit - part * rows, score, -1e30)
            scores.append(score)
            values.append(v_refs[part][:keys, :])
        peak = functools.reduce(jnp.maximum, [jnp.max(score, axis=-1, keepdims=True) for score in scores])
        total = jnp.zeros((q_rows, 1), jnp.float32)
        mixed = jnp.zeros((q_rows, head_dim), jnp.float32)
        for score, value in zip(scores, values):
            weight = jnp.exp(score - peak)
            total = total + jnp.sum(weight, axis=-1, keepdims=True)
            mixed = mixed + jnp.dot(weight.astype(jnp.bfloat16), value, preferred_element_type=jnp.float32)
        out_ref[start:start + q_rows, :] = (mixed / total).astype(out_ref.dtype)


def attend(chunk, chunks, rows, token, s_len, queries, keys, values, head_dim):
    width = queries[0].shape[1]
    heads = width // head_dim

    pick = lambda c: pl.BlockSpec((rows, head_dim), lambda h, slen: (c % 2, h))
    every = range(chunk + 1)
    total_keys = rows * (chunk + 1)
    return pl.pallas_call(
        functools.partial(attend_kernel, chunk, chunks // 2, min(256, rows)),
        out_shape=[jax.ShapeDtypeStruct((rows, width), jnp.bfloat16), TOKEN],
        grid_spec=pltpu.PrefetchScalarGridSpec(
            num_scalar_prefetch=1,
            grid=(heads,),
            in_specs=[pick(c) for c in (chunk, *every, *every)] + [pl.BlockSpec(memory_space=pl.ANY)],
            out_specs=[pick(0), pl.BlockSpec(TOKEN.shape, lambda h, slen: (0, 0))],
        ),
        compiler_params=pltpu.CompilerParams(dimension_semantics=("arbitrary",), vmem_limit_bytes=48 << 20),
        cost_estimate=pl.CostEstimate(flops=8 * heads * rows * total_keys * head_dim, bytes_accessed=2 * width * (2 * total_keys + 2 * rows), transcendentals=heads * rows * total_keys),
    )(s_len, queries[chunk // 2], *[keys[c // 2] for c in every], *[values[c // 2] for c in every], token)


def output_kernel(size, heads, contexts, extra, aliased, where_ref, *refs):
    context_refs, refs = refs[:contexts], refs[contexts:]
    w_refs, refs = refs[:heads], refs[heads:]
    x_ref, gain_ref, refs = refs[0], refs[1], refs[2:]
    if extra:
        context_x_ref, x_x_ref, refs = refs[0], refs[1], refs[2:]
    refs = refs[1:]
    if aliased:
        refs = refs[2:]
    normed_ref, hidden_ref, refs = refs[0], refs[1], refs[2:]
    if extra:
        hidden_x_ref, refs = refs[0], refs[1:]
    token_ref, full_ref, square_ref = refs
    rows, depth = hidden_ref.shape
    head_dim, block = w_refs[0].shape[1:]
    chunk, step = pl.program_id(0), pl.program_id(1)

    @pl.when(step == 0)
    def _():
        square_ref[...] = jnp.zeros_like(square_ref)
        token_ref[...] = jnp.zeros_like(token_ref)
        for number, context_ref in enumerate(context_refs):
            @pl.when((chunk == 0) if number == 0 else (chunk > 0))
            def _():
                for r in range(heads):
                    columns = pl.ds(pl.multiple_of(lax.bitwise_xor(where_ref[0], r) * head_dim, head_dim), head_dim)
                    for t in range(size):
                        there = (r * size + t) * head_dim
                        full_ref[:rows, there:there + head_dim] = context_ref[t, 0, :, columns]
                        if extra:
                            full_ref[rows:, there:there + head_dim] = context_x_ref[t, :, columns]

    w_block = jnp.concatenate([w_ref[...].reshape(size * head_dim, block) for w_ref in w_refs], axis=0)
    acc = jnp.dot(full_ref[...], w_block, preferred_element_type=jnp.float32)
    columns = pl.ds(pl.multiple_of(step * block, block), block)
    hidden = (x_ref[...].astype(jnp.float32) + acc[:rows]).astype(jnp.bfloat16)
    hidden_ref[:, columns] = hidden
    hidden_f32 = hidden.astype(jnp.float32)
    square_ref[:rows] += jnp.sum(hidden_f32 * hidden_f32, axis=-1, keepdims=True)
    if extra:
        hidden = (x_x_ref[...].astype(jnp.float32) + acc[rows:]).astype(jnp.bfloat16)
        hidden_x_ref[:, columns] = hidden
        hidden_f32 = hidden.astype(jnp.float32)
        square_ref[rows:] += jnp.sum(hidden_f32 * hidden_f32, axis=-1, keepdims=True)

    @pl.when(step == pl.num_programs(1) - 1)
    def _():
        half = rows // 2
        inv_rms = lax.rsqrt(square_ref[...] / depth + NORM_EPS)
        for start in range(0, depth, block):
            gain = gain_ref[:, start:start + block].astype(jnp.float32)
            for part in range(2):
                lo, hi = part * half, (part + 1) * half
                normed_ref[part, :half, start:start + block] = (hidden_ref[lo:hi, start:start + block].astype(jnp.float32) * inv_rms[lo:hi] * gain).astype(jnp.bfloat16)
                if extra and part == 1:
                    normed_ref[part, half:, start:start + block] = (hidden_x_ref[:, start:start + block].astype(jnp.float32) * inv_rms[rows:] * gain).astype(jnp.bfloat16)
                else:
                    normed_ref[part, half:, start:start + block] = jnp.zeros((normed_ref.shape[1] - half, block), jnp.bfloat16)


def project_out(first, count, chunks, pad, token, where, contexts, w_heads, x, gain, extras, buffers):
    rows, width = contexts[0].shape[2:]
    depth = x.shape[1]
    heads = len(w_heads)
    size, head_dim = w_heads[0].shape[:2]
    block = min(512, depth)
    total = rows + (pad if extras else 0)
    whole = lambda shape: pl.BlockSpec(shape, lambda c, n, where: (0,) * len(shape), pipeline_mode=pl.Buffered(1))
    in_specs = [whole(contexts[0].shape)]
    if count > 1:
        in_specs.append(pl.BlockSpec((size, 1, rows, width), lambda c, n, where: (0, lax.max(c - 1, 0), 0, 0)))
    in_specs += [pl.BlockSpec((size, head_dim, block), lambda c, n, where: (0, 0, n))] * heads
    in_specs += [pl.BlockSpec((rows, block), lambda c, n, where: (first + c, n)), whole((1, depth))]
    out_shape = [jax.ShapeDtypeStruct((2 * chunks, rows // 2 + pad, depth), jnp.bfloat16), jax.ShapeDtypeStruct((rows * chunks, depth), jnp.bfloat16)]
    mode = {} if count > 1 else dict(pipeline_mode=pl.Buffered(1))
    out_specs = [
        pl.BlockSpec((2, rows // 2 + pad, depth), lambda c, n, where: (first + c, 0, 0), **mode),
        pl.BlockSpec((rows, depth), lambda c, n, where: (first + c, 0), **mode),
    ]
    if extras:
        in_specs += [whole(extras[0].shape), pl.BlockSpec((pad, block), lambda c, n, where: (0, n))]
        out_shape.append(jax.ShapeDtypeStruct((pad, depth), jnp.bfloat16))
        out_specs.append(whole((pad, depth)))
    in_specs.append(pl.BlockSpec(memory_space=pl.ANY))
    out_shape.append(TOKEN)
    out_specs.append(whole(TOKEN.shape))
    aliases = {}
    if buffers:
        aliases = {1 + len(in_specs): 0, 2 + len(in_specs): 1}
        in_specs += [pl.BlockSpec(memory_space=pl.ANY)] * 2
    return pl.pallas_call(
        functools.partial(output_kernel, size, heads, len(contexts), bool(extras), bool(buffers)),
        out_shape=out_shape,
        grid_spec=pltpu.PrefetchScalarGridSpec(
            num_scalar_prefetch=1,
            grid=(count, depth // block),
            in_specs=in_specs,
            out_specs=out_specs,
            scratch_shapes=[pltpu.VMEM((total, size * width), jnp.bfloat16), pltpu.VMEM((total, 1), jnp.float32)],
        ),
        input_output_aliases=aliases,
        compiler_params=pltpu.CompilerParams(dimension_semantics=("arbitrary", "arbitrary"), vmem_limit_bytes=60 << 20),
        cost_estimate=pl.CostEstimate(flops=2 * count * total * size * width * depth, bytes_accessed=2 * count * (size * width * depth + 4 * rows * width + 3 * total * depth), transcendentals=0),
        name="project_out",
    )(where, *contexts, *w_heads, x, gain, *extras, token, *buffers)


def mlp_kernel(size, chunk_rows, ff_steps, slots, token_ref, normed_ref, hextra_ref, wgu_ref, wd_ref, h_ref, out_ref, y_ref,
               acc, landed, outgoing, finished, residual, others, activated,
               rs_send, rs_recv, ag_send, ag_recv, keep_sem, h_sem, x_send, x_recv, credit):
    step = pl.program_id(0)
    me = lax.axis_index('tp')
    depth = wd_ref.shape[1]
    chunks = (out_ref.shape[0] // chunk_rows)
    piece = outgoing.shape[2]
    per_chunk = chunk_rows // (2 * piece)
    pieces = chunks * per_chunk
    subs = per_chunk // ff_steps
    last = size - 1

    @pl.when(step == 0)
    def _():
        barrier = pltpu.get_barrier_semaphore()
        for d in range(1, size):
            pl.semaphore_signal(barrier, inc=1, device_id={'tp': lax.rem(me + d, size)}, device_id_type=pl.DeviceIdType.MESH)
        pl.semaphore_wait(barrier, size - 1)

    def own_part(chain, m):
        start = pl.multiple_of(chain * (chunk_rows // 2) + lax.rem(m, per_chunk) * piece, piece)
        return acc.at[lax.rem(lax.div(m, per_chunk), 3), pl.ds(start, piece)]

    def out_rows(chain, m):
        start = pl.multiple_of(lax.div(m, per_chunk) * chunk_rows + chain * (chunk_rows // 2) + lax.rem(m, per_chunk) * piece, piece)
        return pl.ds(start, piece)

    def exchange(slot):
        for chain in range(2):
            place = me if chain == 0 else last - me
            nearer = me - 1 if chain == 0 else me + 1
            farther = me + 1 if chain == 0 else me - 1

            def sum_copy(source, m):
                return pltpu.make_async_remote_copy(
                    src_ref=source, dst_ref=landed.at[chain, lax.rem(m, slots)], send_sem=rs_send.at[chain, lax.rem(m, 4)],
                    recv_sem=rs_recv.at[chain, lax.rem(m, slots)], device_id={'tp': nearer}, device_id_type=pl.DeviceIdType.MESH)

            def keep_copy(m):
                return pltpu.make_async_copy(finished.at[chain, lax.rem(m, 2)], out_ref.at[out_rows(chain, m)], keep_sem.at[chain, lax.rem(m, 2)])

            def h_copy(m):
                return pltpu.make_async_copy(h_ref.at[out_rows(chain, m)], residual.at[chain, lax.rem(m, 2)], h_sem.at[chain, lax.rem(m, 2)])

            def back_copy(source, m):
                return pltpu.make_async_remote_copy(
                    src_ref=source, dst_ref=out_ref.at[out_rows(chain, m)], send_sem=ag_send.at[chain, lax.rem(m, 4)],
                    recv_sem=ag_recv.at[chain, lax.rem(m, 8)], device_id={'tp': farther}, device_id_type=pl.DeviceIdType.MESH)

            @pl.when((place == last) & (slot >= 0) & (slot < pieces))
            def _():
                @pl.when(slot >= 4)
                def _():
                    sum_copy(own_part(chain, slot - 4), slot - 4).wait_send()

                @pl.when(slot >= slots)
                def _():
                    pl.semaphore_wait(credit.at[chain], 1)

                sum_copy(own_part(chain, slot), slot).start()

            for hops in range(1, last):
                m = slot - (last - hops)

                @pl.when((place == hops) & (m >= 0) & (m < pieces))
                def _():
                    @pl.when(m >= 2)
                    def _():
                        sum_copy(outgoing.at[chain, lax.rem(m, 2)], m - 2).wait_send()

                    sum_copy(outgoing.at[chain, lax.rem(m, 2)], m).wait_recv()
                    outgoing[chain, lax.rem(m, 2)] = landed[chain, lax.rem(m, slots)] + own_part(chain, m)[...]

                    @pl.when(m + slots < pieces)
                    def _():
                        pl.semaphore_signal(credit.at[chain], inc=1, device_id={'tp': farther}, device_id_type=pl.DeviceIdType.MESH)

                    @pl.when(m >= slots)
                    def _():
                        pl.semaphore_wait(credit.at[chain], 1)

                    sum_copy(outgoing.at[chain, lax.rem(m, 2)], m).start()

            m = slot - last

            @pl.when((place == 0) & (slot == 0))
            def _():
                h_copy(0).start()

            @pl.when((place == 0) & (m >= 0) & (m < pieces))
            def _():
                @pl.when(m + 1 < pieces)
                def _():
                    h_copy(m + 1).start()

                @pl.when(m >= 2)
                def _():
                    keep_copy(m - 2).wait()
                    back_copy(finished.at[chain, lax.rem(m, 2)], m - 2).wait_send()

                h_copy(m).wait()
                sum_copy(outgoing.at[chain, lax.rem(m, 2)], m).wait_recv()
                total = landed[chain, lax.rem(m, slots)] + own_part(chain, m)[...]
                finished[chain, lax.rem(m, 2)] = (residual[chain, lax.rem(m, 2)].astype(jnp.float32) + total).astype(jnp.bfloat16)

                @pl.when(m + slots < pieces)
                def _():
                    pl.semaphore_signal(credit.at[chain], inc=1, device_id={'tp': farther}, device_id_type=pl.DeviceIdType.MESH)

                keep_copy(m).start()
                back_copy(finished.at[chain, lax.rem(m, 2)], m).start()

        for chain in range(2):
            place = me if chain == 0 else last - me
            farther = me + 1 if chain == 0 else me - 1

            def relay_copy(m):
                return pltpu.make_async_remote_copy(
                    src_ref=out_ref.at[out_rows(chain, m)], dst_ref=out_ref.at[out_rows(chain, m)], send_sem=ag_send.at[chain, lax.rem(m, 4)],
                    recv_sem=ag_recv.at[chain, lax.rem(m, 8)], device_id={'tp': farther}, device_id_type=pl.DeviceIdType.MESH)

            for hops in range(1, size):
                m = slot - last - 2 * hops

                @pl.when((place == hops) & (m >= 0) & (m < pieces))
                def _():
                    relay_copy(m).wait_recv()
                    if hops < last:
                        @pl.when(m >= 4)
                        def _():
                            relay_copy(m - 4).wait_send()

                        relay_copy(m).start()

    def extra_copy(d):
        return pltpu.make_async_remote_copy(
            src_ref=acc.at[(chunks - 1) % 3, pl.ds(chunk_rows, others.shape[1])], dst_ref=others.at[d], send_sem=x_send.at[d - 1],
            recv_sem=x_recv.at[d - 1], device_id={'tp': lax.rem(me + d, size)}, device_id_type=pl.DeviceIdType.MESH)

    @pl.when(step == chunks * ff_steps)
    def _():
        others[0] = acc[(chunks - 1) % 3, chunk_rows:chunk_rows + others.shape[1]]
        for d in range(1, size):
            extra_copy(d).start()

    @pl.when(step == chunks * ff_steps + 4)
    def _():
        for d in range(1, size):
            extra_copy(d).wait()
        total = others[lax.rem(me, size)]
        for j in range(1, size):
            total = total + others[lax.rem(me + size - j, size)]
        y_ref[...] = (hextra_ref[:others.shape[1]].astype(jnp.float32) + total).astype(jnp.bfloat16)

    chunk = lax.div(step, ff_steps)
    block = min(1024, depth)

    def compute_gate():
        rows_in = normed_ref[0]
        dims = (((1,), (1,)), ((), ()))
        gate = lax.dot_general(rows_in, wgu_ref[0], dims, preferred_element_type=jnp.float32)
        up = lax.dot_general(rows_in, wgu_ref[1], dims, preferred_element_type=jnp.float32)
        activated[...] = (gate * jax.nn.sigmoid(gate) * up).astype(jnp.bfloat16)

    def compute_down():
        first = lax.rem(step, ff_steps) == 0
        for start in range(0, depth, block):
            part = jnp.dot(activated[...], wd_ref[:, start:start + block], preferred_element_type=jnp.float32)

            @pl.when(first)
            def _():
                acc[lax.rem(chunk, 3), :, start:start + block] = part

            @pl.when(jnp.logical_not(first))
            def _():
                acc[lax.rem(chunk, 3), :, start:start + block] += part

    for sub in range(subs):
        exchange((step - ff_steps) * subs + sub)
        for part in range(2):
            if part * subs // 2 == sub:
                pl.when(step < chunks * ff_steps)((compute_gate, compute_down)[part])

    @pl.when(step == pl.num_programs(0) - 1)
    def _():
        for chain in range(2):
            place = me if chain == 0 else last - me
            nearer = me - 1 if chain == 0 else me + 1
            farther = me + 1 if chain == 0 else me - 1

            def sent(m):
                return pltpu.make_async_remote_copy(
                    src_ref=outgoing.at[chain, m % 2], dst_ref=landed.at[chain, m % slots], send_sem=rs_send.at[chain, m % 4],
                    recv_sem=rs_recv.at[chain, m % slots], device_id={'tp': nearer}, device_id_type=pl.DeviceIdType.MESH)

            def returned(m):
                return pltpu.make_async_remote_copy(
                    src_ref=finished.at[chain, m % 2], dst_ref=out_ref.at[pl.ds(0, piece)], send_sem=ag_send.at[chain, m % 4],
                    recv_sem=ag_recv.at[chain, m % 8], device_id={'tp': farther}, device_id_type=pl.DeviceIdType.MESH)

            @pl.when(place == last)
            def _():
                for m in range(pieces - 4, pieces):
                    sent(m).wait_send()

            @pl.when((place > 0) & (place < last))
            def _():
                for m in range(pieces - 2, pieces):
                    sent(m).wait_send()
                for m in range(pieces - 4, pieces):
                    returned(m).wait_send()

            @pl.when(place == 0)
            def _():
                for m in range(pieces - 2, pieces):
                    pltpu.make_async_copy(finished.at[chain, m % 2], out_ref.at[pl.ds(0, piece)], keep_sem.at[chain, m % 2]).wait()
                    returned(m).wait_send()


SUBSLOTS = 2


def mlp(token, normed, hextra, w_gate_up, w_down, hidden, size):
    chunks, lines, depth = normed.shape
    rows = hidden.shape[0]
    chunk_rows = rows // chunks
    ff = w_down.shape[0]
    ff_steps = 4
    piece = chunk_rows // (8 * SUBSLOTS)
    slots = 4
    pieces = chunks * 4 * SUBSLOTS
    extra = lines - chunk_rows
    seen = min(8, extra)
    steps = chunks * ff_steps
    total_steps = ff_steps + -(-(pieces + 3 * (size - 1)) // SUBSLOTS)
    ff_block = ff // ff_steps
    at_ff = lambda g: lax.select(g < steps, lax.rem(g, ff_steps), ff_steps - 1)
    at_chunk = lambda g: lax.min(lax.div(g, ff_steps), chunks - 1)
    f32, bf16 = jnp.float32, jnp.bfloat16
    return pl.pallas_call(
        functools.partial(mlp_kernel, size, chunk_rows, ff_steps, slots),
        out_shape=[jax.ShapeDtypeStruct((rows, depth), bf16), jax.ShapeDtypeStruct((seen, depth), bf16)],
        grid=(total_steps,),
        in_specs=[
            pl.BlockSpec(memory_space=pl.ANY),
            pl.BlockSpec((1, lines, depth), lambda g: (at_chunk(g), 0, 0)),
            pl.BlockSpec((extra, depth), lambda g: (0, 0), pipeline_mode=pl.Buffered(1)),
            pl.BlockSpec((2, ff_block, depth), lambda g: (0, at_ff(g), 0)),
            pl.BlockSpec((ff_block, depth), lambda g: (at_ff(g), 0)),
            pl.BlockSpec(memory_space=pl.ANY),
        ],
        out_specs=[pl.BlockSpec(memory_space=pl.ANY), pl.BlockSpec((seen, depth), lambda g: (0, 0), pipeline_mode=pl.Buffered(1))],
        scratch_shapes=[
            pltpu.VMEM((3, lines, depth), f32),
            pltpu.VMEM((2, slots, piece, depth), f32),
            pltpu.VMEM((2, 2, piece, depth), f32),
            pltpu.VMEM((2, 2, piece, depth), bf16),
            pltpu.VMEM((2, 2, piece, depth), bf16),
            pltpu.VMEM((size, seen, depth), f32),
            pltpu.VMEM((lines, ff_block), bf16),
            pltpu.SemaphoreType.DMA((2, 4)),
            pltpu.SemaphoreType.DMA((2, slots)),
            pltpu.SemaphoreType.DMA((2, 4)),
            pltpu.SemaphoreType.DMA((2, 8)),
            pltpu.SemaphoreType.DMA((2, 2)),
            pltpu.SemaphoreType.DMA((2, 2)),
            pltpu.SemaphoreType.DMA((size - 1,)),
            pltpu.SemaphoreType.DMA((size - 1,)),
            pltpu.SemaphoreType.REGULAR((2,)),
        ],
        compiler_params=pltpu.CompilerParams(dimension_semantics=("arbitrary",), vmem_limit_bytes=63 << 20, collective_id=0, has_side_effects=True),
        cost_estimate=pl.CostEstimate(flops=6 * rows * depth * ff, bytes_accessed=6 * chunks * depth * ff, transcendentals=rows * ff),
        name="mlp",
    )(token, normed, hextra, w_gate_up, w_down, hidden)


def pick_by(index, options):
    result = options[0]
    for place in range(1, len(options)):
        result = jnp.where(index == place, options[place], result)
    return result


def solution(mesh):
    side_size = mesh.shape['side']
    tp_size = mesh.shape['tp']
    seats = mesh.shape['pair'] * side_size
    group_axes = ('pair', 'side')
    last = tp_size - 1

    def cyclic(value, d):
        return lax.ppermute(value, 'tp', [(t, (t + d) % tp_size) for t in range(tp_size)])

    def swap(value, mask):
        return lax.ppermute(value, group_axes, [(q, q ^ mask) for q in range(seats)])

    def in_order(me, copies):
        return [pick_by(me, [copies[(t - j) % tp_size] for t in range(tp_size)]) for j in range(tp_size)]

    def device_fn(x_prompt, s_len, y_tok, c_len, k_cache, v_cache, attn_gain, w_qkv, w_out, mlp_gain, w_gate_up, w_down):
        me = lax.axis_index('tp')
        seat = lax.axis_index('pair') * side_size + lax.axis_index('side')
        where = seat.reshape(1).astype(jnp.int32)
        seq_len, depth = x_prompt.shape[1:]
        heads_local = w_qkv.shape[2]
        head_dim = w_qkv.shape[4]
        width = heads_local * head_dim
        rows = seq_len // tp_size
        decodes = y_tok.shape[0]
        pad = 16
        cache_local = k_cache.shape[2]
        val = {}

        def tie(keys):
            keys = list(dict.fromkeys(keys))
            for key, value in zip(keys, lax.optimization_barrier(tuple(val[key] for key in keys))):
                val[key] = value

        val['w', 0] = lax.all_gather(lax.dynamic_index_in_dim(w_out[0, :, 0], seat, 0, keepdims=False), 'tp', axis=0, tiled=False)

        val['w_all'] = jnp.swapaxes(w_qkv[0], 1, 2).reshape(depth, 3 * width)
        tables = rope_tables(jnp.arange(seq_len, dtype=jnp.int32), head_dim)
        extra_tables = rope_tables(jnp.concatenate([c_len, jnp.zeros((pad - decodes,), jnp.int32)]), head_dim)
        y_pad = jnp.concatenate([y_tok, jnp.zeros((pad - decodes, depth), y_tok.dtype)])
        val['gain'], val['s_len'], val['mlp_gain'] = attn_gain, s_len, mlp_gain
        val['valid'] = (jnp.arange(seq_len) < s_len[0]).astype(jnp.bfloat16)
        for which in range(2):
            val['cache', which] = jnp.zeros((rows, tp_size, heads_local, head_dim), jnp.bfloat16)
        buffers = []
        qkv = []

        def compute(name):
            kind = name[0]
            c = int(name[1:]) if name[1:].isdigit() else 0
            if kind == 'Q':
                tie(thread + ['gain'])
                made = project_qkv(c, rows, val['token'], x_prompt[0], y_pad if c == 0 else None, val['gain'], val['w_all'], tables, extra_tables, head_dim)
                val['token'] = made[3]
                qkv.append(made[:3])
                if c == 0:
                    val['dq', 0] = jnp.stack([part[:decodes].reshape(decodes, heads_local, head_dim) for part in made[4:]])
                    for d in range(1, tp_size):
                        val['dq', d] = cyclic(val['dq', 0], d)
                return ['token']
            if kind == 'T':
                tie(thread + ['s_len'])
                val['context', c], val['token'] = attend(c, tp_size, rows, val['token'], val['s_len'], *zip(*qkv), head_dim)
                return ['token']
            if kind == 'G':
                val['gathered', name[1:]] = lax.all_gather(jnp.stack([val['context', int(digit)] for digit in name[1:]]), 'tp', axis=0, tiled=False)
                return ['token']
            if kind == 'K':
                tie(thread + ['valid'])
                for d in range(tp_size):
                    made = []
                    keep = pick_by(me, [val['valid'][((t + d) % tp_size) * rows:((t + d) % tp_size + 1) * rows] for t in range(tp_size)])
                    for which in (1, 2):
                        rows_d = pick_by(me, [qkv[(t + d) % tp_size // 2][which][(t + d) % tp_size % 2 * rows:][:rows].reshape(rows, heads_local, head_dim) for t in range(tp_size)])
                        made.append(rows_d * keep[:, None, None])
                    val['kv', d] = jnp.stack(made)
                return []
            if name == 'D1':
                tie(thread + [('dq', d) for d in range(tp_size)])
                dec_full = jnp.concatenate(in_order(me, [val['dq', d] for d in range(tp_size)]), axis=2)
                cache_pos = me * cache_local + jnp.arange(cache_local)
                write_mask = (cache_pos[None, :] == c_len[:, None])[:, :, None, None]
                allowed = (cache_pos[None, :] <= c_len[:, None])[:, None, :]
                key_now = jnp.where(write_mask, dec_full[1][:, None], k_cache[0])
                value_now = jnp.where(write_mask, dec_full[2][:, None], v_cache[0])
                val['key_now'], val['value_now'] = key_now, value_now
                scores = jnp.einsum('bkh,btkh->bkt', dec_full[0], key_now, preferred_element_type=jnp.float32) * head_dim ** -0.5
                scores = jnp.where(allowed, scores, -1e30)
                peak = jnp.max(scores, axis=-1, keepdims=True)
                weights = jnp.exp(scores - peak)
                total = jnp.sum(weights, axis=-1, keepdims=True)
                mixed = jnp.einsum('bkt,btkh->bkh', weights.astype(jnp.bfloat16), value_now, preferred_element_type=jnp.float32)
                packed = jnp.stack([mixed, jnp.broadcast_to(peak, mixed.shape), jnp.broadcast_to(total, mixed.shape)])
                packed = packed.reshape(3, decodes, tp_size, heads_local, head_dim)
                for d in range(tp_size):
                    share = lax.dynamic_index_in_dim(packed, lax.rem(me + d, tp_size), 2, keepdims=False)
                    val['ds', d] = share if d == 0 else cyclic(share, d)
                return [('ds', 0)]
            if name == 'D2':
                tie(thread + [('ds', d) for d in range(tp_size)])
                shares = [val['ds', d] for d in range(tp_size)]
                top = functools.reduce(jnp.maximum, [share[1] for share in shares])
                factors = [jnp.exp(share[1] - top) for share in shares]
                dec_mixed = sum(share[0] * factor for share, factor in zip(shares, factors))
                dec_total = sum(share[2] * factor for share, factor in zip(shares, factors))
                val['dc', 0] = (dec_mixed / dec_total).astype(jnp.bfloat16).reshape(decodes, width)
                for d in range(1, tp_size):
                    val['dc', d] = cyclic(val['dc', 0], d)
                return [('dc', 0)]
            if kind == 'O':
                w_keys = [('w', r) for r in range(seats)]
                final = c == last
                parts = [('gathered', '3')] if final else [('gathered', '0'), ('gathered', '12')]
                extra_keys = [('dc', d) for d in range(tp_size)] if final else []
                tie(thread + ['mlp_gain'] + parts + extra_keys + ([] if final else w_keys))
                extras = []
                if final:
                    extras = [jnp.pad(jnp.stack(in_order(me, [val[key] for key in extra_keys])), ((0, 0), (0, pad - decodes), (0, 0))), y_pad]
                made = project_out(last if final else 0, 1 if final else last, tp_size, pad, val['token'], where, [val[key] for key in parts], [val[key] for key in w_keys], x_prompt[0], val['mlp_gain'], extras, [val[key] for key in buffers])
                buffers[:] = ['normed', 'h']
                val['normed'], val['h'], val['token'] = made[0], made[1], made[-1]
                if final:
                    val['hx'] = made[2]
                return ['token']
            val['out'], val['y'] = mlp(val['token'], val['normed'], val['hx'], jnp.transpose(w_gate_up[0], (1, 2, 0)), w_down[0], val['h'], tp_size)
            return ['y']

        def transfer(name):
            if name[0] == 'k':
                d = int(name[1])
                tie(thread + [('kv', d)])
                route = [(t * side_size + s, ((t + d) % tp_size) * side_size + (s + 1) % side_size) for t in range(tp_size) for s in range(side_size)]
                val['landed', d] = lax.ppermute(val['kv', d], ('tp', 'side'), route)
                return
            if name[0] == 'l':
                d = int(name[1])
                tie(thread + [('landed', d)])
                for which in range(2):
                    val['cache', which] = lax.dynamic_update_slice(val['cache', which], val['landed', d][which][:, None], (0, lax.rem(me - d + tp_size, tp_size), 0, 0))
                return
            bases = [0] if name == 'w2' else list(range(0, seats, 2))
            kept = [] if name == 'w2' else [('kv', d) for d in range(tp_size)]
            tie(thread + kept + [('w', base) for base in bases])
            for mask in (range(2, seats, 2) if name == 'w2' else [1]):
                for base in bases:
                    val['w', base ^ mask] = swap(val['w', base], mask)

        val['token'] = jnp.zeros(TOKEN.shape, TOKEN.dtype)
        thread = ['token']
        for name in ORDER:
            if name[0] in 'QTGKDOB':
                made = compute(name)
                thread = thread + made if name in ('K', 'D1', 'D2') else made
            else:
                transfer(name)

        caches = [val['cache', which].reshape(1, 1, rows, tp_size * heads_local, head_dim) for which in range(2)]
        return (val['out'][None], val['y'][:decodes], caches[0], caches[1], val['key_now'][None], val['value_now'][None])

    cache_spec = P(None, group_axes, 'tp', None, None)
    in_specs = (P(group_axes, None, None), P(group_axes), P(group_axes, None), P(group_axes), cache_spec, cache_spec, P(), P(None, None, 'tp', None, None), P(None, 'tp', None, None, None), P(), P(None, None, None, 'tp'), P(None, 'tp', None))
    out_specs = (P(group_axes, None, None), P(group_axes, None), cache_spec, cache_spec, cache_spec, cache_spec)
    return jax.shard_map(device_fn, mesh=mesh, in_specs=in_specs, out_specs=out_specs, check_vma=False)
```

profile of v0, /device:TPU:0, one launch (start us, length us, event | category | flops | bytes accessed | tf_op | source)
XLA Modules:
  0.0 1251.0 jit_solution(7021146000170123799)
XLA Ops:
  7.2 2.3 constant_dynamic-slice_fusion
  9.6 23.4 %copy.143 = bf16[512,8,24,128]{3,1,2,0:T(8,128)(2,1)} copy(bf16[512,8,24,128]{3,2,1,0:T(8,128)(2,1)} %bitcast.379) | data formatting | bytes 50331648
  35.2 3.7 fusion.24
  38.9 1.9 pad_maximum_fusion.5
  41.4 39.5 %project_qkv.2 = (bf16[1024,1024]{1,0:T(8,128)(2,1)}, bf16[1024,1024]{1,0:T(8,128)(2,1)}, bf16[1024,1024]{1,0:T(8,128)(2,1)}, f32[8,128]{1,0:T(8,128)}, bf16[16,...) custom-call(bf16[2048,4096]{1,0:T(8,128)(2,1)} %bitcast.387, bf16[1,4096]{1,0:T(2,128)(2,1)} %refs_1_.1, ...), custom_call_target="tpu_custom_call" | custom-call | flops 25769803776 | bytes 39845888 | tf_op jit(solution)/shard_map/project_qkv/pallas_call | solution.py:82
  80.9 1.6 copy-done
  82.5 1.6 copy-done.2
  84.8 8.6 shard_map.163
  93.7 1.6 copy-done.3
  95.3 11.2 shard_map.164
  107.0 38.3 %project_qkv.3 = (bf16[1024,1024]{1,0:T(8,128)(2,1)}, bf16[1024,1024]{1,0:T(8,128)(2,1)}, bf16[1024,1024]{1,0:T(8,128)(2,1)}, f32[8,128]{1,0:T(8,128)}) custom-call(bf16[2048,4096]{1,0:T(8,128)(2,1)} %bitcast.388, bf16[1,4096]{1,0:T(2,128)(2,1)} %refs_1_.1, bf16[4096,3072]{1,0:T(8,128)(2,1)} %bitcast.383, bf16[4096,3072]{1,0:T(8,128)(2,1)} %bitcast.384, ...), custom_call_target="tpu_custom_call" | custom-call | flops 25769803776 | bytes 39845888 | tf_op jit(solution)/shard_map/project_qkv/pallas_call | solution.py:82
  145.3 1.6 copy-done.4
  147.6 14.4 %shard_map.165 = (bf16[512,1024]{1,0:T(8,128)(2,1)S(1)}, f32[8,128]{1,0:T(8,128)S(1)}) custom-call(s32[1]{0:T(128)} %copy.158.slen_ref, bf16[1024,1024]{1,0:T(8,128)(2,1)S(1)} %copy-done.4, bf16[1024,1024]{1,0:T(8,128)(2,1)S(1)} %copy-done.1, bf16[1024,1024]{1,0:T(8,128)(2,1)S(1)} %copy-done.1, bf16[1024,1024]{1,0:T(8,128)(2,1)} %get-tuple-element.125.refs_3_.refs_4_, ...), custom_call_target="tpu_custom_call" | custom-call | flops 6442450944 | bytes 8388608 | tf_op jit(solution)/shard_map/pallas_call | solution.py:146
  162.1 1.5 pad_maximum_fusion.4
  165.8 3.1 collective-permute-start
  169.0 2.6 collective-permute-start.1
  171.5 1.7 collective-permute-start.2
  177.9 1.5 collective-permute-start.6
  180.9 1.6 copy-done.5
  182.5 18.4 %shard_map.166 = (bf16[512,1024]{1,0:T(8,128)(2,1)}, f32[8,128]{1,0:T(8,128)S(1)}) custom-call(s32[1]{0:T(128)} %copy.158.slen_ref, bf16[1024,1024]{1,0:T(8,128)(2,1)S(1)} %copy-done.5, bf16[1024,1024]{1,0:T(8,128)(2,1)S(1)} %copy-done.1, bf16[1024,1024]{1,0:T(8,128)(2,1)S(1)} %copy-done.1, bf16[1024,1024]{1,0:T(8,128)(2,1)} %get-tuple-element.125.refs_3_.refs_4_, ...), custom_call_target="tpu_custom_call" | custom-call | flops 8589934592 | bytes 10485760 | tf_op jit(solution)/shard_map/pallas_call | solution.py:146
  201.5 3.0 bitcast_select_fusion
  204.5 1.9 fusion.2
  206.9 4.1 fusion
  214.7 4.4 fusion.12
  219.1 1.5 pad_maximum_fusion.3
  220.6 1.5 pad_maximum_fusion.2
  222.1 1.6 pad_maximum_fusion.1
  223.7 2.8 collective-permute-start.5
  226.5 1.5 pad_maximum_fusion
  228.0 1.5 collective-permute-done.5
  229.6 41.2 %collective-permute-done.6.refs_4_.refs_3_ = bf16[4,128,4096]{2,1,0:T(8,128)(2,1)} collective-permute-done((bf16[4,128,4096]{2,1,0:T(8,128)(2,1)}, bf16[4,128,4096]{2,1,0:T(8,128)(2,1)}, u32[]{:S(2)}, u32[]{:S(2)}) %collective-permute-start.6) | collective-permute-done | bytes 4194336 | tf_op jit(solution)/shard_map/ppermute | solution.py:562
  270.7 2.4 collective-permute-done.7.refs_6_.refs_5_
  273.2 87.6 %collective-permute-done.8.refs_8_.refs_7_ = bf16[4,128,4096]{2,1,0:T(8,128)(2,1)} collective-permute-done((bf16[4,128,4096]{2,1,0:T(8,128)(2,1)}, bf16[4,128,4096]{2,1,0:T(8,128)(2,1)}, u32[]{:S(2)}, u32[]{:S(2)}) %collective-permute-start.8) | collective-permute-done | bytes 4194336 | tf_op jit(solution)/shard_map/ppermute | solution.py:562
  361.8 5.9 broadcast_select_fusion
  368.7 5.5 collective-permute-done.11.refs_7_.refs_6_
  374.8 5.4 collective-permute-done.12.refs_9_.refs_8_
  380.2 6.0 collective-permute-done.9.refs_3_.refs_2_
  386.2 81.9 %project_out.2 = (bf16[8,272,4096]{2,1,0:T(8,128)(2,1)}, bf16[2048,4096]{1,0:T(8,128)(2,1)}, f32[8,128]{1,0:T(8,128)}) custom-call(s32[1]{0:T(128)} %bitcast.where_ref, bf16[4,1,512,1024]{3,2,1,0:T(8,128)(2,1)} %bitcast.406, bf16[4,2,512,1024]{3,2,1,0:T(8,128)(2,1)} %bitcast.405, bf16[4,128,4096]{2,1,0:T(8,128)(2,1)} %bitcast.4.refs_2_.refs_1_, ...), custom_call_target="tpu_custom_call" | custom-call | flops 51539607552 | bytes 150994944 | tf_op jit(solution)/shard_map/project_out/pallas_call | solution.py:250
  468.4 1.6 collective-permute-start.17
  470.2 3.2 collective-permute-start.19
  474.2 31.6 %project_out.3 = (bf16[8,272,4096]{2,1,0:T(8,128)(2,1)}, bf16[2048,4096]{1,0:T(8,128)(2,1)}, bf16[16,4096]{1,0:T(8,128)(2,1)}, f32[8,128]{1,0:T(8,128)}) custom-call(s32[1]{0:T(128)} %bitcast.where_ref, bf16[4,1,512,1024]{3,2,1,0:T(8,128)(2,1)} %bitcast.391, ...), custom_call_target="tpu_custom_call", output_to_operand_aliasing={{0}: (15, {}), {1}: (16, {})} | custom-call | flops 17716740096 | bytes 50724864 | tf_op jit(solution)/shard_map/project_out/pallas_call | solution.py:250
  505.8 716.9 %mlp.1 = (bf16[2048,4096]{1,0:T(8,128)(2,1)}, bf16[8,4096]{1,0:T(8,128)(2,1)}) custom-call(f32[8,128]{1,0:T(8,128)} %get-tuple-element.190.token_ref, bf16[8,272,4096]{2,1,0:T(8,128)(2,1)} %get-tuple-element.191.normed_ref, bf16[16,4096]{1,0:T(8,128)(2,1)} %get-tuple-element.192.hextra_ref, bf16[2,2752,4096]{2,1,0:T(8,128)(2,1)} %bitcast.403, ...), custom_call_target="tpu_custom_call" | custom-call | flops 138512695296 | bytes 541065216 | tf_op jit(solution)/shard_map/mlp/pallas_call | solution.py:507
  1225.4 1.7 bitcast_dynamic-update-slice_fusion.7
  1227.1 1.9 slice.187
  1229.0 2.6 bitcast_dynamic-update-slice_fusion.2
  1231.7 2.0 bitcast_dynamic-update-slice_fusion.1
  1233.7 2.0 bitcast_dynamic-update-slice_fusion
  1235.8 6.2 copy.159
  (129 shorter events, 26.0 us)
Async XLA Ops:
  7.2 99.8 %all-gather.9.cloned.1.call-start = ((), (), s32[]{:S(2)}) async-start(), calls=%async_computation | async-start | bytes 5242880 | tf_op jit(solution)/shard_map/all_gather | solution.py:586
  9.5 365.3 %all-gather.11.cloned.1.call-start = ((), (), s32[]{:S(2)}) async-start(), calls=%async_computation.1 | async-start | bytes 5242880 | tf_op jit(solution)/shard_map/all_gather | solution.py:617
  9.6 24.1 %copy-start.21 = (bf16[2,4096]{1,0:T(2,128)(2,1)S(1)}, bf16[2,4096]{1,0:T(2,128)(2,1)}, u32[]{:S(2)}) copy-start(bf16[2,4096]{1,0:T(2,128)(2,1)} %param.14) | copy-start | bytes 49156
  9.6 24.8 %copy-start.22 = (s32[2]{0:T(128)S(1)}, s32[2]{0:T(128)}, u32[]{:S(2)}) copy-start(s32[2]{0:T(128)} %param.15) | copy-start | bytes 28
  80.9 1.6 copy-start
  82.5 1.6 copy-start.2
  84.1 0.7 copy-start.6
  84.8 8.9 copy-start.1
  93.4 292.8 %all-gather.13.cloned.1.call-start = ((), (), s32[]{:S(2)}) async-start(), calls=%async_computation.2 | async-start | bytes 10485760 | tf_op jit(solution)/shard_map/all_gather | solution.py:617
  93.7 1.6 copy-start.3
  106.4 0.6 copy-start.7
  145.3 1.6 copy-start.4
  146.9 0.7 copy-start.8
  163.6 304.6 %all-gather.15.cloned.1.call-start = ((), (), s32[]{:S(2)}) async-start(), calls=%async_computation.3 | async-start | bytes 5242880 | tf_op jit(solution)/shard_map/all_gather | solution.py:617
  165.8 35.0 %collective-permute-start = (bf16[3,2,8,128]{3,2,1,0:T(8,128)(2,1)S(1)}, bf16[3,2,8,128]{3,2,1,0:T(8,128)(2,1)S(1)}, u32[]{:S(2)}, u32[]{:S(2)}) collective-permute-start(bf16[3,2,8,128]{3,2,1,0:T(8,128)(2,1)S(1)} %constant_dynamic-update-slice_fusion), channel_id=1, source_target_pairs={{0,4},{4,8},{8,12},{12,0},{1,5},{5,9},{9,13},{13,1},{2,6},{6,10},{... | collective-permute-start | bytes 36872 | tf_op jit(solution)/shard_map/ppermute | solution.py:559
  169.0 32.5 %collective-permute-start.1 = (bf16[3,2,8,128]{3,2,1,0:T(8,128)(2,1)S(1)}, bf16[3,2,8,128]{3,2,1,0:T(8,128)(2,1)S(1)}, u32[]{:S(2)}, u32[]{:S(2)}) collective-permute-start(bf16[3,2,8,128]{3,2,1,0:T(8,128)(2,1)S(1)} %constant_dynamic-update-slice_fusion), channel_id=1, source_target_pairs={{0,8},{4,12},{8,0},{12,4},{1,9},{5,13},{9,1},{13,5},{2,10},{6,14},... | collective-permute-start | bytes 36872 | tf_op jit(solution)/shard_map/ppermute | solution.py:559
  171.5 29.9 %collective-permute-start.2 = (bf16[3,2,8,128]{3,2,1,0:T(8,128)(2,1)S(1)}, bf16[3,2,8,128]{3,2,1,0:T(8,128)(2,1)S(1)}, u32[]{:S(2)}, u32[]{:S(2)}) collective-permute-start(bf16[3,2,8,128]{3,2,1,0:T(8,128)(2,1)S(1)} %constant_dynamic-update-slice_fusion), channel_id=1, source_target_pairs={{0,12},{4,0},{8,4},{12,8},{1,13},{5,1},{9,5},{13,9},{2,14},{6,2},{... | collective-permute-start | bytes 36872 | tf_op jit(solution)/shard_map/ppermute | solution.py:559
  173.3 1.8 copy-start.20
  177.9 92.9 %collective-permute-start.6 = (bf16[4,128,4096]{2,1,0:T(8,128)(2,1)}, bf16[4,128,4096]{2,1,0:T(8,128)(2,1)}, u32[]{:S(2)}, u32[]{:S(2)}) collective-permute-start(bf16[4,128,4096]{2,1,0:T(8,128)(2,1)} %bitcast.4.refs_2_.refs_1_), channel_id=1, source_target_pairs={{0,2},{1,3},{2,0},{3,1},{16,18},{17,19},{18,16},{19,17},{4,6},{5,7... | collective-permute-start | bytes 12582920 | tf_op jit(solution)/shard_map/ppermute | solution.py:562
  179.4 93.8 %collective-permute-start.7 = (bf16[4,128,4096]{2,1,0:T(8,128)(2,1)}, bf16[4,128,4096]{2,1,0:T(8,128)(2,1)}, u32[]{:S(2)}, u32[]{:S(2)}) collective-permute-start(bf16[4,128,4096]{2,1,0:T(8,128)(2,1)} %bitcast.4.refs_2_.refs_1_), channel_id=1, source_target_pairs={{0,16},{1,17},{2,18},{3,19},{16,0},{17,1},{18,2},{19,3},{4,20},{5,... | collective-permute-start | bytes 12582920 | tf_op jit(solution)/shard_map/ppermute | solution.py:562
  180.9 1.6 copy-start.5
  182.5 19.0 %copy-start.11 = (bf16[1,2,256,32,128]{4,3,2,1,0:T(8,128)(2,1)S(1)}, bf16[1,2,256,32,128]{4,3,2,1,0:T(8,128)(2,1)}, u32[]{:S(2)}) copy-start(bf16[1,2,256,32,128]{4,3,2,1,0:T(8,128)(2,1)} %param.17) | copy-start | bytes 12582916
  182.5 19.0 %copy-start.12 = (bf16[1,2,256,32,128]{4,3,2,1,0:T(8,128)(2,1)S(1)}, bf16[1,2,256,32,128]{4,3,2,1,0:T(8,128)(2,1)}, u32[]{:S(2)}) copy-start(bf16[1,2,256,32,128]{4,3,2,1,0:T(8,128)(2,1)} %param.16) | copy-start | bytes 12582916
  200.9 3.7 copy-start.9
  200.9 159.9 %collective-permute-start.8 = (bf16[4,128,4096]{2,1,0:T(8,128)(2,1)}, bf16[4,128,4096]{2,1,0:T(8,128)(2,1)}, u32[]{:S(2)}, u32[]{:S(2)}) collective-permute-start(bf16[4,128,4096]{2,1,0:T(8,128)(2,1)} %bitcast.4.refs_2_.refs_1_), channel_id=1, source_target_pairs={{0,18},{1,19},{2,16},{3,17},{16,2},{17,3},{18,0},{19,1},{4,22},{5,... | collective-permute-start | bytes 12582920 | tf_op jit(solution)/shard_map/ppermute | solution.py:562
  204.5 6.7 copy-start.19
  211.2 1.6 copy-start.18
  212.8 1.8 copy-start.13
  212.8 1.8 copy-start.14
  212.8 1.9 copy-start.15
  213.5 10.1 collective-permute-start.3
  214.3 13.7 %collective-permute-start.4 = (f32[3,2,8,128]{3,2,1,0:T(8,128)S(1)}, f32[3,2,8,128]{3,2,1,0:T(8,128)S(1)}, u32[]{:S(2)}, u32[]{:S(2)}) collective-permute-start(f32[3,2,8,128]{3,2,1,0:T(8,128)S(1)} %get-tuple-element.231), channel_id=1, source_target_pairs={{0,8},{4,12},{8,0},{12,4},{1,9},{5,13},{9,1},{13,5},{2,10},{6,14},... | collective-permute-start | bytes 73736 | tf_op jit(solution)/shard_map/ppermute | solution.py:559
  223.7 5.8 collective-permute-start.5
  360.7 7.7 collective-permute-start.10
  360.7 13.5 %collective-permute-start.11 = (bf16[4,128,4096]{2,1,0:T(8,128)(2,1)}, bf16[4,128,4096]{2,1,0:T(8,128)(2,1)}, u32[]{:S(2)}, u32[]{:S(2)}) collective-permute-start(bf16[4,128,4096]{2,1,0:T(8,128)(2,1)} %collective-permute-done.7.refs_6_.refs_5_), channel_id=1, source_target_pairs={{0,1},{1,0},{2,3},{3,2},{16,17},{17,16},{18,19},{19,18},{4,5},{5,4... | collective-permute-start | bytes 12582920 | tf_op jit(solution)/shard_map/ppermute | solution.py:562
  361.2 19.0 %collective-permute-start.12 = (bf16[4,128,4096]{2,1,0:T(8,128)(2,1)}, bf16[4,128,4096]{2,1,0:T(8,128)(2,1)}, u32[]{:S(2)}, u32[]{:S(2)}) collective-permute-start(bf16[4,128,4096]{2,1,0:T(8,128)(2,1)} %collective-permute-done.8.refs_8_.refs_7_), channel_id=1, source_target_pairs={{0,1},{1,0},{2,3},{3,2},{16,17},{17,16},{18,19},{19,18},{4,5},{5,4... | collective-permute-start | bytes 12582920 | tf_op jit(solution)/shard_map/ppermute | solution.py:562
  361.3 25.0 %collective-permute-start.9 = (bf16[4,128,4096]{2,1,0:T(8,128)(2,1)}, bf16[4,128,4096]{2,1,0:T(8,128)(2,1)}, u32[]{:S(2)}, u32[]{:S(2)}) collective-permute-start(bf16[4,128,4096]{2,1,0:T(8,128)(2,1)} %bitcast.4.refs_2_.refs_1_), channel_id=1, source_target_pairs={{0,1},{1,0},{2,3},{3,2},{16,17},{17,16},{18,19},{19,18},{4,5},{5,4... | collective-permute-start | bytes 12582920 | tf_op jit(solution)/shard_map/ppermute | solution.py:562
  367.7 100.4 %collective-permute-start.13 = (bf16[2,1024]{1,0:T(2,128)(2,1)S(1)}, bf16[2,1024]{1,0:T(2,128)(2,1)S(1)}, u32[]{:S(2)}, u32[]{:S(2)}) collective-permute-start(bf16[2,1024]{1,0:T(2,128)(2,1)S(1)} %fusion.51), channel_id=1, source_target_pairs={{0,4},{4,8},{8,12},{12,0},{1,5},{5,9},{9,13},{13,1},{2,6},{6,10},{... | collective-permute-start | bytes 12296 | tf_op jit(solution)/shard_map/ppermute | solution.py:559
  368.4 99.8 %collective-permute-start.14 = (bf16[2,1024]{1,0:T(2,128)(2,1)S(1)}, bf16[2,1024]{1,0:T(2,128)(2,1)S(1)}, u32[]{:S(2)}, u32[]{:S(2)}) collective-permute-start(bf16[2,1024]{1,0:T(2,128)(2,1)S(1)} %fusion.51), channel_id=1, source_target_pairs={{0,8},{4,12},{8,0},{12,4},{1,9},{5,13},{9,1},{13,5},{2,10},{6,14},... | collective-permute-start | bytes 12296 | tf_op jit(solution)/shard_map/ppermute | solution.py:559
  374.2 93.9 %collective-permute-start.15 = (bf16[2,1024]{1,0:T(2,128)(2,1)S(1)}, bf16[2,1024]{1,0:T(2,128)(2,1)S(1)}, u32[]{:S(2)}, u32[]{:S(2)}) collective-permute-start(bf16[2,1024]{1,0:T(2,128)(2,1)S(1)} %fusion.51), channel_id=1, source_target_pairs={{0,12},{4,0},{8,4},{12,8},{1,13},{5,1},{9,5},{13,9},{2,14},{6,2},{... | collective-permute-start | bytes 12296 | tf_op jit(solution)/shard_map/ppermute | solution.py:559
  468.2 754.6 %collective-permute-start.16 = (bf16[2,512,8,128]{3,2,1,0:T(8,128)(2,1)}, bf16[2,512,8,128]{3,2,1,0:T(8,128)(2,1)}, u32[]{:S(2)}, u32[]{:S(2)}) collective-permute-start(bf16[2,512,8,128]{3,2,1,0:T(8,128)(2,1)} %pad_maximum_fusion), channel_id=1, source_target_pairs={{0,1},{1,2},{2,3},{3,0},{4,5},{5,6},{6,7},{7,4},{8,9},{9,10},{10,1... | collective-permute-start | bytes 6291464 | tf_op jit(solution)/shard_map/ppermute | solution.py:684
  468.4 754.4 %collective-permute-start.17 = (bf16[2,512,8,128]{3,2,1,0:T(8,128)(2,1)}, bf16[2,512,8,128]{3,2,1,0:T(8,128)(2,1)}, u32[]{:S(2)}, u32[]{:S(2)}) collective-permute-start(bf16[2,512,8,128]{3,2,1,0:T(8,128)(2,1)} %pad_maximum_fusion.2), channel_id=1, source_target_pairs={{0,9},{1,10},{2,11},{3,8},{4,13},{5,14},{6,15},{7,12},{8,1},{9,2},... | collective-permute-start | bytes 6291464 | tf_op jit(solution)/shard_map/ppermute | solution.py:684
  470.0 752.8 %collective-permute-start.18 = (bf16[2,512,8,128]{3,2,1,0:T(8,128)(2,1)}, bf16[2,512,8,128]{3,2,1,0:T(8,128)(2,1)}, u32[]{:S(2)}, u32[]{:S(2)}) collective-permute-start(bf16[2,512,8,128]{3,2,1,0:T(8,128)(2,1)} %pad_maximum_fusion.1), channel_id=1, source_target_pairs={{0,5},{1,6},{2,7},{3,4},{4,9},{5,10},{6,11},{7,8},{8,13},{9,14},{1... | collective-permute-start | bytes 6291464 | tf_op jit(solution)/shard_map/ppermute | solution.py:684
  470.2 756.9 %collective-permute-start.19 = (bf16[2,512,8,128]{3,2,1,0:T(8,128)(2,1)}, bf16[2,512,8,128]{3,2,1,0:T(8,128)(2,1)}, u32[]{:S(2)}, u32[]{:S(2)}) collective-permute-start(bf16[2,512,8,128]{3,2,1,0:T(8,128)(2,1)} %pad_maximum_fusion.3), channel_id=1, source_target_pairs={{0,13},{1,14},{2,15},{3,12},{4,1},{5,2},{6,3},{7,0},{8,5},{9,6},{1... | collective-permute-start | bytes 6291464 | tf_op jit(solution)/shard_map/ppermute | solution.py:684
  1224.8 11.0 copy-start.10
  1235.8 7.1 copy-start.16
  1235.8 8.4 copy-start.17
Sparse Core Ops, SparseCore 0:
  10.1 83.4 all-gather.8
  95.2 82.9 all-gather.10
  180.3 149.9 all-gather.12
  361.9 79.2 all-gather.14
where the time goes:
time: 1260 us; the launch traced here: 1250 us
  Pallas kernels  961 us (76%)
  waiting for transfers between devices  150 us (12%)
  local copies, waits for them, and re-layouts  67.6 us (5%)
  other arithmetic  28.6 us (2%)
  starting transfers between devices  23.1 us (2%)
  between operations  15.1 us (1%)
    pallas_call x1, Pallas kernels, mlp(): pl.pallas_call(functools.partial(mlp_kernel, size, chunk_rows, ff_steps,...  717 us
    ppermute x7, waiting for transfers between devices, swap(): lax.ppermute(value, group_axes, [(q, q ^ mask) for q in range(seats)])  148 us
    pallas_call x2, Pallas kernels, project_out(): pl.pallas_call(functools.partial(output_kernel, size, heads, len(contexts...  114 us
    pallas_call x2, Pallas kernels, project_qkv(): pl.pallas_call(functools.partial(qkv_kernel, head_dim, extra), out_shape=...  77.8 us
    pallas_call x4, Pallas kernels, attend(): pl.pallas_call(functools.partial(attend_kernel, chunk, chunks // 2, min(2...  52.6 us
    unnamed x69, local copies, waits for them, and re-layouts  50.7 us
  transfers between devices with their start and end apart: 24, of which 7 were waited for; matrix products, arithmetic and copies ran while one was open for 6% of the time, Pallas kernels for 77%

commit v1 on v0

--- a/solution.py
+++ b/solution.py
@@ -12,8 +12,8 @@
 NORM_EPS = 1e-5
 
 ORDER = (
-    'Q0', 'T0', 'G0', 'T1', 'w2', 'Q1', 'T2', 'G12', 'T3', 'G3', 'D1', 'K', 'D2', 'w3', 'O012', 'k2', 'k1', 'k3', 'k0',
-    'O3', 'B', 'l0', 'l2', 'l1', 'l3',
+    'Q0', 'T0', 'G0', 'T1', 'w2', 'Q1', 'T2', 'G12', 'T3', 'G3', 'D1', 'K', 'D2', 'w3', 'O012', 'k0', 'k2', 'k1', 'k3',
+    'O3', 'B', 'P',
 )
 
 
@@ -22,13 +22,40 @@
     return (values_f32 * inv_rms * gain_f32).astype(jnp.bfloat16)
 
 
-def rope_tables(positions, head_dim):
+def rope_frequencies(head_dim):
     half_dim = head_dim // 2
     inv_freq = ROPE_BASE ** (-2.0 * jnp.arange(half_dim, dtype=jnp.float32) / head_dim)
-    angles = positions.astype(jnp.float32)[:, None] * inv_freq[None, :]
-    cos_table = jnp.cos(angles)
-    sin_table = jnp.sin(angles)
-    return jnp.concatenate([cos_table, cos_table], axis=1), jnp.concatenate([-sin_table, sin_table], axis=1)
+    return jnp.concatenate([inv_freq, inv_freq])[None]
+
+
+def rope_tables(positions, head_dim):
+    angles = positions.astype(jnp.float32)[:, None] * rope_frequencies(head_dim)
+    sign = jnp.where(jnp.arange(head_dim) < head_dim // 2, -1.0, 1.0)
+    return jnp.cos(angles), jnp.sin(angles) * sign[None]
+
+
+def rope_kernel(freq_ref, cos_ref, sin_ref):
+    rows, head_dim = cos_ref.shape
+    positions = lax.broadcasted_iota(jnp.int32, (rows, head_dim), 0) + pl.program_id(0) * rows
+    angles = positions.astype(jnp.float32) * freq_ref[...]
+    turns = jnp.floor(angles * 0.15915494309189535 + 0.5)
+    angles = (angles - turns * 6.28125) - turns * 0.0019353071795864769
+    sine = jnp.sin(angles)
+    cos_ref[...] = jnp.cos(angles)
+    sin_ref[...] = jnp.where(lax.broadcasted_iota(jnp.int32, (rows, head_dim), 1) < head_dim // 2, -sine, sine)
+
+
+def rope_tables_upto(count, head_dim):
+    rows = min(64, count)
+    table = pl.BlockSpec((rows, head_dim), lambda n: (n, 0))
+    return pl.pallas_call(
+        rope_kernel,
+        out_shape=[jax.ShapeDtypeStruct((count, head_dim), jnp.float32)] * 2,
+        grid=(count // rows,),
+        in_specs=[pl.BlockSpec((1, head_dim), lambda n: (0, 0))],
+        out_specs=[table, table],
+        name="rope_tables",
+    )(rope_frequencies(head_dim))
 
 
 def qkv_kernel(head_dim, extra, *refs):
@@ -43,7 +70,13 @@
     @pl.when(pl.program_id(0) == 0)
     def _():
         gain = gain_ref[...].astype(jnp.float32)
-        normed_ref[chunk, :rows] = rms_scale(x_ref[...].astype(jnp.float32), gain)
+        block = min(64, rows)
+
+        @pl.loop(0, rows // block)
+        def _(number):
+            lines = pl.ds(pl.multiple_of(number * block, block), block)
+            normed_ref[chunk, lines] = rms_scale(x_ref[lines].astype(jnp.float32), gain)
+
         if extra:
             normed_ref[chunk, rows:] = rms_scale(extra_refs[0][...].astype(jnp.float32), gain)
         token_ref[...] = jnp.zeros_like(token_ref)
@@ -109,13 +142,14 @@
     rows, head_dim = q_ref.shape
     scale = head_dim ** -0.5
     limit = slen_ref[0]
-    for start in range(0, rows, q_rows):
-        query = q_ref[start:start + q_rows, :]
+
+    @pl.loop(0, rows // q_rows)
+    def _(number):
+        start = pl.multiple_of(number * q_rows, q_rows)
+        query = q_ref[pl.ds(start, q_rows), :]
         scores = []
-        values = []
         for part in range(chunk + 1):
-            keys = rows if part < chunk else start + q_rows
-            score = lax.dot_general(query, k_refs[part][:keys, :], (((1,), (1,)), ((), ())), preferred_element_type=jnp.float32) * scale
+            score = lax.dot_general(query, k_refs[part][...], (((1,), (1,)), ((), ())), preferred_element_type=jnp.float32) * scale
             key_pos = lax.broadcasted_iota(jnp.int32, score.shape, 1)
             if part == chunk:
                 allowed = key_pos <= lax.broadcasted_iota(jnp.int32, score.shape, 0) + start
@@ -125,15 +159,14 @@
             elif part >= first_checked:
                 score = jnp.where(key_pos < limit - part * rows, score, -1e30)
             scores.append(score)
-            values.append(v_refs[part][:keys, :])
         peak = functools.reduce(jnp.maximum, [jnp.max(score, axis=-1, keepdims=True) for score in scores])
         total = jnp.zeros((q_rows, 1), jnp.float32)
         mixed = jnp.zeros((q_rows, head_dim), jnp.float32)
-        for score, value in zip(scores, values):
+        for score, v_ref in zip(scores, v_refs):
             weight = jnp.exp(score - peak)
             total = total + jnp.sum(weight, axis=-1, keepdims=True)
-            mixed = mixed + jnp.dot(weight.astype(jnp.bfloat16), value, preferred_element_type=jnp.float32)
-        out_ref[start:start + q_rows, :] = (mixed / total).astype(out_ref.dtype)
+            mixed = mixed + jnp.dot(weight.astype(jnp.bfloat16), v_ref[...], preferred_element_type=jnp.float32)
+        out_ref[pl.ds(start, q_rows), :] = (mixed / total).astype(out_ref.dtype)
 
 
 def attend(chunk, chunks, rows, token, s_len, queries, keys, values, head_dim):
@@ -181,13 +214,14 @@
         for number, context_ref in enumerate(context_refs):
             @pl.when((chunk == 0) if number == 0 else (chunk > 0))
             def _():
-                for r in range(heads):
+                @pl.loop(0, heads)
+                def _(r):
                     columns = pl.ds(pl.multiple_of(lax.bitwise_xor(where_ref[0], r) * head_dim, head_dim), head_dim)
                     for t in range(size):
-                        there = (r * size + t) * head_dim
-                        full_ref[:rows, there:there + head_dim] = context_ref[t, 0, :, columns]
+                        there = pl.ds(pl.multiple_of((r * size + t) * head_dim, head_dim), head_dim)
+                        full_ref[:rows, there] = context_ref[t, 0, :, columns]
                         if extra:
-                            full_ref[rows:, there:there + head_dim] = context_x_ref[t, :, columns]
+                            full_ref[rows:, there] = context_x_ref[t, :, columns]
 
     w_block = jnp.concatenate([w_ref[...].reshape(size * head_dim, block) for w_ref in w_refs], axis=0)
     acc = jnp.dot(full_ref[...], w_block, preferred_element_type=jnp.float32)
@@ -206,15 +240,18 @@
     def _():
         half = rows // 2
         inv_rms = lax.rsqrt(square_ref[...] / depth + NORM_EPS)
-        for start in range(0, depth, block):
-            gain = gain_ref[:, start:start + block].astype(jnp.float32)
+
+        @pl.loop(0, depth // block)
+        def _(number):
+            columns = pl.ds(pl.multiple_of(number * block, block), block)
+            gain = gain_ref[:, columns].astype(jnp.float32)
             for part in range(2):
                 lo, hi = part * half, (part + 1) * half
-                normed_ref[part, :half, start:start + block] = (hidden_ref[lo:hi, start:start + block].astype(jnp.float32) * inv_rms[lo:hi] * gain).astype(jnp.bfloat16)
+                normed_ref[part, :half, columns] = (hidden_ref[lo:hi, columns].astype(jnp.float32) * inv_rms[lo:hi] * gain).astype(jnp.bfloat16)
                 if extra and part == 1:
-                    normed_ref[part, half:, start:start + block] = (hidden_x_ref[:, start:start + block].astype(jnp.float32) * inv_rms[rows:] * gain).astype(jnp.bfloat16)
+                    normed_ref[part, half:, columns] = (hidden_x_ref[:, columns].astype(jnp.float32) * inv_rms[rows:] * gain).astype(jnp.bfloat16)
                 else:
-                    normed_ref[part, half:, start:start + block] = jnp.zeros((normed_ref.shape[1] - half, block), jnp.bfloat16)
+                    normed_ref[part, half:, columns] = jnp.zeros((normed_ref.shape[1] - half, block), jnp.bfloat16)
 
 
 def project_out(first, count, chunks, pad, token, where, contexts, w_heads, x, gain, extras, buffers):
@@ -326,27 +363,26 @@
 
                 sum_copy(own_part(chain, slot), slot).start()
 
-            for hops in range(1, last):
-                m = slot - (last - hops)
-
-                @pl.when((place == hops) & (m >= 0) & (m < pieces))
-                def _():
-                    @pl.when(m >= 2)
-                    def _():
-                        sum_copy(outgoing.at[chain, lax.rem(m, 2)], m - 2).wait_send()
-
-                    sum_copy(outgoing.at[chain, lax.rem(m, 2)], m).wait_recv()
-                    outgoing[chain, lax.rem(m, 2)] = landed[chain, lax.rem(m, slots)] + own_part(chain, m)[...]
-
-                    @pl.when(m + slots < pieces)
-                    def _():
-                        pl.semaphore_signal(credit.at[chain], inc=1, device_id={'tp': farther}, device_id_type=pl.DeviceIdType.MESH)
-
-                    @pl.when(m >= slots)
-                    def _():
-                        pl.semaphore_wait(credit.at[chain], 1)
-
-                    sum_copy(outgoing.at[chain, lax.rem(m, 2)], m).start()
+            m = slot - (last - place)
+
+            @pl.when((place > 0) & (place < last) & (m >= 0) & (m < pieces))
+            def _():
+                @pl.when(m >= 2)
+                def _():
+                    sum_copy(outgoing.at[chain, lax.rem(m, 2)], m - 2).wait_send()
+
+                sum_copy(outgoing.at[chain, lax.rem(m, 2)], m).wait_recv()
+                outgoing[chain, lax.rem(m, 2)] = landed[chain, lax.rem(m, slots)] + own_part(chain, m)[...]
+
+                @pl.when(m + slots < pieces)
+                def _():
+                    pl.semaphore_signal(credit.at[chain], inc=1, device_id={'tp': farther}, device_id_type=pl.DeviceIdType.MESH)
+
+                @pl.when(m >= slots)
+                def _():
+                    pl.semaphore_wait(credit.at[chain], 1)
+
+                sum_copy(outgoing.at[chain, lax.rem(m, 2)], m).start()
 
             m = slot - last
 
@@ -386,18 +422,19 @@
                     src_ref=out_ref.at[out_rows(chain, m)], dst_ref=out_ref.at[out_rows(chain, m)], send_sem=ag_send.at[chain, lax.rem(m, 4)],
                     recv_sem=ag_recv.at[chain, lax.rem(m, 8)], device_id={'tp': farther}, device_id_type=pl.DeviceIdType.MESH)
 
-            for hops in range(1, size):
-                m = slot - last - 2 * hops
-
-                @pl.when((place == hops) & (m >= 0) & (m < pieces))
-                def _():
-                    relay_copy(m).wait_recv()
-                    if hops < last:
-                        @pl.when(m >= 4)
-                        def _():
-                            relay_copy(m - 4).wait_send()
-
-                        relay_copy(m).start()
+            m = slot - last - 2 * place
+
+            @pl.when((place > 0) & (m >= 0) & (m < pieces))
+            def _():
+                relay_copy(m).wait_recv()
+
+                @pl.when((place < last) & (m >= 4))
+                def _():
+                    relay_copy(m - 4).wait_send()
+
+                @pl.when(place < last)
+                def _():
+                    relay_copy(m).start()
 
     def extra_copy(d):
         return pltpu.make_async_remote_copy(
@@ -442,11 +479,11 @@
             def _():
                 acc[lax.rem(chunk, 3), :, start:start + block] += part
 
-    for sub in range(subs):
+    @pl.loop(0, subs)
+    def _(sub):
         exchange((step - ff_steps) * subs + sub)
         for part in range(2):
-            if part * subs // 2 == sub:
-                pl.when(step < chunks * ff_steps)((compute_gate, compute_down)[part])
+            pl.when((step < chunks * ff_steps) & (sub == part * subs // 2))((compute_gate, compute_down)[part])
 
     @pl.when(step == pl.num_programs(0) - 1)
     def _():
@@ -541,6 +578,40 @@
     )(token, normed, hextra, w_gate_up, w_down, hidden)
 
 
+def place_kernel(size, where_ref, *refs):
+    k_ref, v_ref = refs[-2:]
+    for d in range(size):
+        @pl.when(pl.program_id(0) == d)
+        def _():
+            k_ref[:, 0] = refs[d][0]
+            v_ref[:, 0] = refs[d][1]
+
+
+def place_caches(where, landed):
+    rows, heads, head_dim = landed[0].shape[1:]
+    size = len(landed)
+    block = rows // 4
+    blocks = rows // block
+
+    def turn(number):
+        return lambda d, n, where: (0, lax.select(d == number, n, lax.select(d < number, 0, blocks - 1)), 0, 0)
+
+    out = pl.BlockSpec((block, 1, heads, head_dim), lambda d, n, where: (n, lax.rem(where[0] - d + size, size), 0, 0))
+    return pl.pallas_call(
+        functools.partial(place_kernel, size),
+        out_shape=[jax.ShapeDtypeStruct((rows, size, heads, head_dim), jnp.bfloat16)] * 2,
+        grid_spec=pltpu.PrefetchScalarGridSpec(
+            num_scalar_prefetch=1,
+            grid=(size, blocks),
+            in_specs=[pl.BlockSpec((2, block, heads, head_dim), turn(d)) for d in range(size)],
+            out_specs=[out, out],
+        ),
+        compiler_params=pltpu.CompilerParams(dimension_semantics=("arbitrary", "arbitrary")),
+        cost_estimate=pl.CostEstimate(flops=0, bytes_accessed=8 * size * rows * heads * head_dim, transcendentals=0),
+        name="place_caches",
+    )(where, *landed)
+
+
 def pick_by(index, options):
     result = options[0]
     for place in range(1, len(options)):
@@ -586,13 +657,11 @@
         val['w', 0] = lax.all_gather(lax.dynamic_index_in_dim(w_out[0, :, 0], seat, 0, keepdims=False), 'tp', axis=0, tiled=False)
 
         val['w_all'] = jnp.swapaxes(w_qkv[0], 1, 2).reshape(depth, 3 * width)
-        tables = rope_tables(jnp.arange(seq_len, dtype=jnp.int32), head_dim)
+        tables = rope_tables_upto(seq_len, head_dim)
         extra_tables = rope_tables(jnp.concatenate([c_len, jnp.zeros((pad - decodes,), jnp.int32)]), head_dim)
         y_pad = jnp.concatenate([y_tok, jnp.zeros((pad - decodes, depth), y_tok.dtype)])
         val['gain'], val['s_len'], val['mlp_gain'] = attn_gain, s_len, mlp_gain
         val['valid'] = (jnp.arange(seq_len) < s_len[0]).astype(jnp.bfloat16)
-        for which in range(2):
-            val['cache', which] = jnp.zeros((rows, tp_size, heads_local, head_dim), jnp.bfloat16)
         buffers = []
         qkv = []
 
@@ -631,16 +700,17 @@
                 dec_full = jnp.concatenate(in_order(me, [val['dq', d] for d in range(tp_size)]), axis=2)
                 cache_pos = me * cache_local + jnp.arange(cache_local)
                 write_mask = (cache_pos[None, :] == c_len[:, None])[:, :, None, None]
-                allowed = (cache_pos[None, :] <= c_len[:, None])[:, None, :]
+                allowed = (cache_pos[None, :] <= c_len[:, None])[:, :, None]
                 key_now = jnp.where(write_mask, dec_full[1][:, None], k_cache[0])
                 value_now = jnp.where(write_mask, dec_full[2][:, None], v_cache[0])
                 val['key_now'], val['value_now'] = key_now, value_now
-                scores = jnp.einsum('bkh,btkh->bkt', dec_full[0], key_now, preferred_element_type=jnp.float32) * head_dim ** -0.5
+                scores = jnp.sum(dec_full[0][:, None].astype(jnp.float32) * key_now.astype(jnp.float32), axis=-1) * head_dim ** -0.5
                 scores = jnp.where(allowed, scores, -1e30)
-                peak = jnp.max(scores, axis=-1, keepdims=True)
+                peak = jnp.max(scores, axis=1, keepdims=True)
                 weights = jnp.exp(scores - peak)
-                total = jnp.sum(weights, axis=-1, keepdims=True)
-                mixed = jnp.einsum('bkt,btkh->bkh', weights.astype(jnp.bfloat16), value_now, preferred_element_type=jnp.float32)
+                total = jnp.sum(weights, axis=1)[..., None]
+                peak = peak[:, 0, :, None]
+                mixed = jnp.sum(weights.astype(jnp.bfloat16).astype(jnp.float32)[..., None] * value_now.astype(jnp.float32), axis=1)
                 packed = jnp.stack([mixed, jnp.broadcast_to(peak, mixed.shape), jnp.broadcast_to(total, mixed.shape)])
                 packed = packed.reshape(3, decodes, tp_size, heads_local, head_dim)
                 for d in range(tp_size):
@@ -673,6 +743,10 @@
                 if final:
                     val['hx'] = made[2]
                 return ['token']
+            if kind == 'P':
+                tie(thread + [('landed', d) for d in range(tp_size)])
+                val['k'], val['v'] = place_caches(me.reshape(1).astype(jnp.int32), [val['landed', d] for d in range(tp_size)])
+                return ['k']
             val['out'], val['y'] = mlp(val['token'], val['normed'], val['hx'], jnp.transpose(w_gate_up[0], (1, 2, 0)), w_down[0], val['h'], tp_size)
             return ['y']
 
@@ -683,12 +757,6 @@
                 route = [(t * side_size + s, ((t + d) % tp_size) * side_size + (s + 1) % side_size) for t in range(tp_size) for s in range(side_size)]
                 val['landed', d] = lax.ppermute(val['kv', d], ('tp', 'side'), route)
                 return
-            if name[0] == 'l':
-                d = int(name[1])
-                tie(thread + [('landed', d)])
-                for which in range(2):
-                    val['cache', which] = lax.dynamic_update_slice(val['cache', which], val['landed', d][which][:, None], (0, lax.rem(me - d + tp_size, tp_size), 0, 0))
-                return
             bases = [0] if name == 'w2' else list(range(0, seats, 2))
             kept = [] if name == 'w2' else [('kv', d) for d in range(tp_size)]
             tie(thread + kept + [('w', base) for base in bases])
@@ -699,13 +767,13 @@
         val['token'] = jnp.zeros(TOKEN.shape, TOKEN.dtype)
         thread = ['token']
         for name in ORDER:
-            if name[0] in 'QTGKDOB':
+            if name[0] in 'QTGKDOBP':
                 made = compute(name)
                 thread = thread + made if name in ('K', 'D1', 'D2') else made
             else:
                 transfer(name)
 
-        caches = [val['cache', which].reshape(1, 1, rows, tp_size * heads_local, head_dim) for which in range(2)]
+        caches = [val[name].reshape(1, 1, rows, tp_size * heads_local, head_dim) for name in 'kv']
         return (val['out'][None], val['y'][:decodes], caches[0], caches[1], val['key_now'][None], val['value_now'][None])
 
     cache_spec = P(None, group_axes, 'tp', None, None)

time: 1260 us -> 1270 us (level)
  Pallas kernels: 961 us -> 997 us
    pallas_call x0 -> x2, Pallas kernels: none -> 26.2 us  [the longest x1 13.1 us: rope_tables_upto(): pl.pallas_call(rope_kernel, out_shape=[jax.ShapeDtypeStruct((count, head_...]
    reduce_sum x0 -> x2, other arithmetic: none -> 15.5 us  [the longest x1 9.02 us: compute(): jnp.sum(dec_full[0][:, None].astype(jnp.float32) * key_now.astype(jnp.flo...]
    unnamed x69 -> x59, local copies, waits for them, and re-layouts: 50.7 us -> 57.5 us
where the time goes in v1:
time: 1270 us
  Pallas kernels  997 us (79%)
  waiting for transfers between devices  139 us (11%)
  local copies, waits for them, and re-layouts  62.8 us (5%)
  other arithmetic  36 us (3%)
  starting transfers between devices  20.1 us (2%)
  between operations  14.8 us (1%)
    pallas_call x1, Pallas kernels, mlp(): pl.pallas_call(functools.partial(mlp_kernel, size, chunk_rows, ff_steps,...  718 us
    ppermute x7, waiting for transfers between devices, swap(): lax.ppermute(value, group_axes, [(q, q ^ mask) for q in range(seats)])  137 us
    pallas_call x2, Pallas kernels, project_out(): pl.pallas_call(functools.partial(output_kernel, size, heads, len(contexts...  113 us
    pallas_call x2, Pallas kernels, project_qkv(): pl.pallas_call(functools.partial(qkv_kernel, head_dim, extra), out_shape=...  78.1 us
    pallas_call x4, Pallas kernels, attend(): pl.pallas_call(functools.partial(attend_kernel, chunk, chunks // 2, min(2...  61.4 us
    unnamed x59, local copies, waits for them, and re-layouts  57.5 us
  transfers between devices with their start and end apart: 24, of which 7 were waited for; matrix products, arithmetic and copies ran while one was open for 6% of the time, Pallas kernels for 77%

profile of v1, /device:TPU:0, one launch (start us, length us, event | category | flops | bytes accessed | tf_op | source)
XLA Modules:
  0.0 1269.6 jit_solution(4004482103409467547)
XLA Ops:
  7.2 2.3 constant_dynamic-slice_fusion
  10.2 13.1 %rope_tables.1 = (f32[2048,128]{1,0:T(8,128)}, f32[2048,128]{1,0:T(8,128)}) custom-call(f32[1,128]{1,0:T(1,128)} %get-tuple-element.270.freq_ref), custom_call_target="tpu_custom_call" | custom-call | tf_op jit(solution)/shard_map/rope_tables/pallas_call | solution.py:51
  23.3 23.2 %copy.88 = bf16[512,8,24,128]{3,1,2,0:T(8,128)(2,1)} copy(bf16[512,8,24,128]{3,2,1,0:T(8,128)(2,1)} %bitcast.339) | data formatting | bytes 50331648
  47.9 0.7 fusion.32
  49.2 39.7 %project_qkv.2 = (bf16[1024,1024]{1,0:T(8,128)(2,1)}, bf16[1024,1024]{1,0:T(8,128)(2,1)}, bf16[1024,1024]{1,0:T(8,128)(2,1)}, f32[8,128]{1,0:T(8,128)}, bf16[16,...) custom-call(bf16[2048,4096]{1,0:T(8,128)(2,1)} %bitcast.347, bf16[1,4096]{1,0:T(2,128)(2,1)} %refs_1_.1, ...), custom_call_target="tpu_custom_call" | custom-call | flops 25769803776 | bytes 39845888 | tf_op jit(solution)/shard_map/project_qkv/pallas_call | solution.py:115
  88.9 1.6 copy-done
  90.5 1.6 copy-done.2
  92.7 9.8 shard_map.163
  102.6 1.6 copy-done.3
  104.2 13.3 %shard_map.164 = (bf16[512,1024]{1,0:T(8,128)(2,1)S(1)}, f32[8,128]{1,0:T(8,128)S(1)}) custom-call(s32[1]{0:T(128)} %copy.94.slen_ref, bf16[1024,1024]{1,0:T(8,128)(2,1)S(1)} %copy-done.3, bf16[1024,1024]{1,0:T(8,128)(2,1)S(1)} %copy-done.1, bf16[1024,1024]{1,0:T(8,128)(2,1)S(1)} %copy-done.1, ...), custom_call_target="tpu_custom_call" | custom-call | flops 4294967296 | bytes 6291456 | tf_op jit(solution)/shard_map/pallas_call | solution.py:179
  118.1 38.4 %project_qkv.3 = (bf16[1024,1024]{1,0:T(8,128)(2,1)}, bf16[1024,1024]{1,0:T(8,128)(2,1)}, bf16[1024,1024]{1,0:T(8,128)(2,1)}, f32[8,128]{1,0:T(8,128)}) custom-call(bf16[2048,4096]{1,0:T(8,128)(2,1)} %bitcast.348, bf16[1,4096]{1,0:T(2,128)(2,1)} %refs_1_.1, bf16[4096,3072]{1,0:T(8,128)(2,1)} %bitcast.343, bf16[4096,3072]{1,0:T(8,128)(2,1)} %bitcast.344, ...), custom_call_target="tpu_custom_call" | custom-call | flops 25769803776 | bytes 39845888 | tf_op jit(solution)/shard_map/project_qkv/pallas_call | solution.py:115
  156.5 1.6 copy-done.4
  158.8 17.0 %shard_map.165 = (bf16[512,1024]{1,0:T(8,128)(2,1)S(1)}, f32[8,128]{1,0:T(8,128)S(1)}) custom-call(s32[1]{0:T(128)} %copy.94.slen_ref, bf16[1024,1024]{1,0:T(8,128)(2,1)S(1)} %copy-done.4, bf16[1024,1024]{1,0:T(8,128)(2,1)S(1)} %copy-done.1, bf16[1024,1024]{1,0:T(8,128)(2,1)S(1)} %copy-done.1, bf16[1024,1024]{1,0:T(8,128)(2,1)} %get-tuple-element.128.refs_3_.refs_4_, ...), custom_call_target="tpu_custom_call" | custom-call | flops 6442450944 | bytes 8388608 | tf_op jit(solution)/shard_map/pallas_call | solution.py:179
  175.8 1.5 pad_maximum_fusion.4
  179.5 3.1 collective-permute-start
  182.6 2.6 collective-permute-start.1
  185.2 1.3 collective-permute-start.2
  187.0 1.3 copy.42
  188.5 1.3 copy.47
  189.8 1.3 copy.46
  191.1 1.5 collective-permute-start.6
  192.7 1.5 collective-permute-start.7
  194.2 1.9 copy-done.5
  196.0 21.3 %shard_map.166 = (bf16[512,1024]{1,0:T(8,128)(2,1)}, f32[8,128]{1,0:T(8,128)S(1)}) custom-call(s32[1]{0:T(128)} %copy.94.slen_ref, bf16[1024,1024]{1,0:T(8,128)(2,1)S(1)} %copy-done.5, bf16[1024,1024]{1,0:T(8,128)(2,1)S(1)} %copy-done.1, bf16[1024,1024]{1,0:T(8,128)(2,1)S(1)} %copy-done.1, bf16[1024,1024]{1,0:T(8,128)(2,1)} %get-tuple-element.128.refs_3_.refs_4_, ...), custom_call_target="tpu_custom_call" | custom-call | flops 8589934592 | bytes 10485760 | tf_op jit(solution)/shard_map/pallas_call | solution.py:179
  217.7 9.0 multiply_reduce_fusion.1
  227.2 6.5 multiply_reduce_fusion
  234.0 1.9 slice_bitcast_fusion.7
  238.3 4.4 fusion.8
  242.7 1.6 pad_maximum_fusion.3
  244.3 1.6 pad_maximum_fusion.2
  245.8 1.5 pad_maximum_fusion.1
  247.3 2.8 collective-permute-start.5
  250.2 1.5 pad_maximum_fusion
  251.7 1.8 collective-permute-done.5
  253.6 30.4 %collective-permute-done.6.refs_4_.refs_3_ = bf16[4,128,4096]{2,1,0:T(8,128)(2,1)} collective-permute-done((bf16[4,128,4096]{2,1,0:T(8,128)(2,1)}, bf16[4,128,4096]{2,1,0:T(8,128)(2,1)}, u32[]{:S(2)}, u32[]{:S(2)}) %collective-permute-start.6) | collective-permute-done | bytes 4194336 | tf_op jit(solution)/shard_map/ppermute | solution.py:633
  284.0 2.4 collective-permute-done.7.refs_6_.refs_5_
  286.4 87.6 %collective-permute-done.8.refs_8_.refs_7_ = bf16[4,128,4096]{2,1,0:T(8,128)(2,1)} collective-permute-done((bf16[4,128,4096]{2,1,0:T(8,128)(2,1)}, bf16[4,128,4096]{2,1,0:T(8,128)(2,1)}, u32[]{:S(2)}, u32[]{:S(2)}) %collective-permute-start.8) | collective-permute-done | bytes 4194336 | tf_op jit(solution)/shard_map/ppermute | solution.py:633
  375.1 5.9 broadcast_select_fusion
  382.0 5.5 collective-permute-done.11.refs_7_.refs_6_
  388.0 5.5 collective-permute-done.12.refs_9_.refs_8_
  393.5 6.0 collective-permute-done.9.refs_3_.refs_2_
  399.5 81.4 %project_out.2 = (bf16[8,272,4096]{2,1,0:T(8,128)(2,1)}, bf16[2048,4096]{1,0:T(8,128)(2,1)}, f32[8,128]{1,0:T(8,128)}) custom-call(s32[1]{0:T(128)} %bitcast.where_ref, bf16[4,1,512,1024]{3,2,1,0:T(8,128)(2,1)} %bitcast.364, bf16[4,2,512,1024]{3,2,1,0:T(8,128)(2,1)} %bitcast.363, bf16[4,128,4096]{2,1,0:T(8,128)(2,1)} %bitcast.5.refs_2_.refs_1_, ...), custom_call_target="tpu_custom_call" | custom-call | flops 51539607552 | bytes 150994944 | tf_op jit(solution)/shard_map/project_out/pallas_call | solution.py:287
  481.2 2.5 collective-permute-start.17
  485.0 31.6 %project_out.3 = (bf16[8,272,4096]{2,1,0:T(8,128)(2,1)}, bf16[2048,4096]{1,0:T(8,128)(2,1)}, bf16[16,4096]{1,0:T(8,128)(2,1)}, f32[8,128]{1,0:T(8,128)}) custom-call(s32[1]{0:T(128)} %bitcast.where_ref, bf16[4,1,512,1024]{3,2,1,0:T(8,128)(2,1)} %bitcast.351, ...), custom_call_target="tpu_custom_call", output_to_operand_aliasing={{0}: (15, {}), {1}: (16, {})} | custom-call | flops 17716740096 | bytes 50724864 | tf_op jit(solution)/shard_map/project_out/pallas_call | solution.py:287
  516.5 718.0 %mlp.1 = (bf16[2048,4096]{1,0:T(8,128)(2,1)}, bf16[8,4096]{1,0:T(8,128)(2,1)}) custom-call(f32[8,128]{1,0:T(8,128)} %get-tuple-element.193.token_ref, bf16[8,272,4096]{2,1,0:T(8,128)(2,1)} %get-tuple-element.194.normed_ref, bf16[16,4096]{1,0:T(8,128)(2,1)} %get-tuple-element.195.hextra_ref, bf16[2,2752,4096]{2,1,0:T(8,128)(2,1)} %bitcast.361, ...), custom_call_target="tpu_custom_call" | custom-call | flops 138512695296 | bytes 541065216 | tf_op jit(solution)/shard_map/mlp/pallas_call | solution.py:544
  1234.5 1.5 slice.163
  1236.0 13.1 %place_caches.1 = (bf16[512,4,8,128]{3,2,1,0:T(8,128)(2,1)}, bf16[512,4,8,128]{3,2,1,0:T(8,128)(2,1)}) custom-call(s32[1]{0:T(128)} %bitcast.30.where_ref, bf16[2,512,8,128]{3,2,1,0:T(8,128)(2,1)} %collective-permute-done.16.refs_0_, bf16[2,512,8,128]{3,2,1,0:T(8,128)(2,1)} %collective-permute-done.17.refs_1_, ...), custom_call_target="tpu_custom_call" | custom-call | bytes 16777216 | tf_op jit(solution)/shard_map/place_caches/pallas_call | solution.py:600
  1249.1 14.1 %copy.95 = bf16[1,2048,4096]{2,1,0:T(8,128)(2,1)} copy(bf16[1,2048,4096]{2,1,0:T(8,128)(2,1)} %bitcast.346) | data formatting | bytes 33554432
  (110 shorter events, 14.6 us)
Async XLA Ops:
  7.2 110.9 %all-gather.9.cloned.1.call-start = ((), (), s32[]{:S(2)}) async-start(), calls=%async_computation | async-start | bytes 5242880 | tf_op jit(solution)/shard_map/all_gather | solution.py:657
  9.5 378.5 %all-gather.11.cloned.1.call-start = ((), (), s32[]{:S(2)}) async-start(), calls=%async_computation.1 | async-start | bytes 5242880 | tf_op jit(solution)/shard_map/all_gather | solution.py:686
  23.3 23.9 %copy-start.16 = (bf16[2,4096]{1,0:T(2,128)(2,1)S(1)}, bf16[2,4096]{1,0:T(2,128)(2,1)}, u32[]{:S(2)}) copy-start(bf16[2,4096]{1,0:T(2,128)(2,1)} %param.14) | copy-start | bytes 49156
  23.3 24.6 %copy-start.17 = (s32[2]{0:T(128)S(1)}, s32[2]{0:T(128)}, u32[]{:S(2)}) copy-start(s32[2]{0:T(128)} %param.15) | copy-start | bytes 28
  88.9 1.6 copy-start
  90.5 1.6 copy-start.2
  92.0 0.7 copy-start.6
  92.7 9.9 copy-start.1
  102.6 297.0 %all-gather.13.cloned.1.call-start = ((), (), s32[]{:S(2)}) async-start(), calls=%async_computation.2 | async-start | bytes 10485760 | tf_op jit(solution)/shard_map/all_gather | solution.py:686
  102.6 1.6 copy-start.3
  117.5 0.6 copy-start.7
  156.5 1.6 copy-start.4
  158.1 0.7 copy-start.8
  177.3 303.7 %all-gather.15.cloned.1.call-start = ((), (), s32[]{:S(2)}) async-start(), calls=%async_computation.3 | async-start | bytes 5242880 | tf_op jit(solution)/shard_map/all_gather | solution.py:686
  179.5 37.8 %collective-permute-start = (bf16[3,2,8,128]{3,2,1,0:T(8,128)(2,1)S(1)}, bf16[3,2,8,128]{3,2,1,0:T(8,128)(2,1)S(1)}, u32[]{:S(2)}, u32[]{:S(2)}) collective-permute-start(bf16[3,2,8,128]{3,2,1,0:T(8,128)(2,1)S(1)} %constant_dynamic-update-slice_fusion), channel_id=1, source_target_pairs={{0,4},{4,8},{8,12},{12,0},{1,5},{5,9},{9,13},{13,1},{2,6},{6,10},{... | collective-permute-start | bytes 36872 | tf_op jit(solution)/shard_map/ppermute | solution.py:630
  182.6 35.0 %collective-permute-start.1 = (bf16[3,2,8,128]{3,2,1,0:T(8,128)(2,1)S(1)}, bf16[3,2,8,128]{3,2,1,0:T(8,128)(2,1)S(1)}, u32[]{:S(2)}, u32[]{:S(2)}) collective-permute-start(bf16[3,2,8,128]{3,2,1,0:T(8,128)(2,1)S(1)} %constant_dynamic-update-slice_fusion), channel_id=1, source_target_pairs={{0,8},{4,12},{8,0},{12,4},{1,9},{5,13},{9,1},{13,5},{2,10},{6,14},... | collective-permute-start | bytes 36872 | tf_op jit(solution)/shard_map/ppermute | solution.py:630
  185.2 32.5 %collective-permute-start.2 = (bf16[3,2,8,128]{3,2,1,0:T(8,128)(2,1)S(1)}, bf16[3,2,8,128]{3,2,1,0:T(8,128)(2,1)S(1)}, u32[]{:S(2)}, u32[]{:S(2)}) collective-permute-start(bf16[3,2,8,128]{3,2,1,0:T(8,128)(2,1)S(1)} %constant_dynamic-update-slice_fusion), channel_id=1, source_target_pairs={{0,12},{4,0},{8,4},{12,8},{1,13},{5,1},{9,5},{13,9},{2,14},{6,2},{... | collective-permute-start | bytes 36872 | tf_op jit(solution)/shard_map/ppermute | solution.py:630
  186.6 1.8 copy-start.15
  191.1 92.9 %collective-permute-start.6 = (bf16[4,128,4096]{2,1,0:T(8,128)(2,1)}, bf16[4,128,4096]{2,1,0:T(8,128)(2,1)}, u32[]{:S(2)}, u32[]{:S(2)}) collective-permute-start(bf16[4,128,4096]{2,1,0:T(8,128)(2,1)} %bitcast.5.refs_2_.refs_1_), channel_id=1, source_target_pairs={{0,2},{1,3},{2,0},{3,1},{16,18},{17,19},{18,16},{19,17},{4,6},{5,7... | collective-permute-start | bytes 12582920 | tf_op jit(solution)/shard_map/ppermute | solution.py:633
  192.7 93.8 %collective-permute-start.7 = (bf16[4,128,4096]{2,1,0:T(8,128)(2,1)}, bf16[4,128,4096]{2,1,0:T(8,128)(2,1)}, u32[]{:S(2)}, u32[]{:S(2)}) collective-permute-start(bf16[4,128,4096]{2,1,0:T(8,128)(2,1)} %bitcast.5.refs_2_.refs_1_), channel_id=1, source_target_pairs={{0,16},{1,17},{2,18},{3,19},{16,0},{17,1},{18,2},{19,3},{4,20},{5,... | collective-permute-start | bytes 12582920 | tf_op jit(solution)/shard_map/ppermute | solution.py:633
  194.2 1.9 copy-start.5
  196.0 21.7 %copy-start.10 = (bf16[1,2,256,32,128]{4,3,2,1,0:T(8,128)(2,1)S(1)}, bf16[1,2,256,32,128]{4,3,2,1,0:T(8,128)(2,1)}, u32[]{:S(2)}) copy-start(bf16[1,2,256,32,128]{4,3,2,1,0:T(8,128)(2,1)} %param.16) | copy-start | bytes 12582916
  217.3 16.4 %copy-start.9 = (f32[8,128]{1,0:T(8,128)}, f32[8,128]{1,0:T(8,128)S(1)}, u32[]{:S(2)}) copy-start(f32[8,128]{1,0:T(8,128)S(1)} %get-tuple-element.172.refs_12_) | copy-start | bytes 12292
  217.4 156.7 %collective-permute-start.8 = (bf16[4,128,4096]{2,1,0:T(8,128)(2,1)}, bf16[4,128,4096]{2,1,0:T(8,128)(2,1)}, u32[]{:S(2)}, u32[]{:S(2)}) collective-permute-start(bf16[4,128,4096]{2,1,0:T(8,128)(2,1)} %bitcast.5.refs_2_.refs_1_), channel_id=1, source_target_pairs={{0,18},{1,19},{2,16},{3,17},{16,2},{17,3},{18,0},{19,1},{4,22},{5,... | collective-permute-start | bytes 12582920 | tf_op jit(solution)/shard_map/ppermute | solution.py:633
  234.0 2.4 copy-start.14
  236.4 1.7 copy-start.11
  236.4 1.7 copy-start.12
  236.4 1.9 copy-start.13
  237.2 10.1 collective-permute-start.3
  237.9 13.8 %collective-permute-start.4 = (f32[3,2,8,128]{3,2,1,0:T(8,128)S(1)}, f32[3,2,8,128]{3,2,1,0:T(8,128)S(1)}, u32[]{:S(2)}, u32[]{:S(2)}) collective-permute-start(f32[3,2,8,128]{3,2,1,0:T(8,128)S(1)} %get-tuple-element.229), channel_id=1, source_target_pairs={{0,8},{4,12},{8,0},{12,4},{1,9},{5,13},{9,1},{13,5},{2,10},{6,14},... | collective-permute-start | bytes 73736 | tf_op jit(solution)/shard_map/ppermute | solution.py:630
  247.3 6.2 collective-permute-start.5
  374.0 7.7 collective-permute-start.10
  374.0 13.5 %collective-permute-start.11 = (bf16[4,128,4096]{2,1,0:T(8,128)(2,1)}, bf16[4,128,4096]{2,1,0:T(8,128)(2,1)}, u32[]{:S(2)}, u32[]{:S(2)}) collective-permute-start(bf16[4,128,4096]{2,1,0:T(8,128)(2,1)} %collective-permute-done.7.refs_6_.refs_5_), channel_id=1, source_target_pairs={{0,1},{1,0},{2,3},{3,2},{16,17},{17,16},{18,19},{19,18},{4,5},{5,4... | collective-permute-start | bytes 12582920 | tf_op jit(solution)/shard_map/ppermute | solution.py:633
  374.5 19.0 %collective-permute-start.12 = (bf16[4,128,4096]{2,1,0:T(8,128)(2,1)}, bf16[4,128,4096]{2,1,0:T(8,128)(2,1)}, u32[]{:S(2)}, u32[]{:S(2)}) collective-permute-start(bf16[4,128,4096]{2,1,0:T(8,128)(2,1)} %collective-permute-done.8.refs_8_.refs_7_), channel_id=1, source_target_pairs={{0,1},{1,0},{2,3},{3,2},{16,17},{17,16},{18,19},{19,18},{4,5},{5,4... | collective-permute-start | bytes 12582920 | tf_op jit(solution)/shard_map/ppermute | solution.py:633
  374.5 25.0 %collective-permute-start.9 = (bf16[4,128,4096]{2,1,0:T(8,128)(2,1)}, bf16[4,128,4096]{2,1,0:T(8,128)(2,1)}, u32[]{:S(2)}, u32[]{:S(2)}) collective-permute-start(bf16[4,128,4096]{2,1,0:T(8,128)(2,1)} %bitcast.5.refs_2_.refs_1_), channel_id=1, source_target_pairs={{0,1},{1,0},{2,3},{3,2},{16,17},{17,16},{18,19},{19,18},{4,5},{5,4... | collective-permute-start | bytes 12582920 | tf_op jit(solution)/shard_map/ppermute | solution.py:633
  381.0 99.9 %collective-permute-start.13 = (bf16[2,1024]{1,0:T(2,128)(2,1)S(1)}, bf16[2,1024]{1,0:T(2,128)(2,1)S(1)}, u32[]{:S(2)}, u32[]{:S(2)}) collective-permute-start(bf16[2,1024]{1,0:T(2,128)(2,1)S(1)} %fusion.45), channel_id=1, source_target_pairs={{0,4},{4,8},{8,12},{12,0},{1,5},{5,9},{9,13},{13,1},{2,6},{6,10},{... | collective-permute-start | bytes 12296 | tf_op jit(solution)/shard_map/ppermute | solution.py:630
  381.7 99.2 %collective-permute-start.14 = (bf16[2,1024]{1,0:T(2,128)(2,1)S(1)}, bf16[2,1024]{1,0:T(2,128)(2,1)S(1)}, u32[]{:S(2)}, u32[]{:S(2)}) collective-permute-start(bf16[2,1024]{1,0:T(2,128)(2,1)S(1)} %fusion.45), channel_id=1, source_target_pairs={{0,8},{4,12},{8,0},{12,4},{1,9},{5,13},{9,1},{13,5},{2,10},{6,14},... | collective-permute-start | bytes 12296 | tf_op jit(solution)/shard_map/ppermute | solution.py:630
  387.5 93.4 %collective-permute-start.15 = (bf16[2,1024]{1,0:T(2,128)(2,1)S(1)}, bf16[2,1024]{1,0:T(2,128)(2,1)S(1)}, u32[]{:S(2)}, u32[]{:S(2)}) collective-permute-start(bf16[2,1024]{1,0:T(2,128)(2,1)S(1)} %fusion.45), channel_id=1, source_target_pairs={{0,12},{4,0},{8,4},{12,8},{1,13},{5,1},{9,5},{13,9},{2,14},{6,2},{... | collective-permute-start | bytes 12296 | tf_op jit(solution)/shard_map/ppermute | solution.py:630
  480.9 753.5 %collective-permute-start.19 = (bf16[2,512,8,128]{3,2,1,0:T(8,128)(2,1)}, bf16[2,512,8,128]{3,2,1,0:T(8,128)(2,1)}, u32[]{:S(2)}, u32[]{:S(2)}) collective-permute-start(bf16[2,512,8,128]{3,2,1,0:T(8,128)(2,1)} %pad_maximum_fusion.3), channel_id=1, source_target_pairs={{0,13},{1,14},{2,15},{3,12},{4,1},{5,2},{6,3},{7,0},{8,5},{9,6},{1... | collective-permute-start | bytes 6291464 | tf_op jit(solution)/shard_map/ppermute | solution.py:758
  481.2 753.3 %collective-permute-start.17 = (bf16[2,512,8,128]{3,2,1,0:T(8,128)(2,1)}, bf16[2,512,8,128]{3,2,1,0:T(8,128)(2,1)}, u32[]{:S(2)}, u32[]{:S(2)}) collective-permute-start(bf16[2,512,8,128]{3,2,1,0:T(8,128)(2,1)} %pad_maximum_fusion.1), channel_id=1, source_target_pairs={{0,5},{1,6},{2,7},{3,4},{4,9},{5,10},{6,11},{7,8},{8,13},{9,14},{1... | collective-permute-start | bytes 6291464 | tf_op jit(solution)/shard_map/ppermute | solution.py:758
  483.7 750.8 %collective-permute-start.18 = (bf16[2,512,8,128]{3,2,1,0:T(8,128)(2,1)}, bf16[2,512,8,128]{3,2,1,0:T(8,128)(2,1)}, u32[]{:S(2)}, u32[]{:S(2)}) collective-permute-start(bf16[2,512,8,128]{3,2,1,0:T(8,128)(2,1)} %pad_maximum_fusion.2), channel_id=1, source_target_pairs={{0,9},{1,10},{2,11},{3,8},{4,13},{5,14},{6,15},{7,12},{8,1},{9,2},... | collective-permute-start | bytes 6291464 | tf_op jit(solution)/shard_map/ppermute | solution.py:758
  483.9 750.6 %collective-permute-start.16 = (bf16[2,512,8,128]{3,2,1,0:T(8,128)(2,1)}, bf16[2,512,8,128]{3,2,1,0:T(8,128)(2,1)}, u32[]{:S(2)}, u32[]{:S(2)}) collective-permute-start(bf16[2,512,8,128]{3,2,1,0:T(8,128)(2,1)} %pad_maximum_fusion), channel_id=1, source_target_pairs={{0,1},{1,2},{2,3},{3,0},{4,5},{5,6},{6,7},{7,4},{8,9},{9,10},{10,1... | collective-permute-start | bytes 6291464 | tf_op jit(solution)/shard_map/ppermute | solution.py:758
Sparse Core Ops, SparseCore 0:
  10.1 83.4 all-gather.8
  102.7 83.8 all-gather.10
  188.7 149.9 all-gather.12
  375.2 79.2 all-gather.14

commit v2 on v1

--- a/solution.py
+++ b/solution.py
@@ -12,7 +12,7 @@
 NORM_EPS = 1e-5
 
 ORDER = (
-    'Q0', 'T0', 'G0', 'T1', 'w2', 'Q1', 'T2', 'G12', 'T3', 'G3', 'D1', 'K', 'D2', 'w3', 'O012', 'k0', 'k2', 'k1', 'k3',
+    'Q0', 'T0', 'G0', 'T1', 'w2', 'Q1', 'T2', 'G12', 'T3', 'G3', 'K', 'k1', 'k3', 'D1', 'D2', 'w3', 'O012', 'k0', 'k2',
     'O3', 'B', 'P',
 )
 
@@ -34,36 +34,22 @@
     return jnp.cos(angles), jnp.sin(angles) * sign[None]
 
 
-def rope_kernel(freq_ref, cos_ref, sin_ref):
-    rows, head_dim = cos_ref.shape
-    positions = lax.broadcasted_iota(jnp.int32, (rows, head_dim), 0) + pl.program_id(0) * rows
-    angles = positions.astype(jnp.float32) * freq_ref[...]
+def rope_rows(first, rows, freq):
+    head_dim = freq.shape[1]
+    positions = lax.broadcasted_iota(jnp.int32, (rows, head_dim), 0) + first
+    angles = positions.astype(jnp.float32) * freq
     turns = jnp.floor(angles * 0.15915494309189535 + 0.5)
     angles = (angles - turns * 6.28125) - turns * 0.0019353071795864769
     sine = jnp.sin(angles)
-    cos_ref[...] = jnp.cos(angles)
-    sin_ref[...] = jnp.where(lax.broadcasted_iota(jnp.int32, (rows, head_dim), 1) < head_dim // 2, -sine, sine)
-
-
-def rope_tables_upto(count, head_dim):
-    rows = min(64, count)
-    table = pl.BlockSpec((rows, head_dim), lambda n: (n, 0))
-    return pl.pallas_call(
-        rope_kernel,
-        out_shape=[jax.ShapeDtypeStruct((count, head_dim), jnp.float32)] * 2,
-        grid=(count // rows,),
-        in_specs=[pl.BlockSpec((1, head_dim), lambda n: (0, 0))],
-        out_specs=[table, table],
-        name="rope_tables",
-    )(rope_frequencies(head_dim))
-
-
-def qkv_kernel(head_dim, extra, *refs):
-    x_ref, gain_ref, wq_ref, wk_ref, wv_ref, cos_ref, sin_ref = refs[:7]
-    extra_refs = refs[7:10] if extra else None
-    normed_ref = refs[-1]
-    q_ref, k_ref, v_ref, token_ref = refs[-5 - 3 * extra:-1 - 3 * extra]
-    extra_outs = refs[-4:-1] if extra else (None,) * 3
+    return jnp.cos(angles), jnp.where(lax.broadcasted_iota(jnp.int32, (rows, head_dim), 1) < head_dim // 2, -sine, sine)
+
+
+def qkv_kernel(half, head_dim, extra, *refs):
+    x_ref, gain_ref, wq_ref, wk_ref, wv_ref, freq_ref = refs[:6]
+    extra_refs = refs[6:9] if extra else None
+    normed_ref, cos_ref, sin_ref = refs[-3:]
+    q_ref, k_ref, v_ref, token_ref = refs[-7 - 3 * extra:-3 - 3 * extra]
+    extra_outs = refs[-6:-3] if extra else (None,) * 3
     rows = x_ref.shape[0]
     chunk = pl.program_id(1)
 
@@ -76,12 +62,13 @@
         def _(number):
             lines = pl.ds(pl.multiple_of(number * block, block), block)
             normed_ref[chunk, lines] = rms_scale(x_ref[lines].astype(jnp.float32), gain)
+            cos_ref[chunk, lines], sin_ref[chunk, lines] = rope_rows((2 * half + chunk) * rows + number * block, block, freq_ref[...])
 
         if extra:
             normed_ref[chunk, rows:] = rms_scale(extra_refs[0][...].astype(jnp.float32), gain)
         token_ref[...] = jnp.zeros_like(token_ref)
 
-    cos, sin = cos_ref[...], sin_ref[...]
+    cos, sin = cos_ref[chunk], sin_ref[chunk]
     if extra:
         cos = jnp.concatenate([cos, extra_refs[1][...]], axis=0)
         sin = jnp.concatenate([sin, extra_refs[2][...]], axis=0)
@@ -99,7 +86,7 @@
 TOKEN = jax.ShapeDtypeStruct((8, 128), jnp.float32)
 
 
-def project_qkv(half, rows, token, x, extra_rows, gain, w_all, tables, extra_tables, head_dim):
+def project_qkv(half, rows, token, x, extra_rows, gain, w_all, extra_tables, head_dim):
     depth = x.shape[1]
     width = w_all.shape[1] // 3
     block = 2 * head_dim
@@ -110,10 +97,9 @@
     bf16 = jnp.bfloat16
     whole = lambda shape: pl.BlockSpec(shape, lambda n, c: (0, 0), pipeline_mode=pl.Buffered(1))
     columns = lambda part: pl.BlockSpec((depth, block), lambda n, c: (0, part * steps + n))
-    table = pl.BlockSpec((rows, head_dim), lambda n, c: (2 * half + c, 0))
     extra_outs = [jax.ShapeDtypeStruct((pad, width), bf16)] * 3 if extra else []
     return pl.pallas_call(
-        functools.partial(qkv_kernel, head_dim, extra),
+        functools.partial(qkv_kernel, half, head_dim, extra),
         out_shape=[jax.ShapeDtypeStruct((2 * rows, width), bf16)] * 3 + [TOKEN] + extra_outs,
         grid=(steps, 2),
         in_specs=[
@@ -122,15 +108,14 @@
             columns(0),
             columns(1),
             columns(2),
-            table,
-            table,
+            whole((1, head_dim)),
         ] + [whole(e.shape) for e in extras] + [pl.BlockSpec(memory_space=pl.ANY)],
         out_specs=[pl.BlockSpec((rows, block), lambda n, c: (c, n))] * 3 + [whole(TOKEN.shape)] + [pl.BlockSpec((pad, block), lambda n, c: (0, n))] * len(extra_outs),
-        scratch_shapes=[pltpu.VMEM((2, rows + pad, depth), bf16)],
+        scratch_shapes=[pltpu.VMEM((2, rows + pad, depth), bf16)] + [pltpu.VMEM((2, rows, head_dim), jnp.float32)] * 2,
         compiler_params=pltpu.CompilerParams(dimension_semantics=("arbitrary", "arbitrary"), vmem_limit_bytes=56 << 20),
         cost_estimate=pl.CostEstimate(flops=12 * rows * depth * width, bytes_accessed=2 * (2 * rows * depth + 3 * depth * width + 6 * rows * width), transcendentals=0),
         name="project_qkv",
-    )(x, gain, w_all, w_all, w_all, *tables, *extras, token)
+    )(x, gain, w_all, w_all, w_all, rope_frequencies(head_dim), *extras, token)
 
 
 def attend_kernel(chunk, first_checked, q_rows, slen_ref, *refs):
@@ -590,7 +575,7 @@
 def place_caches(where, landed):
     rows, heads, head_dim = landed[0].shape[1:]
     size = len(landed)
-    block = rows // 4
+    block = rows // 2
     blocks = rows // block
 
     def turn(number):
@@ -606,8 +591,8 @@
             in_specs=[pl.BlockSpec((2, block, heads, head_dim), turn(d)) for d in range(size)],
             out_specs=[out, out],
         ),
-        compiler_params=pltpu.CompilerParams(dimension_semantics=("arbitrary", "arbitrary")),
-        cost_estimate=pl.CostEstimate(flops=0, bytes_accessed=8 * size * rows * heads * head_dim, transcendentals=0),
+        compiler_params=pltpu.CompilerParams(dimension_semantics=("arbitrary", "arbitrary"), vmem_limit_bytes=16 << 20),
+        cost_estimate=pl.CostEstimate(flops=20 * rows * size * heads * head_dim, bytes_accessed=8 * size * rows * heads * head_dim, transcendentals=0),
         name="place_caches",
     )(where, *landed)
 
@@ -657,7 +642,6 @@
         val['w', 0] = lax.all_gather(lax.dynamic_index_in_dim(w_out[0, :, 0], seat, 0, keepdims=False), 'tp', axis=0, tiled=False)
 
         val['w_all'] = jnp.swapaxes(w_qkv[0], 1, 2).reshape(depth, 3 * width)
-        tables = rope_tables_upto(seq_len, head_dim)
         extra_tables = rope_tables(jnp.concatenate([c_len, jnp.zeros((pad - decodes,), jnp.int32)]), head_dim)
         y_pad = jnp.concatenate([y_tok, jnp.zeros((pad - decodes, depth), y_tok.dtype)])
         val['gain'], val['s_len'], val['mlp_gain'] = attn_gain, s_len, mlp_gain
@@ -670,7 +654,7 @@
             c = int(name[1:]) if name[1:].isdigit() else 0
             if kind == 'Q':
                 tie(thread + ['gain'])
-                made = project_qkv(c, rows, val['token'], x_prompt[0], y_pad if c == 0 else None, val['gain'], val['w_all'], tables, extra_tables, head_dim)
+                made = project_qkv(c, rows, val['token'], x_prompt[0], y_pad if c == 0 else None, val['gain'], val['w_all'], extra_tables, head_dim)
                 val['token'] = made[3]
                 qkv.append(made[:3])
                 if c == 0:
@@ -758,7 +742,7 @@
                 val['landed', d] = lax.ppermute(val['kv', d], ('tp', 'side'), route)
                 return
             bases = [0] if name == 'w2' else list(range(0, seats, 2))
-            kept = [] if name == 'w2' else [('kv', d) for d in range(tp_size)]
+            kept = [] if name == 'w2' else [('kv', 0), ('kv', 2)]
             tie(thread + kept + [('w', base) for base in bases])
             for mask in (range(2, seats, 2) if name == 'w2' else [1]):
                 for base in bases:

time: 1270 us -> 1220 us (0.961)
  Pallas kernels: 997 us -> 896 us
  waiting for transfers between devices: 139 us -> 190 us
    pallas_call x1, Pallas kernels: 718 us -> 630 us  [mlp(): pl.pallas_call(functools.partial(mlp_kernel, size, chunk_rows, ff_steps,...]
    ppermute x9, waiting for transfers between devices: 1.85 us -> 64.6 us  [cyclic(): lax.ppermute(value, 'tp', [(t, (t + d) % tp_size) for t in range(tp_size)])]
    pallas_call x3 -> x2, Pallas kernels: 91.2 us -> 81.8 us  [project_qkv(): pl.pallas_call(functools.partial(qkv_kernel, half, head_dim, extra), out_...]
    unnamed x59 -> x63, local copies, waits for them, and re-layouts: 57.5 us -> 57 us
  transfers between devices with their start and end apart: 24 -> 24, of which waited for: 7 -> 10; matrix products, arithmetic and copies ran while one was open for 6% -> 6% of each run, Pallas kernels for 77% -> 72%
where the time goes in v2:
time: 1220 us
  Pallas kernels  896 us (73%)
  waiting for transfers between devices  190 us (16%)
  local copies, waits for them, and re-layouts  62.3 us (5%)
  other arithmetic  38.3 us (3%)
  starting transfers between devices  22.2 us (2%)
  between operations  14.8 us (1%)
    pallas_call x1, Pallas kernels, mlp(): pl.pallas_call(functools.partial(mlp_kernel, size, chunk_rows, ff_steps,...  630 us
    ppermute x7, waiting for transfers between devices, swap(): lax.ppermute(value, group_axes, [(q, q ^ mask) for q in range(seats)])  125 us
    pallas_call x2, Pallas kernels, project_out(): pl.pallas_call(functools.partial(output_kernel, size, heads, len(contexts...  113 us
    pallas_call x2, Pallas kernels, project_qkv(): pl.pallas_call(functools.partial(qkv_kernel, half, head_dim, extra), out_...  81.8 us
    ppermute x9, waiting for transfers between devices, cyclic(): lax.ppermute(value, 'tp', [(t, (t + d) % tp_size) for t in range(tp_size)])  64.6 us
    pallas_call x4, Pallas kernels, attend(): pl.pallas_call(functools.partial(attend_kernel, chunk, chunks // 2, min(2...  61.3 us
    unnamed x63, local copies, waits for them, and re-layouts  57 us
  transfers between devices with their start and end apart: 24, of which 10 were waited for; matrix products, arithmetic and copies ran while one was open for 6% of the time, Pallas kernels for 72%

profile of v2, /device:TPU:0, one launch (start us, length us, event | category | flops | bytes accessed | tf_op | source)
XLA Modules:
  0.0 1223.6 jit_solution(11476685791500892945)
XLA Ops:
  7.2 2.3 constant_dynamic-slice_fusion
  9.6 23.3 %copy.88 = bf16[512,8,24,128]{3,1,2,0:T(8,128)(2,1)} copy(bf16[512,8,24,128]{3,2,1,0:T(8,128)(2,1)} %bitcast.339) | data formatting | bytes 50331648
  36.3 41.5 %project_qkv.2 = (bf16[1024,1024]{1,0:T(8,128)(2,1)}, bf16[1024,1024]{1,0:T(8,128)(2,1)}, bf16[1024,1024]{1,0:T(8,128)(2,1)}, f32[8,128]{1,0:T(8,128)}, bf16[16,...) custom-call(bf16[2048,4096]{1,0:T(8,128)(2,1)} %bitcast.347, bf16[1,4096]{1,0:T(2,128)(2,1)} %refs_1_.1, ...), custom_call_target="tpu_custom_call" | custom-call | flops 25769803776 | bytes 39845888 | tf_op jit(solution)/shard_map/project_qkv/pallas_call | solution.py:101
  77.8 1.6 copy-done
  79.4 1.6 copy-done.2
  81.7 9.8 shard_map.163
  91.6 1.6 copy-done.3
  93.2 13.3 %shard_map.164 = (bf16[512,1024]{1,0:T(8,128)(2,1)S(1)}, f32[8,128]{1,0:T(8,128)S(1)}) custom-call(s32[1]{0:T(128)} %copy.94.slen_ref, bf16[1024,1024]{1,0:T(8,128)(2,1)S(1)} %copy-done.3, bf16[1024,1024]{1,0:T(8,128)(2,1)S(1)} %copy-done.1, bf16[1024,1024]{1,0:T(8,128)(2,1)S(1)} %copy-done.1, ...), custom_call_target="tpu_custom_call" | custom-call | flops 4294967296 | bytes 6291456 | tf_op jit(solution)/shard_map/pallas_call | solution.py:164
  107.1 40.3 %project_qkv.3 = (bf16[1024,1024]{1,0:T(8,128)(2,1)}, bf16[1024,1024]{1,0:T(8,128)(2,1)}, bf16[1024,1024]{1,0:T(8,128)(2,1)}, f32[8,128]{1,0:T(8,128)}) custom-call(bf16[2048,4096]{1,0:T(8,128)(2,1)} %bitcast.348, bf16[1,4096]{1,0:T(2,128)(2,1)} %refs_1_.1, bf16[4096,3072]{1,0:T(8,128)(2,1)} %bitcast.343, bf16[4096,3072]{1,0:T(8,128)(2,1)} %bitcast.344, ...), custom_call_target="tpu_custom_call" | custom-call | flops 25769803776 | bytes 39845888 | tf_op jit(solution)/shard_map/project_qkv/pallas_call | solution.py:101
  147.4 1.6 copy-done.4
  149.7 16.9 %shard_map.165 = (bf16[512,1024]{1,0:T(8,128)(2,1)S(1)}, f32[8,128]{1,0:T(8,128)S(1)}) custom-call(s32[1]{0:T(128)} %copy.94.slen_ref, bf16[1024,1024]{1,0:T(8,128)(2,1)S(1)} %copy-done.4, bf16[1024,1024]{1,0:T(8,128)(2,1)S(1)} %copy-done.1, bf16[1024,1024]{1,0:T(8,128)(2,1)S(1)} %copy-done.1, bf16[1024,1024]{1,0:T(8,128)(2,1)} %get-tuple-element.121.refs_3_.refs_4_, ...), custom_call_target="tpu_custom_call" | custom-call | flops 6442450944 | bytes 8388608 | tf_op jit(solution)/shard_map/pallas_call | solution.py:164
  166.6 1.5 pad_maximum_fusion.4
  170.4 3.3 collective-permute-start
  173.7 2.5 collective-permute-start.1
  176.7 1.3 copy.25
  178.2 1.3 copy.32
  180.9 1.5 collective-permute-start.6
  182.4 1.5 collective-permute-start.7
  184.4 2.2 slice_bitcast_fusion.6
  188.9 21.2 %shard_map.166 = (bf16[512,1024]{1,0:T(8,128)(2,1)}, f32[8,128]{1,0:T(8,128)S(1)}) custom-call(s32[1]{0:T(128)} %copy.94.slen_ref, bf16[1024,1024]{1,0:T(8,128)(2,1)S(1)} %copy-done.5, bf16[1024,1024]{1,0:T(8,128)(2,1)S(1)} %copy-done.1, bf16[1024,1024]{1,0:T(8,128)(2,1)S(1)} %copy-done.1, bf16[1024,1024]{1,0:T(8,128)(2,1)} %get-tuple-element.121.refs_3_.refs_4_, ...), custom_call_target="tpu_custom_call" | custom-call | flops 8589934592 | bytes 10485760 | tf_op jit(solution)/shard_map/pallas_call | solution.py:164
  210.2 5.8 fusion.8
  216.0 1.6 pad_maximum_fusion.1
  217.6 1.4 collective-permute-start.2
  219.0 1.5 pad_maximum_fusion
  220.5 4.0 collective-permute-done.2
  224.6 9.0 multiply_reduce_fusion.1
  234.8 6.6 multiply_reduce_fusion
  242.8 1.5 pad_maximum_fusion.3
  244.3 3.9 collective-permute-done.3
  248.3 1.5 pad_maximum_fusion.2
  249.8 4.0 collective-permute-done.4
  253.9 19.9 %collective-permute-done.6.refs_4_.refs_3_ = bf16[4,128,4096]{2,1,0:T(8,128)(2,1)} collective-permute-done((bf16[4,128,4096]{2,1,0:T(8,128)(2,1)}, bf16[4,128,4096]{2,1,0:T(8,128)(2,1)}, u32[]{:S(2)}, u32[]{:S(2)}) %collective-permute-start.6) | collective-permute-done | bytes 4194336 | tf_op jit(solution)/shard_map/ppermute | solution.py:618
  273.7 2.4 collective-permute-done.7.refs_6_.refs_5_
  276.2 87.8 %collective-permute-done.8.refs_8_.refs_7_ = bf16[4,128,4096]{2,1,0:T(8,128)(2,1)} collective-permute-done((bf16[4,128,4096]{2,1,0:T(8,128)(2,1)}, bf16[4,128,4096]{2,1,0:T(8,128)(2,1)}, u32[]{:S(2)}, u32[]{:S(2)}) %collective-permute-start.8) | collective-permute-done | bytes 4194336 | tf_op jit(solution)/shard_map/ppermute | solution.py:618
  366.0 5.9 broadcast_select_fusion
  371.9 1.8 collective-permute-start.17
  373.7 3.8 collective-permute-done.11.refs_7_.refs_6_
  377.9 5.6 collective-permute-done.12.refs_9_.refs_8_
  383.9 5.6 collective-permute-done.9.refs_3_.refs_2_
  389.5 1.3 collective-permute-start.15
  390.8 81.4 %project_out.2 = (bf16[8,272,4096]{2,1,0:T(8,128)(2,1)}, bf16[2048,4096]{1,0:T(8,128)(2,1)}, f32[8,128]{1,0:T(8,128)}) custom-call(s32[1]{0:T(128)} %bitcast.where_ref, bf16[4,1,512,1024]{3,2,1,0:T(8,128)(2,1)} %bitcast.364, bf16[4,2,512,1024]{3,2,1,0:T(8,128)(2,1)} %bitcast.363, bf16[4,128,4096]{2,1,0:T(8,128)(2,1)} %bitcast.5.refs_2_.refs_1_, ...), custom_call_target="tpu_custom_call" | custom-call | flops 51539607552 | bytes 150994944 | tf_op jit(solution)/shard_map/project_out/pallas_call | solution.py:272
  472.2 52.7 %collective-permute-done.13 = bf16[2,1024]{1,0:T(2,128)(2,1)S(1)} collective-permute-done((bf16[2,1024]{1,0:T(2,128)(2,1)S(1)}, bf16[2,1024]{1,0:T(2,128)(2,1)S(1)}, u32[]{:S(2)}, u32[]{:S(2)}) %collective-permute-start.13) | collective-permute-done | bytes 4128 | tf_op jit(solution)/shard_map/ppermute | solution.py:615
  525.0 3.1 collective-permute-start.18
  529.8 31.4 %project_out.3 = (bf16[8,272,4096]{2,1,0:T(8,128)(2,1)}, bf16[2048,4096]{1,0:T(8,128)(2,1)}, bf16[16,4096]{1,0:T(8,128)(2,1)}, f32[8,128]{1,0:T(8,128)}) custom-call(s32[1]{0:T(128)} %bitcast.where_ref, bf16[4,1,512,1024]{3,2,1,0:T(8,128)(2,1)} %bitcast.351, ...), custom_call_target="tpu_custom_call", output_to_operand_aliasing={{0}: (15, {}), {1}: (16, {})} | custom-call | flops 17716740096 | bytes 50724864 | tf_op jit(solution)/shard_map/project_out/pallas_call | solution.py:272
  561.3 630.2 %mlp.1 = (bf16[2048,4096]{1,0:T(8,128)(2,1)}, bf16[8,4096]{1,0:T(8,128)(2,1)}) custom-call(f32[8,128]{1,0:T(8,128)} %get-tuple-element.183.token_ref, bf16[8,272,4096]{2,1,0:T(8,128)(2,1)} %get-tuple-element.184.normed_ref, bf16[16,4096]{1,0:T(8,128)(2,1)} %get-tuple-element.185.hextra_ref, bf16[2,2752,4096]{2,1,0:T(8,128)(2,1)} %bitcast.361, ...), custom_call_target="tpu_custom_call" | custom-call | flops 138512695296 | bytes 541065216 | tf_op jit(solution)/shard_map/mlp/pallas_call | solution.py:529
  1191.5 1.5 slice.163
  1193.0 10.0 place_caches.1
  1203.0 14.1 %copy.95 = bf16[1,2048,4096]{2,1,0:T(8,128)(2,1)} copy(bf16[1,2048,4096]{2,1,0:T(8,128)(2,1)} %bitcast.346) | data formatting | bytes 33554432
  (113 shorter events, 19.1 us)
Async XLA Ops:
  7.2 99.9 %all-gather.9.cloned.1.call-start = ((), (), s32[]{:S(2)}) async-start(), calls=%async_computation | async-start | bytes 5242880 | tf_op jit(solution)/shard_map/all_gather | solution.py:642
  9.5 381.3 %all-gather.11.cloned.1.call-start = ((), (), s32[]{:S(2)}) async-start(), calls=%async_computation.1 | async-start | bytes 5242880 | tf_op jit(solution)/shard_map/all_gather | solution.py:670
  9.6 24.0 %copy-start.18 = (bf16[2,4096]{1,0:T(2,128)(2,1)S(1)}, bf16[2,4096]{1,0:T(2,128)(2,1)}, u32[]{:S(2)}) copy-start(bf16[2,4096]{1,0:T(2,128)(2,1)} %param.14) | copy-start | bytes 49156
  9.6 24.7 %copy-start.19 = (s32[2]{0:T(128)S(1)}, s32[2]{0:T(128)}, u32[]{:S(2)}) copy-start(s32[2]{0:T(128)} %param.15) | copy-start | bytes 28
  77.8 1.6 copy-start
  79.4 1.6 copy-start.2
  81.0 0.7 copy-start.6
  81.7 9.9 copy-start.1
  91.5 299.3 %all-gather.13.cloned.1.call-start = ((), (), s32[]{:S(2)}) async-start(), calls=%async_computation.2 | async-start | bytes 10485760 | tf_op jit(solution)/shard_map/all_gather | solution.py:670
  91.6 1.6 copy-start.3
  106.5 0.6 copy-start.7
  147.4 1.6 copy-start.4
  149.0 0.7 copy-start.8
  168.1 356.8 %all-gather.15.cloned.1.call-start = ((), (), s32[]{:S(2)}) async-start(), calls=%async_computation.3 | async-start | bytes 5242880 | tf_op jit(solution)/shard_map/all_gather | solution.py:670
  170.4 47.2 %collective-permute-start = (bf16[3,2,8,128]{3,2,1,0:T(8,128)(2,1)S(1)}, bf16[3,2,8,128]{3,2,1,0:T(8,128)(2,1)S(1)}, u32[]{:S(2)}, u32[]{:S(2)}) collective-permute-start(bf16[3,2,8,128]{3,2,1,0:T(8,128)(2,1)S(1)} %constant_dynamic-update-slice_fusion), channel_id=1, source_target_pairs={{0,4},{4,8},{8,12},{12,0},{1,5},{5,9},{9,13},{13,1},{2,6},{6,10},{... | collective-permute-start | bytes 36872 | tf_op jit(solution)/shard_map/ppermute | solution.py:615
  173.7 46.8 %collective-permute-start.1 = (bf16[3,2,8,128]{3,2,1,0:T(8,128)(2,1)S(1)}, bf16[3,2,8,128]{3,2,1,0:T(8,128)(2,1)S(1)}, u32[]{:S(2)}, u32[]{:S(2)}) collective-permute-start(bf16[3,2,8,128]{3,2,1,0:T(8,128)(2,1)S(1)} %constant_dynamic-update-slice_fusion), channel_id=1, source_target_pairs={{0,8},{4,12},{8,0},{12,4},{1,9},{5,13},{9,1},{13,5},{2,10},{6,14},... | collective-permute-start | bytes 36872 | tf_op jit(solution)/shard_map/ppermute | solution.py:615
  176.3 1.8 copy-start.16
  180.9 92.9 %collective-permute-start.6 = (bf16[4,128,4096]{2,1,0:T(8,128)(2,1)}, bf16[4,128,4096]{2,1,0:T(8,128)(2,1)}, u32[]{:S(2)}, u32[]{:S(2)}) collective-permute-start(bf16[4,128,4096]{2,1,0:T(8,128)(2,1)} %bitcast.5.refs_2_.refs_1_), channel_id=1, source_target_pairs={{0,2},{1,3},{2,0},{3,1},{16,18},{17,19},{18,16},{19,17},{4,6},{5,7... | collective-permute-start | bytes 12582920 | tf_op jit(solution)/shard_map/ppermute | solution.py:618
  182.4 93.8 %collective-permute-start.7 = (bf16[4,128,4096]{2,1,0:T(8,128)(2,1)}, bf16[4,128,4096]{2,1,0:T(8,128)(2,1)}, u32[]{:S(2)}, u32[]{:S(2)}) collective-permute-start(bf16[4,128,4096]{2,1,0:T(8,128)(2,1)} %bitcast.5.refs_2_.refs_1_), channel_id=1, source_target_pairs={{0,16},{1,17},{2,18},{3,19},{16,0},{17,1},{18,2},{19,3},{4,20},{5,... | collective-permute-start | bytes 12582920 | tf_op jit(solution)/shard_map/ppermute | solution.py:618
  183.9 180.1 %collective-permute-start.8 = (bf16[4,128,4096]{2,1,0:T(8,128)(2,1)}, bf16[4,128,4096]{2,1,0:T(8,128)(2,1)}, u32[]{:S(2)}, u32[]{:S(2)}) collective-permute-start(bf16[4,128,4096]{2,1,0:T(8,128)(2,1)} %bitcast.5.refs_2_.refs_1_), channel_id=1, source_target_pairs={{0,18},{1,19},{2,16},{3,17},{16,2},{17,3},{18,0},{19,1},{4,22},{5,... | collective-permute-start | bytes 12582920 | tf_op jit(solution)/shard_map/ppermute | solution.py:618
  184.4 2.7 copy-start.17
  187.1 1.8 copy-start.5
  188.9 21.2 %copy-start.11 = (bf16[64,8,8,128]{3,2,1,0:T(8,128)(2,1)S(1)}, bf16[64,8,8,128]{3,2,1,0:T(8,128)(2,1)}, u32[]{:S(2)}) copy-start(bf16[64,8,8,128]{3,2,1,0:T(8,128)(2,1)} %copy.25) | copy-start | bytes 3145732
  188.9 21.2 %copy-start.12 = (bf16[64,8,8,128]{3,2,1,0:T(8,128)(2,1)S(1)}, bf16[64,8,8,128]{3,2,1,0:T(8,128)(2,1)}, u32[]{:S(2)}) copy-start(bf16[64,8,8,128]{3,2,1,0:T(8,128)(2,1)} %copy.32) | copy-start | bytes 3145732
  188.9 21.2 %copy-start.13 = (bf16[64,8,8,128]{3,2,1,0:T(8,128)(2,1)S(1)}, bf16[64,8,8,128]{3,2,1,0:T(8,128)(2,1)}, u32[]{:S(2)}) copy-start(bf16[64,8,8,128]{3,2,1,0:T(8,128)(2,1)} %copy.29) | copy-start | bytes 3145732
  210.1 5.9 copy-start.9
  216.0 8.6 copy-start.10
  217.6 7.0 collective-permute-start.2
  224.6 18.1 %copy-start.14 = (bf16[1,512,8,128]{3,2,1,0:T(8,128)(2,1)S(1)}, bf16[1,512,8,128]{3,2,1,0:T(8,128)(2,1)}, u32[]{:S(2)}) copy-start(bf16[1,512,8,128]{3,2,1,0:T(8,128)(2,1)} %get-tuple-element.204) | copy-start | bytes 3145732
  234.8 7.9 copy-start.15
  241.7 6.5 collective-permute-start.3
  241.8 12.0 collective-permute-start.4
  248.2 5.6 collective-permute-start.5
  364.0 7.9 collective-permute-start.10
  364.0 13.5 %collective-permute-start.11 = (bf16[4,128,4096]{2,1,0:T(8,128)(2,1)}, bf16[4,128,4096]{2,1,0:T(8,128)(2,1)}, u32[]{:S(2)}, u32[]{:S(2)}) collective-permute-start(bf16[4,128,4096]{2,1,0:T(8,128)(2,1)} %collective-permute-done.7.refs_6_.refs_5_), channel_id=1, source_target_pairs={{0,1},{1,0},{2,3},{3,2},{16,17},{17,16},{18,19},{19,18},{4,5},{5,4... | collective-permute-start | bytes 12582920 | tf_op jit(solution)/shard_map/ppermute | solution.py:618
  364.5 19.0 %collective-permute-start.12 = (bf16[4,128,4096]{2,1,0:T(8,128)(2,1)}, bf16[4,128,4096]{2,1,0:T(8,128)(2,1)}, u32[]{:S(2)}, u32[]{:S(2)}) collective-permute-start(bf16[4,128,4096]{2,1,0:T(8,128)(2,1)} %collective-permute-done.8.refs_8_.refs_7_), channel_id=1, source_target_pairs={{0,1},{1,0},{2,3},{3,2},{16,17},{17,16},{18,19},{19,18},{4,5},{5,4... | collective-permute-start | bytes 12582920 | tf_op jit(solution)/shard_map/ppermute | solution.py:618
  364.5 25.0 %collective-permute-start.9 = (bf16[4,128,4096]{2,1,0:T(8,128)(2,1)}, bf16[4,128,4096]{2,1,0:T(8,128)(2,1)}, u32[]{:S(2)}, u32[]{:S(2)}) collective-permute-start(bf16[4,128,4096]{2,1,0:T(8,128)(2,1)} %bitcast.5.refs_2_.refs_1_), channel_id=1, source_target_pairs={{0,1},{1,0},{2,3},{3,2},{16,17},{17,16},{18,19},{19,18},{4,5},{5,4... | collective-permute-start | bytes 12582920 | tf_op jit(solution)/shard_map/ppermute | solution.py:618
  365.0 826.4 %collective-permute-start.19 = (bf16[2,512,8,128]{3,2,1,0:T(8,128)(2,1)}, bf16[2,512,8,128]{3,2,1,0:T(8,128)(2,1)}, u32[]{:S(2)}, u32[]{:S(2)}) collective-permute-start(bf16[2,512,8,128]{3,2,1,0:T(8,128)(2,1)} %pad_maximum_fusion.1), channel_id=1, source_target_pairs={{0,13},{1,14},{2,15},{3,12},{4,1},{5,2},{6,3},{7,0},{8,5},{9,6},{1... | collective-permute-start | bytes 6291464 | tf_op jit(solution)/shard_map/ppermute | solution.py:742
  371.9 819.5 %collective-permute-start.17 = (bf16[2,512,8,128]{3,2,1,0:T(8,128)(2,1)}, bf16[2,512,8,128]{3,2,1,0:T(8,128)(2,1)}, u32[]{:S(2)}, u32[]{:S(2)}) collective-permute-start(bf16[2,512,8,128]{3,2,1,0:T(8,128)(2,1)} %pad_maximum_fusion), channel_id=1, source_target_pairs={{0,5},{1,6},{2,7},{3,4},{4,9},{5,10},{6,11},{7,8},{8,13},{9,14},{1... | collective-permute-start | bytes 6291464 | tf_op jit(solution)/shard_map/ppermute | solution.py:742
  377.5 147.4 %collective-permute-start.13 = (bf16[2,1024]{1,0:T(2,128)(2,1)S(1)}, bf16[2,1024]{1,0:T(2,128)(2,1)S(1)}, u32[]{:S(2)}, u32[]{:S(2)}) collective-permute-start(bf16[2,1024]{1,0:T(2,128)(2,1)S(1)} %fusion.45), channel_id=1, source_target_pairs={{0,4},{4,8},{8,12},{12,0},{1,5},{5,9},{9,13},{13,1},{2,6},{6,10},{... | collective-permute-start | bytes 12296 | tf_op jit(solution)/shard_map/ppermute | solution.py:615
  383.5 141.4 %collective-permute-start.14 = (bf16[2,1024]{1,0:T(2,128)(2,1)S(1)}, bf16[2,1024]{1,0:T(2,128)(2,1)S(1)}, u32[]{:S(2)}, u32[]{:S(2)}) collective-permute-start(bf16[2,1024]{1,0:T(2,128)(2,1)S(1)} %fusion.45), channel_id=1, source_target_pairs={{0,8},{4,12},{8,0},{12,4},{1,9},{5,13},{9,1},{13,5},{2,10},{6,14},... | collective-permute-start | bytes 12296 | tf_op jit(solution)/shard_map/ppermute | solution.py:615
  389.5 135.4 %collective-permute-start.15 = (bf16[2,1024]{1,0:T(2,128)(2,1)S(1)}, bf16[2,1024]{1,0:T(2,128)(2,1)S(1)}, u32[]{:S(2)}, u32[]{:S(2)}) collective-permute-start(bf16[2,1024]{1,0:T(2,128)(2,1)S(1)} %fusion.45), channel_id=1, source_target_pairs={{0,12},{4,0},{8,4},{12,8},{1,13},{5,1},{9,5},{13,9},{2,14},{6,2},{... | collective-permute-start | bytes 12296 | tf_op jit(solution)/shard_map/ppermute | solution.py:615
  525.0 666.5 %collective-permute-start.18 = (bf16[2,512,8,128]{3,2,1,0:T(8,128)(2,1)}, bf16[2,512,8,128]{3,2,1,0:T(8,128)(2,1)}, u32[]{:S(2)}, u32[]{:S(2)}) collective-permute-start(bf16[2,512,8,128]{3,2,1,0:T(8,128)(2,1)} %pad_maximum_fusion.3), channel_id=1, source_target_pairs={{0,9},{1,10},{2,11},{3,8},{4,13},{5,14},{6,15},{7,12},{8,1},{9,2},... | collective-permute-start | bytes 6291464 | tf_op jit(solution)/shard_map/ppermute | solution.py:742
  528.1 663.4 %collective-permute-start.16 = (bf16[2,512,8,128]{3,2,1,0:T(8,128)(2,1)}, bf16[2,512,8,128]{3,2,1,0:T(8,128)(2,1)}, u32[]{:S(2)}, u32[]{:S(2)}) collective-permute-start(bf16[2,512,8,128]{3,2,1,0:T(8,128)(2,1)} %pad_maximum_fusion.2), channel_id=1, source_target_pairs={{0,1},{1,2},{2,3},{3,0},{4,5},{5,6},{6,7},{7,4},{8,9},{9,10},{10,1... | collective-permute-start | bytes 6291464 | tf_op jit(solution)/shard_map/ppermute | solution.py:742
Sparse Core Ops, SparseCore 0:
  10.1 83.4 all-gather.8
  95.2 80.1 all-gather.10
  177.5 150.2 all-gather.12
  365.2 145.4 all-gather.14

commit v3 on v2

--- a/solution.py
+++ b/solution.py
@@ -12,7 +12,7 @@
 NORM_EPS = 1e-5
 
 ORDER = (
-    'Q0', 'T0', 'G0', 'T1', 'w2', 'Q1', 'T2', 'G12', 'T3', 'G3', 'K', 'k1', 'k3', 'D1', 'D2', 'w3', 'O012', 'k0', 'k2',
+    'Q0', 'T0', 'G0', 'T1', 'w2', 'Q1', 'T2', 'G12', 'T3', 'G3', 'K', 'k1', 'k3', 'D1', 'w3', 'O012', 'D2', 'k0', 'k2',
     'O3', 'B', 'P',
 )
 
@@ -592,7 +592,7 @@
             out_specs=[out, out],
         ),
         compiler_params=pltpu.CompilerParams(dimension_semantics=("arbitrary", "arbitrary"), vmem_limit_bytes=16 << 20),
-        cost_estimate=pl.CostEstimate(flops=20 * rows * size * heads * head_dim, bytes_accessed=8 * size * rows * heads * head_dim, transcendentals=0),
+        cost_estimate=pl.CostEstimate(flops=4000 * rows * size * heads * head_dim, bytes_accessed=8 * size * rows * heads * head_dim, transcendentals=0),
         name="place_caches",
     )(where, *landed)
 
@@ -688,7 +688,8 @@
                 key_now = jnp.where(write_mask, dec_full[1][:, None], k_cache[0])
                 value_now = jnp.where(write_mask, dec_full[2][:, None], v_cache[0])
                 val['key_now'], val['value_now'] = key_now, value_now
-                scores = jnp.sum(dec_full[0][:, None].astype(jnp.float32) * key_now.astype(jnp.float32), axis=-1) * head_dim ** -0.5
+                scores = jnp.sum(dec_full[0][:, None].astype(jnp.float32) * key_now.astype(jnp.float32), axis=-1)
+                scores = scores * head_dim ** -0.5
                 scores = jnp.where(allowed, scores, -1e30)
                 peak = jnp.max(scores, axis=1, keepdims=True)
                 weights = jnp.exp(scores - peak)
@@ -737,7 +738,7 @@
         def transfer(name):
             if name[0] == 'k':
                 d = int(name[1])
-                tie(thread + [('kv', d)])
+                tie(thread + [('kv', d)] + ([('gathered', '3')] if d in (0, 2) else []))
                 route = [(t * side_size + s, ((t + d) % tp_size) * side_size + (s + 1) % side_size) for t in range(tp_size) for s in range(side_size)]
                 val['landed', d] = lax.ppermute(val['kv', d], ('tp', 'side'), route)
                 return

time: 1220 us -> 1260 us (1.033)
  Pallas kernels: 896 us -> 986 us
  waiting for transfers between devices: 190 us -> 145 us
    pallas_call x1, Pallas kernels: 630 us -> 718 us  [mlp(): pl.pallas_call(functools.partial(mlp_kernel, size, chunk_rows, ff_steps,...]
    ppermute x9, waiting for transfers between devices: 64.6 us -> 2.16 us  [cyclic(): lax.ppermute(value, 'tp', [(t, (t + d) % tp_size) for t in range(tp_size)])]
    ppermute x7, waiting for transfers between devices: 125 us -> 143 us  [swap(): lax.ppermute(value, group_axes, [(q, q ^ mask) for q in range(seats)])]
    unnamed x63 -> x73, local copies, waits for them, and re-layouts: 57 us -> 51.2 us
  transfers between devices with their start and end apart: 24 -> 24, of which waited for: 10 -> 8; matrix products, arithmetic and copies ran while one was open for 6% -> 6% of each run, Pallas kernels for 72% -> 77%
where the time goes in v3:
time: 1260 us
  Pallas kernels  986 us (78%)
  waiting for transfers between devices  145 us (12%)
  local copies, waits for them, and re-layouts  56.6 us (4%)
  other arithmetic  37.9 us (3%)
  starting transfers between devices  22.7 us (2%)
  between operations  14.9 us (1%)
    pallas_call x1, Pallas kernels, mlp(): pl.pallas_call(functools.partial(mlp_kernel, size, chunk_rows, ff_steps,...  718 us
    ppermute x7, waiting for transfers between devices, swap(): lax.ppermute(value, group_axes, [(q, q ^ mask) for q in range(seats)])  143 us
    pallas_call x2, Pallas kernels, project_out(): pl.pallas_call(functools.partial(output_kernel, size, heads, len(contexts...  113 us
    pallas_call x2, Pallas kernels, project_qkv(): pl.pallas_call(functools.partial(qkv_kernel, half, head_dim, extra), out_...  81.9 us
    pallas_call x4, Pallas kernels, attend(): pl.pallas_call(functools.partial(attend_kernel, chunk, chunks // 2, min(2...  61.4 us
    unnamed x73, local copies, waits for them, and re-layouts  51.2 us
  transfers between devices with their start and end apart: 24, of which 8 were waited for; matrix products, arithmetic and copies ran while one was open for 6% of the time, Pallas kernels for 77%

profile of v3, /device:TPU:0, one launch (start us, length us, event | category | flops | bytes accessed | tf_op | source)
XLA Modules:
  0.0 1262.6 jit_solution(10776130753822677362)
XLA Ops:
  7.2 2.3 constant_dynamic-slice_fusion
  9.6 23.4 %copy.88 = bf16[512,8,24,128]{3,1,2,0:T(8,128)(2,1)} copy(bf16[512,8,24,128]{3,2,1,0:T(8,128)(2,1)} %bitcast.339) | data formatting | bytes 50331648
  36.3 41.6 %project_qkv.2 = (bf16[1024,1024]{1,0:T(8,128)(2,1)}, bf16[1024,1024]{1,0:T(8,128)(2,1)}, bf16[1024,1024]{1,0:T(8,128)(2,1)}, f32[8,128]{1,0:T(8,128)}, bf16[16,...) custom-call(bf16[2048,4096]{1,0:T(8,128)(2,1)} %bitcast.349, bf16[1,4096]{1,0:T(2,128)(2,1)} %refs_1_.1, ...), custom_call_target="tpu_custom_call" | custom-call | flops 25769803776 | bytes 39845888 | tf_op jit(solution)/shard_map/project_qkv/pallas_call | solution.py:101
  77.9 1.6 copy-done
  79.5 1.6 copy-done.2
  81.8 9.9 shard_map.163
  91.7 1.6 copy-done.3
  93.3 13.3 %shard_map.164 = (bf16[512,1024]{1,0:T(8,128)(2,1)S(1)}, f32[8,128]{1,0:T(8,128)S(1)}) custom-call(s32[1]{0:T(128)} %copy.94.slen_ref, bf16[1024,1024]{1,0:T(8,128)(2,1)S(1)} %copy-done.3, bf16[1024,1024]{1,0:T(8,128)(2,1)S(1)} %copy-done.1, bf16[1024,1024]{1,0:T(8,128)(2,1)S(1)} %copy-done.1, ...), custom_call_target="tpu_custom_call" | custom-call | flops 4294967296 | bytes 6291456 | tf_op jit(solution)/shard_map/pallas_call | solution.py:164
  107.2 40.3 %project_qkv.3 = (bf16[1024,1024]{1,0:T(8,128)(2,1)}, bf16[1024,1024]{1,0:T(8,128)(2,1)}, bf16[1024,1024]{1,0:T(8,128)(2,1)}, f32[8,128]{1,0:T(8,128)}) custom-call(bf16[2048,4096]{1,0:T(8,128)(2,1)} %bitcast.350, bf16[1,4096]{1,0:T(2,128)(2,1)} %refs_1_.1, bf16[4096,3072]{1,0:T(8,128)(2,1)} %bitcast.343, bf16[4096,3072]{1,0:T(8,128)(2,1)} %bitcast.344, ...), custom_call_target="tpu_custom_call" | custom-call | flops 25769803776 | bytes 39845888 | tf_op jit(solution)/shard_map/project_qkv/pallas_call | solution.py:101
  147.5 1.6 copy-done.4
  149.8 17.0 %shard_map.165 = (bf16[512,1024]{1,0:T(8,128)(2,1)S(1)}, f32[8,128]{1,0:T(8,128)S(1)}) custom-call(s32[1]{0:T(128)} %copy.94.slen_ref, bf16[1024,1024]{1,0:T(8,128)(2,1)S(1)} %copy-done.4, bf16[1024,1024]{1,0:T(8,128)(2,1)S(1)} %copy-done.1, bf16[1024,1024]{1,0:T(8,128)(2,1)S(1)} %copy-done.1, bf16[1024,1024]{1,0:T(8,128)(2,1)} %get-tuple-element.125.refs_3_.refs_4_, ...), custom_call_target="tpu_custom_call" | custom-call | flops 6442450944 | bytes 8388608 | tf_op jit(solution)/shard_map/pallas_call | solution.py:164
  166.7 1.5 pad_maximum_fusion.4
  170.5 3.3 collective-permute-start
  173.8 2.6 collective-permute-start.1
  176.6 1.3 copy.28
  179.4 1.3 copy.32
  182.0 1.5 collective-permute-start.3
  183.5 1.5 collective-permute-start.4
  185.5 1.8 copy-done.5
  187.3 21.3 %shard_map.166 = (bf16[512,1024]{1,0:T(8,128)(2,1)}, f32[8,128]{1,0:T(8,128)S(1)}) custom-call(s32[1]{0:T(128)} %copy.94.slen_ref, bf16[1024,1024]{1,0:T(8,128)(2,1)S(1)} %copy-done.5, bf16[1024,1024]{1,0:T(8,128)(2,1)S(1)} %copy-done.1, bf16[1024,1024]{1,0:T(8,128)(2,1)S(1)} %copy-done.1, bf16[1024,1024]{1,0:T(8,128)(2,1)} %get-tuple-element.125.refs_3_.refs_4_, ...), custom_call_target="tpu_custom_call" | custom-call | flops 8589934592 | bytes 10485760 | tf_op jit(solution)/shard_map/pallas_call | solution.py:164
  208.7 1.4 copy-done.17
  212.5 5.6 fusion.8
  218.1 1.6 pad_maximum_fusion.1
  219.7 1.4 collective-permute-start.2
  221.0 1.5 pad_maximum_fusion
  222.5 2.1 collective-permute-done.2
  224.7 9.0 multiply_reduce_fusion.1
  234.9 6.6 multiply_reduce_fusion
  241.8 1.5 pad_maximum_fusion.3
  243.3 1.5 pad_maximum_fusion.2
  244.8 30.0 %collective-permute-done.3.refs_4_.refs_3_ = bf16[4,128,4096]{2,1,0:T(8,128)(2,1)} collective-permute-done((bf16[4,128,4096]{2,1,0:T(8,128)(2,1)}, bf16[4,128,4096]{2,1,0:T(8,128)(2,1)}, u32[]{:S(2)}, u32[]{:S(2)}) %collective-permute-start.3) | collective-permute-done | bytes 4194336 | tf_op jit(solution)/shard_map/ppermute | solution.py:618
  274.8 2.4 collective-permute-done.4.refs_6_.refs_5_
  277.3 87.8 %collective-permute-done.5.refs_8_.refs_7_ = bf16[4,128,4096]{2,1,0:T(8,128)(2,1)} collective-permute-done((bf16[4,128,4096]{2,1,0:T(8,128)(2,1)}, bf16[4,128,4096]{2,1,0:T(8,128)(2,1)}, u32[]{:S(2)}, u32[]{:S(2)}) %collective-permute-start.5) | collective-permute-done | bytes 4194336 | tf_op jit(solution)/shard_map/ppermute | solution.py:618
  366.5 6.1 collective-permute-done.6.refs_3_.refs_2_
  373.0 5.6 collective-permute-done.7.refs_5_.refs_4_
  378.6 1.3 collective-permute-start.12
  379.9 4.7 collective-permute-done.8.refs_7_.refs_6_
  384.6 6.0 collective-permute-done.9.refs_9_.refs_8_
  390.6 81.4 %project_out.2 = (bf16[8,272,4096]{2,1,0:T(8,128)(2,1)}, bf16[2048,4096]{1,0:T(8,128)(2,1)}, f32[8,128]{1,0:T(8,128)}) custom-call(s32[1]{0:T(128)} %bitcast.where_ref, bf16[4,1,512,1024]{3,2,1,0:T(8,128)(2,1)} %bitcast.366, bf16[4,2,512,1024]{3,2,1,0:T(8,128)(2,1)} %bitcast.365, bf16[4,128,4096]{2,1,0:T(8,128)(2,1)} %bitcast.5.refs_2_.refs_1_, ...), custom_call_target="tpu_custom_call" | custom-call | flops 51539607552 | bytes 150994944 | tf_op jit(solution)/shard_map/project_out/pallas_call | solution.py:272
  472.6 1.5 collective-permute-start.14
  474.1 1.9 collective-permute-start.15
  476.0 5.9 broadcast_select_fusion
  481.9 2.7 collective-permute-start.17
  487.4 31.4 %project_out.3 = (bf16[8,272,4096]{2,1,0:T(8,128)(2,1)}, bf16[2048,4096]{1,0:T(8,128)(2,1)}, bf16[16,4096]{1,0:T(8,128)(2,1)}, f32[8,128]{1,0:T(8,128)}) custom-call(s32[1]{0:T(128)} %bitcast.where_ref, bf16[4,1,512,1024]{3,2,1,0:T(8,128)(2,1)} %bitcast.353, ...), custom_call_target="tpu_custom_call", output_to_operand_aliasing={{0}: (15, {}), {1}: (16, {})} | custom-call | flops 17716740096 | bytes 50724864 | tf_op jit(solution)/shard_map/project_out/pallas_call | solution.py:272
  518.8 717.5 %mlp.1 = (bf16[2048,4096]{1,0:T(8,128)(2,1)}, bf16[8,4096]{1,0:T(8,128)(2,1)}) custom-call(f32[8,128]{1,0:T(8,128)} %get-tuple-element.191.token_ref, bf16[8,272,4096]{2,1,0:T(8,128)(2,1)} %get-tuple-element.192.normed_ref, bf16[16,4096]{1,0:T(8,128)(2,1)} %get-tuple-element.193.hextra_ref, bf16[2,2752,4096]{2,1,0:T(8,128)(2,1)} %bitcast.363, ...), custom_call_target="tpu_custom_call" | custom-call | flops 138512695296 | bytes 541065216 | tf_op jit(solution)/shard_map/mlp/pallas_call | solution.py:529
  1236.4 1.5 slice.163
  1237.9 12.0 place_caches.1
  1249.9 6.2 copy.95
  (124 shorter events, 19.4 us)
Async XLA Ops:
  7.2 100.0 %all-gather.9.cloned.1.call-start = ((), (), s32[]{:S(2)}) async-start(), calls=%async_computation | async-start | bytes 5242880 | tf_op jit(solution)/shard_map/all_gather | solution.py:642
  9.5 370.4 %all-gather.11.cloned.1.call-start = ((), (), s32[]{:S(2)}) async-start(), calls=%async_computation.1 | async-start | bytes 5242880 | tf_op jit(solution)/shard_map/all_gather | solution.py:670
  9.6 24.1 %copy-start.19 = (bf16[2,4096]{1,0:T(2,128)(2,1)S(1)}, bf16[2,4096]{1,0:T(2,128)(2,1)}, u32[]{:S(2)}) copy-start(bf16[2,4096]{1,0:T(2,128)(2,1)} %param.14) | copy-start | bytes 49156
  9.6 24.8 %copy-start.20 = (s32[2]{0:T(128)S(1)}, s32[2]{0:T(128)}, u32[]{:S(2)}) copy-start(s32[2]{0:T(128)} %param.15) | copy-start | bytes 28
  77.9 1.6 copy-start
  79.5 1.6 copy-start.2
  81.1 0.7 copy-start.6
  81.8 9.9 copy-start.1
  91.7 298.9 %all-gather.13.cloned.1.call-start = ((), (), s32[]{:S(2)}) async-start(), calls=%async_computation.2 | async-start | bytes 10485760 | tf_op jit(solution)/shard_map/all_gather | solution.py:670
  91.7 1.6 copy-start.3
  147.5 1.6 copy-start.4
  149.1 0.7 copy-start.8
  168.3 316.4 %all-gather.15.cloned.1.call-start = ((), (), s32[]{:S(2)}) async-start(), calls=%async_computation.3 | async-start | bytes 5242880 | tf_op jit(solution)/shard_map/all_gather | solution.py:670
  170.5 49.2 %collective-permute-start = (bf16[3,2,8,128]{3,2,1,0:T(8,128)(2,1)S(1)}, bf16[3,2,8,128]{3,2,1,0:T(8,128)(2,1)S(1)}, u32[]{:S(2)}, u32[]{:S(2)}) collective-permute-start(bf16[3,2,8,128]{3,2,1,0:T(8,128)(2,1)S(1)} %constant_dynamic-update-slice_fusion), channel_id=1, source_target_pairs={{0,4},{4,8},{8,12},{12,0},{1,5},{5,9},{9,13},{13,1},{2,6},{6,10},{... | collective-permute-start | bytes 36872 | tf_op jit(solution)/shard_map/ppermute | solution.py:615
  173.8 48.7 %collective-permute-start.1 = (bf16[3,2,8,128]{3,2,1,0:T(8,128)(2,1)S(1)}, bf16[3,2,8,128]{3,2,1,0:T(8,128)(2,1)S(1)}, u32[]{:S(2)}, u32[]{:S(2)}) collective-permute-start(bf16[3,2,8,128]{3,2,1,0:T(8,128)(2,1)S(1)} %constant_dynamic-update-slice_fusion), channel_id=1, source_target_pairs={{0,8},{4,12},{8,0},{12,4},{1,9},{5,13},{9,1},{13,5},{2,10},{6,14},... | collective-permute-start | bytes 36872 | tf_op jit(solution)/shard_map/ppermute | solution.py:615
  176.4 2.8 copy-start.16
  182.0 92.9 %collective-permute-start.3 = (bf16[4,128,4096]{2,1,0:T(8,128)(2,1)}, bf16[4,128,4096]{2,1,0:T(8,128)(2,1)}, u32[]{:S(2)}, u32[]{:S(2)}) collective-permute-start(bf16[4,128,4096]{2,1,0:T(8,128)(2,1)} %bitcast.5.refs_2_.refs_1_), channel_id=1, source_target_pairs={{0,2},{1,3},{2,0},{3,1},{16,18},{17,19},{18,16},{19,17},{4,6},{5,7... | collective-permute-start | bytes 12582920 | tf_op jit(solution)/shard_map/ppermute | solution.py:618
  183.5 93.8 %collective-permute-start.4 = (bf16[4,128,4096]{2,1,0:T(8,128)(2,1)}, bf16[4,128,4096]{2,1,0:T(8,128)(2,1)}, u32[]{:S(2)}, u32[]{:S(2)}) collective-permute-start(bf16[4,128,4096]{2,1,0:T(8,128)(2,1)} %bitcast.5.refs_2_.refs_1_), channel_id=1, source_target_pairs={{0,16},{1,17},{2,18},{3,19},{16,0},{17,1},{18,2},{19,3},{4,20},{5,... | collective-permute-start | bytes 12582920 | tf_op jit(solution)/shard_map/ppermute | solution.py:618
  185.0 180.1 %collective-permute-start.5 = (bf16[4,128,4096]{2,1,0:T(8,128)(2,1)}, bf16[4,128,4096]{2,1,0:T(8,128)(2,1)}, u32[]{:S(2)}, u32[]{:S(2)}) collective-permute-start(bf16[4,128,4096]{2,1,0:T(8,128)(2,1)} %bitcast.5.refs_2_.refs_1_), channel_id=1, source_target_pairs={{0,18},{1,19},{2,16},{3,17},{16,2},{17,3},{18,0},{19,1},{4,22},{5,... | collective-permute-start | bytes 12582920 | tf_op jit(solution)/shard_map/ppermute | solution.py:618
  185.5 1.8 copy-start.5
  187.3 21.3 %copy-start.18 = (bf16[1024,1024]{1,0:T(8,128)(2,1)S(1)}, bf16[1024,1024]{1,0:T(8,128)(2,1)}, u32[]{:S(2)}) copy-start(bf16[1024,1024]{1,0:T(8,128)(2,1)} %get-tuple-element.125.refs_3_.refs_4_) | copy-start | bytes 6291460
  208.5 1.8 copy-start.9
  208.5 1.6 copy-start.17
  210.3 1.2 copy-start.11
  210.3 1.5 copy-start.12
  210.4 1.8 copy-start.13
  210.4 2.1 copy-start.14
  218.1 6.6 copy-start.10
  219.7 5.0 collective-permute-start.2
  234.9 6.8 copy-start.15
  365.1 7.5 collective-permute-start.6
  365.1 13.5 %collective-permute-start.7 = (bf16[4,128,4096]{2,1,0:T(8,128)(2,1)}, bf16[4,128,4096]{2,1,0:T(8,128)(2,1)}, u32[]{:S(2)}, u32[]{:S(2)}) collective-permute-start(bf16[4,128,4096]{2,1,0:T(8,128)(2,1)} %collective-permute-done.3.refs_4_.refs_3_), channel_id=1, source_target_pairs={{0,1},{1,0},{2,3},{3,2},{16,17},{17,16},{18,19},{19,18},{4,5},{5,4... | collective-permute-start | bytes 12582920 | tf_op jit(solution)/shard_map/ppermute | solution.py:618
  365.6 19.0 %collective-permute-start.8 = (bf16[4,128,4096]{2,1,0:T(8,128)(2,1)}, bf16[4,128,4096]{2,1,0:T(8,128)(2,1)}, u32[]{:S(2)}, u32[]{:S(2)}) collective-permute-start(bf16[4,128,4096]{2,1,0:T(8,128)(2,1)} %collective-permute-done.4.refs_6_.refs_5_), channel_id=1, source_target_pairs={{0,1},{1,0},{2,3},{3,2},{16,17},{17,16},{18,19},{19,18},{4,5},{5,4... | collective-permute-start | bytes 12582920 | tf_op jit(solution)/shard_map/ppermute | solution.py:618
  365.6 25.0 %collective-permute-start.9 = (bf16[4,128,4096]{2,1,0:T(8,128)(2,1)}, bf16[4,128,4096]{2,1,0:T(8,128)(2,1)}, u32[]{:S(2)}, u32[]{:S(2)}) collective-permute-start(bf16[4,128,4096]{2,1,0:T(8,128)(2,1)} %collective-permute-done.5.refs_8_.refs_7_), channel_id=1, source_target_pairs={{0,1},{1,0},{2,3},{3,2},{16,17},{17,16},{18,19},{19,18},{4,5},{5,4... | collective-permute-start | bytes 12582920 | tf_op jit(solution)/shard_map/ppermute | solution.py:618
  366.1 105.9 %collective-permute-start.10 = (f32[3,2,8,128]{3,2,1,0:T(8,128)S(1)}, f32[3,2,8,128]{3,2,1,0:T(8,128)S(1)}, u32[]{:S(2)}, u32[]{:S(2)}) collective-permute-start(f32[3,2,8,128]{3,2,1,0:T(8,128)S(1)} %get-tuple-element.228), channel_id=1, source_target_pairs={{0,4},{4,8},{8,12},{12,0},{1,5},{5,9},{9,13},{13,1},{2,6},{6,10},{... | collective-permute-start | bytes 73736 | tf_op jit(solution)/shard_map/ppermute | solution.py:615
  372.6 99.4 %collective-permute-start.11 = (f32[3,2,8,128]{3,2,1,0:T(8,128)S(1)}, f32[3,2,8,128]{3,2,1,0:T(8,128)S(1)}, u32[]{:S(2)}, u32[]{:S(2)}) collective-permute-start(f32[3,2,8,128]{3,2,1,0:T(8,128)S(1)} %get-tuple-element.227), channel_id=1, source_target_pairs={{0,8},{4,12},{8,0},{12,4},{1,9},{5,13},{9,1},{13,5},{2,10},{6,14},... | collective-permute-start | bytes 73736 | tf_op jit(solution)/shard_map/ppermute | solution.py:615
  378.6 93.4 %collective-permute-start.12 = (f32[3,2,8,128]{3,2,1,0:T(8,128)S(1)}, f32[3,2,8,128]{3,2,1,0:T(8,128)S(1)}, u32[]{:S(2)}, u32[]{:S(2)}) collective-permute-start(f32[3,2,8,128]{3,2,1,0:T(8,128)S(1)} %get-tuple-element.226), channel_id=1, source_target_pairs={{0,12},{4,0},{8,4},{12,8},{1,13},{5,1},{9,5},{13,9},{2,14},{6,2},{... | collective-permute-start | bytes 73736 | tf_op jit(solution)/shard_map/ppermute | solution.py:615
  472.1 12.5 collective-permute-start.13
  472.6 13.0 %collective-permute-start.14 = (bf16[2,1024]{1,0:T(2,128)(2,1)S(1)}, bf16[2,1024]{1,0:T(2,128)(2,1)S(1)}, u32[]{:S(2)}, u32[]{:S(2)}) collective-permute-start(bf16[2,1024]{1,0:T(2,128)(2,1)S(1)} %fusion.45), channel_id=1, source_target_pairs={{0,8},{4,12},{8,0},{12,4},{1,9},{5,13},{9,1},{13,5},{2,10},{6,14},... | collective-permute-start | bytes 12296 | tf_op jit(solution)/shard_map/ppermute | solution.py:615
  474.1 12.6 %collective-permute-start.15 = (bf16[2,1024]{1,0:T(2,128)(2,1)S(1)}, bf16[2,1024]{1,0:T(2,128)(2,1)S(1)}, u32[]{:S(2)}, u32[]{:S(2)}) collective-permute-start(bf16[2,1024]{1,0:T(2,128)(2,1)S(1)} %fusion.45), channel_id=1, source_target_pairs={{0,12},{4,0},{8,4},{12,8},{1,13},{5,1},{9,5},{13,9},{2,14},{6,2},{... | collective-permute-start | bytes 12296 | tf_op jit(solution)/shard_map/ppermute | solution.py:615
  481.9 754.4 %collective-permute-start.19 = (bf16[2,512,8,128]{3,2,1,0:T(8,128)(2,1)}, bf16[2,512,8,128]{3,2,1,0:T(8,128)(2,1)}, u32[]{:S(2)}, u32[]{:S(2)}) collective-permute-start(bf16[2,512,8,128]{3,2,1,0:T(8,128)(2,1)} %pad_maximum_fusion.1), channel_id=1, source_target_pairs={{0,13},{1,14},{2,15},{3,12},{4,1},{5,2},{6,3},{7,0},{8,5},{9,6},{1... | collective-permute-start | bytes 6291464 | tf_op jit(solution)/shard_map/ppermute | solution.py:743
  481.9 754.5 %collective-permute-start.17 = (bf16[2,512,8,128]{3,2,1,0:T(8,128)(2,1)}, bf16[2,512,8,128]{3,2,1,0:T(8,128)(2,1)}, u32[]{:S(2)}, u32[]{:S(2)}) collective-permute-start(bf16[2,512,8,128]{3,2,1,0:T(8,128)(2,1)} %pad_maximum_fusion), channel_id=1, source_target_pairs={{0,5},{1,6},{2,7},{3,4},{4,9},{5,10},{6,11},{7,8},{8,13},{9,14},{1... | collective-permute-start | bytes 6291464 | tf_op jit(solution)/shard_map/ppermute | solution.py:743
  484.6 751.8 %collective-permute-start.18 = (bf16[2,512,8,128]{3,2,1,0:T(8,128)(2,1)}, bf16[2,512,8,128]{3,2,1,0:T(8,128)(2,1)}, u32[]{:S(2)}, u32[]{:S(2)}) collective-permute-start(bf16[2,512,8,128]{3,2,1,0:T(8,128)(2,1)} %pad_maximum_fusion.3), channel_id=1, source_target_pairs={{0,9},{1,10},{2,11},{3,8},{4,13},{5,14},{6,15},{7,12},{8,1},{9,2},... | collective-permute-start | bytes 6291464 | tf_op jit(solution)/shard_map/ppermute | solution.py:743
  485.6 750.8 %collective-permute-start.16 = (bf16[2,512,8,128]{3,2,1,0:T(8,128)(2,1)}, bf16[2,512,8,128]{3,2,1,0:T(8,128)(2,1)}, u32[]{:S(2)}, u32[]{:S(2)}) collective-permute-start(bf16[2,512,8,128]{3,2,1,0:T(8,128)(2,1)} %pad_maximum_fusion.2), channel_id=1, source_target_pairs={{0,1},{1,2},{2,3},{3,0},{4,5},{5,6},{6,7},{7,4},{8,9},{9,10},{10,1... | collective-permute-start | bytes 6291464 | tf_op jit(solution)/shard_map/ppermute | solution.py:743
  1237.9 12.0 slice-start
  1237.9 12.0 slice-start.1
  1237.9 12.0 slice-start.2
  1237.9 12.0 slice-start.3
  (1 other events, 0.6 us)
Sparse Core Ops, SparseCore 0:
  10.1 83.4 all-gather.8
  95.2 80.1 all-gather.10
  177.5 148.3 all-gather.12
  366.6 82.3 all-gather.14

commit v4 on v2

--- a/solution.py
+++ b/solution.py
@@ -12,7 +12,7 @@
 NORM_EPS = 1e-5
 
 ORDER = (
-    'Q0', 'T0', 'G0', 'T1', 'w2', 'Q1', 'T2', 'G12', 'T3', 'G3', 'K', 'k1', 'k3', 'D1', 'D2', 'w3', 'O012', 'k0', 'k2',
+    'Q0', 'T0', 'G0', 'T1', 'w2', 'Q1', 'T2', 'G12', 'T3', 'G3', 'K', 'k1', 'k3', 'k0', 'D1', 'D2', 'w3', 'O012', 'k2',
     'O3', 'B', 'P',
 )
 
@@ -592,7 +592,7 @@
             out_specs=[out, out],
         ),
         compiler_params=pltpu.CompilerParams(dimension_semantics=("arbitrary", "arbitrary"), vmem_limit_bytes=16 << 20),
-        cost_estimate=pl.CostEstimate(flops=20 * rows * size * heads * head_dim, bytes_accessed=8 * size * rows * heads * head_dim, transcendentals=0),
+        cost_estimate=pl.CostEstimate(flops=4000 * rows * size * heads * head_dim, bytes_accessed=8 * size * rows * heads * head_dim, transcendentals=0),
         name="place_caches",
     )(where, *landed)
 
@@ -737,12 +737,12 @@
         def transfer(name):
             if name[0] == 'k':
                 d = int(name[1])
-                tie(thread + [('kv', d)])
+                tie(thread + [('kv', d)] + ([('gathered', '3')] if d == 2 else []))
                 route = [(t * side_size + s, ((t + d) % tp_size) * side_size + (s + 1) % side_size) for t in range(tp_size) for s in range(side_size)]
                 val['landed', d] = lax.ppermute(val['kv', d], ('tp', 'side'), route)
                 return
             bases = [0] if name == 'w2' else list(range(0, seats, 2))
-            kept = [] if name == 'w2' else [('kv', 0), ('kv', 2)]
+            kept = [] if name == 'w2' else [('kv', 2)]
             tie(thread + kept + [('w', base) for base in bases])
             for mask in (range(2, seats, 2) if name == 'w2' else [1]):
                 for base in bases:

time: 1220 us -> 1220 us (level)
  Pallas kernels: 896 us -> 941 us
  waiting for transfers between devices: 190 us -> 153 us
    ppermute x9, waiting for transfers between devices: 64.6 us -> 11.4 us  [cyclic(): lax.ppermute(value, 'tp', [(t, (t + d) % tp_size) for t in range(tp_size)])]
    pallas_call x1, Pallas kernels: 630 us -> 673 us  [mlp(): pl.pallas_call(functools.partial(mlp_kernel, size, chunk_rows, ff_steps,...]
    all_gather x3, waiting for transfers between devices: 0.02 us -> 13.7 us  [compute(): lax.all_gather(jnp.stack([val['context', int(digit)] for digit in name[1:...]
    unnamed x63 -> x67, local copies, waits for them, and re-layouts: 57 us -> 49.1 us
  transfers between devices with their start and end apart: 24 -> 24, of which waited for: 10 -> 11; matrix products, arithmetic and copies ran while one was open for 6% -> 6% of each run, Pallas kernels for 72% -> 76%
where the time goes in v4:
time: 1220 us
  Pallas kernels  941 us (77%)
  waiting for transfers between devices  153 us (13%)
  local copies, waits for them, and re-layouts  54.4 us (4%)
  other arithmetic  36 us (3%)
  starting transfers between devices  24.1 us (2%)
  between operations  14.8 us (1%)
    pallas_call x1, Pallas kernels, mlp(): pl.pallas_call(functools.partial(mlp_kernel, size, chunk_rows, ff_steps,...  673 us
    ppermute x7, waiting for transfers between devices, swap(): lax.ppermute(value, group_axes, [(q, q ^ mask) for q in range(seats)])  128 us
    pallas_call x2, Pallas kernels, project_out(): pl.pallas_call(functools.partial(output_kernel, size, heads, len(contexts...  113 us
    pallas_call x2, Pallas kernels, project_qkv(): pl.pallas_call(functools.partial(qkv_kernel, half, head_dim, extra), out_...  81.8 us
    pallas_call x4, Pallas kernels, attend(): pl.pallas_call(functools.partial(attend_kernel, chunk, chunks // 2, min(2...  61.3 us
    unnamed x67, local copies, waits for them, and re-layouts  49.1 us
  transfers between devices with their start and end apart: 24, of which 11 were waited for; matrix products, arithmetic and copies ran while one was open for 6% of the time, Pallas kernels for 76%

profile of v4, /device:TPU:0, one launch (start us, length us, event | category | flops | bytes accessed | tf_op | source)
XLA Modules:
  0.0 1223.2 jit_solution(7223176669268931020)
XLA Ops:
  7.2 2.3 constant_dynamic-slice_fusion
  9.6 23.4 %copy.88 = bf16[512,8,24,128]{3,1,2,0:T(8,128)(2,1)} copy(bf16[512,8,24,128]{3,2,1,0:T(8,128)(2,1)} %bitcast.339) | data formatting | bytes 50331648
  36.2 41.5 %project_qkv.2 = (bf16[1024,1024]{1,0:T(8,128)(2,1)}, bf16[1024,1024]{1,0:T(8,128)(2,1)}, bf16[1024,1024]{1,0:T(8,128)(2,1)}, f32[8,128]{1,0:T(8,128)}, bf16[16,...) custom-call(bf16[2048,4096]{1,0:T(8,128)(2,1)} %bitcast.349, bf16[1,4096]{1,0:T(2,128)(2,1)} %refs_1_.1, ...), custom_call_target="tpu_custom_call" | custom-call | flops 25769803776 | bytes 39845888 | tf_op jit(solution)/shard_map/project_qkv/pallas_call | solution.py:101
  77.8 1.6 copy-done
  79.4 1.6 copy-done.2
  81.7 9.8 shard_map.163
  91.6 1.6 copy-done.3
  93.2 13.3 %shard_map.164 = (bf16[512,1024]{1,0:T(8,128)(2,1)S(1)}, f32[8,128]{1,0:T(8,128)S(1)}) custom-call(s32[1]{0:T(128)} %copy.94.slen_ref, bf16[1024,1024]{1,0:T(8,128)(2,1)S(1)} %copy-done.3, bf16[1024,1024]{1,0:T(8,128)(2,1)S(1)} %copy-done.1, bf16[1024,1024]{1,0:T(8,128)(2,1)S(1)} %copy-done.1, ...), custom_call_target="tpu_custom_call" | custom-call | flops 4294967296 | bytes 6291456 | tf_op jit(solution)/shard_map/pallas_call | solution.py:164
  107.0 40.3 %project_qkv.3 = (bf16[1024,1024]{1,0:T(8,128)(2,1)}, bf16[1024,1024]{1,0:T(8,128)(2,1)}, bf16[1024,1024]{1,0:T(8,128)(2,1)}, f32[8,128]{1,0:T(8,128)}) custom-call(bf16[2048,4096]{1,0:T(8,128)(2,1)} %bitcast.350, bf16[1,4096]{1,0:T(2,128)(2,1)} %refs_1_.1, bf16[4096,3072]{1,0:T(8,128)(2,1)} %bitcast.343, bf16[4096,3072]{1,0:T(8,128)(2,1)} %bitcast.344, ...), custom_call_target="tpu_custom_call" | custom-call | flops 25769803776 | bytes 39845888 | tf_op jit(solution)/shard_map/project_qkv/pallas_call | solution.py:101
  147.3 1.6 copy-done.4
  149.6 17.0 %shard_map.165 = (bf16[512,1024]{1,0:T(8,128)(2,1)S(1)}, f32[8,128]{1,0:T(8,128)S(1)}) custom-call(s32[1]{0:T(128)} %copy.94.slen_ref, bf16[1024,1024]{1,0:T(8,128)(2,1)S(1)} %copy-done.4, bf16[1024,1024]{1,0:T(8,128)(2,1)S(1)} %copy-done.1, bf16[1024,1024]{1,0:T(8,128)(2,1)S(1)} %copy-done.1, bf16[1024,1024]{1,0:T(8,128)(2,1)} %get-tuple-element.121.refs_3_.refs_4_, ...), custom_call_target="tpu_custom_call" | custom-call | flops 6442450944 | bytes 8388608 | tf_op jit(solution)/shard_map/pallas_call | solution.py:164
  166.6 1.5 pad_maximum_fusion.4
  170.4 3.3 collective-permute-start
  173.7 2.5 collective-permute-start.1
  176.7 1.3 copy.25
  180.8 1.5 collective-permute-start.6
  182.3 1.5 collective-permute-start.7
  184.3 2.2 slice_bitcast_fusion.6
  188.9 21.2 %shard_map.166 = (bf16[512,1024]{1,0:T(8,128)(2,1)}, f32[8,128]{1,0:T(8,128)S(1)}) custom-call(s32[1]{0:T(128)} %copy.94.slen_ref, bf16[1024,1024]{1,0:T(8,128)(2,1)S(1)} %copy-done.5, bf16[1024,1024]{1,0:T(8,128)(2,1)S(1)} %copy-done.1, bf16[1024,1024]{1,0:T(8,128)(2,1)S(1)} %copy-done.1, bf16[1024,1024]{1,0:T(8,128)(2,1)} %get-tuple-element.121.refs_3_.refs_4_, ...), custom_call_target="tpu_custom_call" | custom-call | flops 8589934592 | bytes 10485760 | tf_op jit(solution)/shard_map/pallas_call | solution.py:164
  210.1 4.4 fusion.8
  214.5 1.5 pad_maximum_fusion.2
  216.0 1.6 pad_maximum_fusion.1
  217.6 1.4 collective-permute-start.2
  219.0 1.5 pad_maximum_fusion
  220.5 4.0 collective-permute-done.2
  224.6 9.0 multiply_reduce_fusion.1
  234.1 6.5 multiply_reduce_fusion
  241.9 5.3 collective-permute-done.3
  248.2 1.5 pad_maximum_fusion.3
  249.7 2.1 collective-permute-done.5
  251.8 21.8 %collective-permute-done.6.refs_4_.refs_3_ = bf16[4,128,4096]{2,1,0:T(8,128)(2,1)} collective-permute-done((bf16[4,128,4096]{2,1,0:T(8,128)(2,1)}, bf16[4,128,4096]{2,1,0:T(8,128)(2,1)}, u32[]{:S(2)}, u32[]{:S(2)}) %collective-permute-start.6) | collective-permute-done | bytes 4194336 | tf_op jit(solution)/shard_map/ppermute | solution.py:618
  273.7 2.4 collective-permute-done.7.refs_6_.refs_5_
  276.1 87.8 %collective-permute-done.8.refs_8_.refs_7_ = bf16[4,128,4096]{2,1,0:T(8,128)(2,1)} collective-permute-done((bf16[4,128,4096]{2,1,0:T(8,128)(2,1)}, bf16[4,128,4096]{2,1,0:T(8,128)(2,1)}, u32[]{:S(2)}, u32[]{:S(2)}) %collective-permute-start.8) | collective-permute-done | bytes 4194336 | tf_op jit(solution)/shard_map/ppermute | solution.py:618
  365.0 5.9 broadcast_select_fusion
  371.4 2.1 collective-permute-start.19
  373.5 3.9 collective-permute-done.11.refs_7_.refs_6_
  377.8 5.6 collective-permute-done.12.refs_9_.refs_8_
  383.8 5.6 collective-permute-done.9.refs_3_.refs_2_
  389.4 1.3 collective-permute-start.15
  390.7 81.4 %project_out.2 = (bf16[8,272,4096]{2,1,0:T(8,128)(2,1)}, bf16[2048,4096]{1,0:T(8,128)(2,1)}, f32[8,128]{1,0:T(8,128)}) custom-call(s32[1]{0:T(128)} %bitcast.where_ref, bf16[4,1,512,1024]{3,2,1,0:T(8,128)(2,1)} %bitcast.366, bf16[4,2,512,1024]{3,2,1,0:T(8,128)(2,1)} %bitcast.365, bf16[4,128,4096]{2,1,0:T(8,128)(2,1)} %bitcast.5.refs_2_.refs_1_, ...), custom_call_target="tpu_custom_call" | custom-call | flops 51539607552 | bytes 150994944 | tf_op jit(solution)/shard_map/project_out/pallas_call | solution.py:272
  472.2 13.7 %all-gather.15.cloned.1.call-done = bf16[2048,1024]{1,0:T(8,128)(2,1)} async-done(((bf16[512,1024]{1,0:T(8,128)(2,1)}), bf16[2048,1024]{1,0:T(8,128)(2,1)}) %all-gather.15.cloned.1.call-update) | async-done | bytes 4194320 | tf_op jit(solution)/shard_map/all_gather | solution.py:670
  485.8 2.2 collective-permute-start.17
  488.0 3.7 collective-permute-start.18
  492.5 31.4 %project_out.3 = (bf16[8,272,4096]{2,1,0:T(8,128)(2,1)}, bf16[2048,4096]{1,0:T(8,128)(2,1)}, bf16[16,4096]{1,0:T(8,128)(2,1)}, f32[8,128]{1,0:T(8,128)}) custom-call(s32[1]{0:T(128)} %bitcast.where_ref, bf16[4,1,512,1024]{3,2,1,0:T(8,128)(2,1)} %bitcast.353, ...), custom_call_target="tpu_custom_call", output_to_operand_aliasing={{0}: (15, {}), {1}: (16, {})} | custom-call | flops 17716740096 | bytes 50724864 | tf_op jit(solution)/shard_map/project_out/pallas_call | solution.py:272
  523.9 673.1 %mlp.1 = (bf16[2048,4096]{1,0:T(8,128)(2,1)}, bf16[8,4096]{1,0:T(8,128)(2,1)}) custom-call(f32[8,128]{1,0:T(8,128)} %get-tuple-element.183.token_ref, bf16[8,272,4096]{2,1,0:T(8,128)(2,1)} %get-tuple-element.184.normed_ref, bf16[16,4096]{1,0:T(8,128)(2,1)} %get-tuple-element.185.hextra_ref, bf16[2,2752,4096]{2,1,0:T(8,128)(2,1)} %bitcast.363, ...), custom_call_target="tpu_custom_call" | custom-call | flops 138512695296 | bytes 541065216 | tf_op jit(solution)/shard_map/mlp/pallas_call | solution.py:529
  1197.0 1.5 slice.163
  1198.5 12.0 place_caches.1
  1210.5 6.2 copy.95
  (118 shorter events, 18.9 us)
Async XLA Ops:
  7.2 99.9 %all-gather.9.cloned.1.call-start = ((), (), s32[]{:S(2)}) async-start(), calls=%async_computation | async-start | bytes 5242880 | tf_op jit(solution)/shard_map/all_gather | solution.py:642
  9.5 381.2 %all-gather.11.cloned.1.call-start = ((), (), s32[]{:S(2)}) async-start(), calls=%async_computation.1 | async-start | bytes 5242880 | tf_op jit(solution)/shard_map/all_gather | solution.py:670
  9.6 24.0 %copy-start.16 = (bf16[2,4096]{1,0:T(2,128)(2,1)S(1)}, bf16[2,4096]{1,0:T(2,128)(2,1)}, u32[]{:S(2)}) copy-start(bf16[2,4096]{1,0:T(2,128)(2,1)} %param.14) | copy-start | bytes 49156
  9.6 24.7 %copy-start.17 = (s32[2]{0:T(128)S(1)}, s32[2]{0:T(128)}, u32[]{:S(2)}) copy-start(s32[2]{0:T(128)} %param.15) | copy-start | bytes 28
  77.8 1.6 copy-start
  79.4 1.6 copy-start.2
  81.0 0.7 copy-start.6
  81.7 9.9 copy-start.1
  91.5 299.2 %all-gather.13.cloned.1.call-start = ((), (), s32[]{:S(2)}) async-start(), calls=%async_computation.2 | async-start | bytes 10485760 | tf_op jit(solution)/shard_map/all_gather | solution.py:670
  91.6 1.6 copy-start.3
  106.4 0.6 copy-start.7
  147.3 1.6 copy-start.4
  148.9 0.7 copy-start.8
  168.1 317.7 %all-gather.15.cloned.1.call-start = ((), (), s32[]{:S(2)}) async-start(), calls=%async_computation.3 | async-start | bytes 5242880 | tf_op jit(solution)/shard_map/all_gather | solution.py:670
  170.4 47.3 %collective-permute-start = (bf16[3,2,8,128]{3,2,1,0:T(8,128)(2,1)S(1)}, bf16[3,2,8,128]{3,2,1,0:T(8,128)(2,1)S(1)}, u32[]{:S(2)}, u32[]{:S(2)}) collective-permute-start(bf16[3,2,8,128]{3,2,1,0:T(8,128)(2,1)S(1)} %constant_dynamic-update-slice_fusion), channel_id=1, source_target_pairs={{0,4},{4,8},{8,12},{12,0},{1,5},{5,9},{9,13},{13,1},{2,6},{6,10},{... | collective-permute-start | bytes 36872 | tf_op jit(solution)/shard_map/ppermute | solution.py:615
  173.7 46.9 %collective-permute-start.1 = (bf16[3,2,8,128]{3,2,1,0:T(8,128)(2,1)S(1)}, bf16[3,2,8,128]{3,2,1,0:T(8,128)(2,1)S(1)}, u32[]{:S(2)}, u32[]{:S(2)}) collective-permute-start(bf16[3,2,8,128]{3,2,1,0:T(8,128)(2,1)S(1)} %constant_dynamic-update-slice_fusion), channel_id=1, source_target_pairs={{0,8},{4,12},{8,0},{12,4},{1,9},{5,13},{9,1},{13,5},{2,10},{6,14},... | collective-permute-start | bytes 36872 | tf_op jit(solution)/shard_map/ppermute | solution.py:615
  176.2 1.8 copy-start.14
  180.8 92.9 %collective-permute-start.6 = (bf16[4,128,4096]{2,1,0:T(8,128)(2,1)}, bf16[4,128,4096]{2,1,0:T(8,128)(2,1)}, u32[]{:S(2)}, u32[]{:S(2)}) collective-permute-start(bf16[4,128,4096]{2,1,0:T(8,128)(2,1)} %bitcast.5.refs_2_.refs_1_), channel_id=1, source_target_pairs={{0,2},{1,3},{2,0},{3,1},{16,18},{17,19},{18,16},{19,17},{4,6},{5,7... | collective-permute-start | bytes 12582920 | tf_op jit(solution)/shard_map/ppermute | solution.py:618
  182.3 93.8 %collective-permute-start.7 = (bf16[4,128,4096]{2,1,0:T(8,128)(2,1)}, bf16[4,128,4096]{2,1,0:T(8,128)(2,1)}, u32[]{:S(2)}, u32[]{:S(2)}) collective-permute-start(bf16[4,128,4096]{2,1,0:T(8,128)(2,1)} %bitcast.5.refs_2_.refs_1_), channel_id=1, source_target_pairs={{0,16},{1,17},{2,18},{3,19},{16,0},{17,1},{18,2},{19,3},{4,20},{5,... | collective-permute-start | bytes 12582920 | tf_op jit(solution)/shard_map/ppermute | solution.py:618
  183.8 180.1 %collective-permute-start.8 = (bf16[4,128,4096]{2,1,0:T(8,128)(2,1)}, bf16[4,128,4096]{2,1,0:T(8,128)(2,1)}, u32[]{:S(2)}, u32[]{:S(2)}) collective-permute-start(bf16[4,128,4096]{2,1,0:T(8,128)(2,1)} %bitcast.5.refs_2_.refs_1_), channel_id=1, source_target_pairs={{0,18},{1,19},{2,16},{3,17},{16,2},{17,3},{18,0},{19,1},{4,22},{5,... | collective-permute-start | bytes 12582920 | tf_op jit(solution)/shard_map/ppermute | solution.py:618
  184.3 2.7 copy-start.15
  187.0 1.8 copy-start.5
  188.8 21.2 %copy-start.11 = (bf16[64,8,8,128]{3,2,1,0:T(8,128)(2,1)S(1)}, bf16[64,8,8,128]{3,2,1,0:T(8,128)(2,1)}, u32[]{:S(2)}) copy-start(bf16[64,8,8,128]{3,2,1,0:T(8,128)(2,1)} %copy.25) | copy-start | bytes 3145732
  188.8 21.2 %copy-start.12 = (bf16[64,8,8,128]{3,2,1,0:T(8,128)(2,1)S(1)}, bf16[64,8,8,128]{3,2,1,0:T(8,128)(2,1)}, u32[]{:S(2)}) copy-start(bf16[64,8,8,128]{3,2,1,0:T(8,128)(2,1)} %copy.32) | copy-start | bytes 3145732
  188.8 21.3 %copy-start.13 = (bf16[64,8,8,128]{3,2,1,0:T(8,128)(2,1)S(1)}, bf16[64,8,8,128]{3,2,1,0:T(8,128)(2,1)}, u32[]{:S(2)}) copy-start(bf16[64,8,8,128]{3,2,1,0:T(8,128)(2,1)} %copy.29) | copy-start | bytes 3145732
  210.1 4.4 copy-start.9
  216.0 8.6 copy-start.10
  217.6 6.9 collective-permute-start.2
  240.8 6.5 collective-permute-start.3
  240.9 8.8 collective-permute-start.4
  247.3 4.5 collective-permute-start.5
  363.9 7.5 collective-permute-start.10
  363.9 13.5 %collective-permute-start.11 = (bf16[4,128,4096]{2,1,0:T(8,128)(2,1)}, bf16[4,128,4096]{2,1,0:T(8,128)(2,1)}, u32[]{:S(2)}, u32[]{:S(2)}) collective-permute-start(bf16[4,128,4096]{2,1,0:T(8,128)(2,1)} %collective-permute-done.7.refs_6_.refs_5_), channel_id=1, source_target_pairs={{0,1},{1,0},{2,3},{3,2},{16,17},{17,16},{18,19},{19,18},{4,5},{5,4... | collective-permute-start | bytes 12582920 | tf_op jit(solution)/shard_map/ppermute | solution.py:618
  364.4 19.0 %collective-permute-start.12 = (bf16[4,128,4096]{2,1,0:T(8,128)(2,1)}, bf16[4,128,4096]{2,1,0:T(8,128)(2,1)}, u32[]{:S(2)}, u32[]{:S(2)}) collective-permute-start(bf16[4,128,4096]{2,1,0:T(8,128)(2,1)} %collective-permute-done.8.refs_8_.refs_7_), channel_id=1, source_target_pairs={{0,1},{1,0},{2,3},{3,2},{16,17},{17,16},{18,19},{19,18},{4,5},{5,4... | collective-permute-start | bytes 12582920 | tf_op jit(solution)/shard_map/ppermute | solution.py:618
  364.4 25.0 %collective-permute-start.9 = (bf16[4,128,4096]{2,1,0:T(8,128)(2,1)}, bf16[4,128,4096]{2,1,0:T(8,128)(2,1)}, u32[]{:S(2)}, u32[]{:S(2)}) collective-permute-start(bf16[4,128,4096]{2,1,0:T(8,128)(2,1)} %bitcast.5.refs_2_.refs_1_), channel_id=1, source_target_pairs={{0,1},{1,0},{2,3},{3,2},{16,17},{17,16},{18,19},{19,18},{4,5},{5,4... | collective-permute-start | bytes 12582920 | tf_op jit(solution)/shard_map/ppermute | solution.py:618
  365.0 832.0 %collective-permute-start.16 = (bf16[2,512,8,128]{3,2,1,0:T(8,128)(2,1)}, bf16[2,512,8,128]{3,2,1,0:T(8,128)(2,1)}, u32[]{:S(2)}, u32[]{:S(2)}) collective-permute-start(bf16[2,512,8,128]{3,2,1,0:T(8,128)(2,1)} %pad_maximum_fusion.2), channel_id=1, source_target_pairs={{0,1},{1,2},{2,3},{3,0},{4,5},{5,6},{6,7},{7,4},{8,9},{9,10},{10,1... | collective-permute-start | bytes 6291464 | tf_op jit(solution)/shard_map/ppermute | solution.py:742
  371.4 825.6 %collective-permute-start.19 = (bf16[2,512,8,128]{3,2,1,0:T(8,128)(2,1)}, bf16[2,512,8,128]{3,2,1,0:T(8,128)(2,1)}, u32[]{:S(2)}, u32[]{:S(2)}) collective-permute-start(bf16[2,512,8,128]{3,2,1,0:T(8,128)(2,1)} %pad_maximum_fusion.1), channel_id=1, source_target_pairs={{0,13},{1,14},{2,15},{3,12},{4,1},{5,2},{6,3},{7,0},{8,5},{9,6},{1... | collective-permute-start | bytes 6291464 | tf_op jit(solution)/shard_map/ppermute | solution.py:742
  377.4 108.4 %collective-permute-start.13 = (bf16[2,1024]{1,0:T(2,128)(2,1)S(1)}, bf16[2,1024]{1,0:T(2,128)(2,1)S(1)}, u32[]{:S(2)}, u32[]{:S(2)}) collective-permute-start(bf16[2,1024]{1,0:T(2,128)(2,1)S(1)} %fusion.45), channel_id=1, source_target_pairs={{0,4},{4,8},{8,12},{12,0},{1,5},{5,9},{9,13},{13,1},{2,6},{6,10},{... | collective-permute-start | bytes 12296 | tf_op jit(solution)/shard_map/ppermute | solution.py:615
  383.4 104.6 %collective-permute-start.14 = (bf16[2,1024]{1,0:T(2,128)(2,1)S(1)}, bf16[2,1024]{1,0:T(2,128)(2,1)S(1)}, u32[]{:S(2)}, u32[]{:S(2)}) collective-permute-start(bf16[2,1024]{1,0:T(2,128)(2,1)S(1)} %fusion.45), channel_id=1, source_target_pairs={{0,8},{4,12},{8,0},{12,4},{1,9},{5,13},{9,1},{13,5},{2,10},{6,14},... | collective-permute-start | bytes 12296 | tf_op jit(solution)/shard_map/ppermute | solution.py:615
  389.4 98.6 %collective-permute-start.15 = (bf16[2,1024]{1,0:T(2,128)(2,1)S(1)}, bf16[2,1024]{1,0:T(2,128)(2,1)S(1)}, u32[]{:S(2)}, u32[]{:S(2)}) collective-permute-start(bf16[2,1024]{1,0:T(2,128)(2,1)S(1)} %fusion.45), channel_id=1, source_target_pairs={{0,12},{4,0},{8,4},{12,8},{1,13},{5,1},{9,5},{13,9},{2,14},{6,2},{... | collective-permute-start | bytes 12296 | tf_op jit(solution)/shard_map/ppermute | solution.py:615
  485.8 711.2 %collective-permute-start.17 = (bf16[2,512,8,128]{3,2,1,0:T(8,128)(2,1)}, bf16[2,512,8,128]{3,2,1,0:T(8,128)(2,1)}, u32[]{:S(2)}, u32[]{:S(2)}) collective-permute-start(bf16[2,512,8,128]{3,2,1,0:T(8,128)(2,1)} %pad_maximum_fusion), channel_id=1, source_target_pairs={{0,5},{1,6},{2,7},{3,4},{4,9},{5,10},{6,11},{7,8},{8,13},{9,14},{1... | collective-permute-start | bytes 6291464 | tf_op jit(solution)/shard_map/ppermute | solution.py:742
  488.0 709.0 %collective-permute-start.18 = (bf16[2,512,8,128]{3,2,1,0:T(8,128)(2,1)}, bf16[2,512,8,128]{3,2,1,0:T(8,128)(2,1)}, u32[]{:S(2)}, u32[]{:S(2)}) collective-permute-start(bf16[2,512,8,128]{3,2,1,0:T(8,128)(2,1)} %pad_maximum_fusion.3), channel_id=1, source_target_pairs={{0,9},{1,10},{2,11},{3,8},{4,13},{5,14},{6,15},{7,12},{8,1},{9,2},... | collective-permute-start | bytes 6291464 | tf_op jit(solution)/shard_map/ppermute | solution.py:742
  1198.5 12.0 slice-start
  1198.5 12.0 slice-start.1
  1198.5 12.0 slice-start.2
  1198.5 12.0 slice-start.3
Sparse Core Ops, SparseCore 0:
  10.1 83.4 all-gather.8
  95.2 80.1 all-gather.10
  177.5 150.2 all-gather.12
  365.1 120.6 all-gather.14
